TPU v7x, 32 devices: a whole 2x2x4 slice. The times are simulated.
32 devices in a mesh: rep: 4 (over y, core), fsdp: 8 (over z, x).
Axes of the slice: x: 2, y: 2, z: 4, core: 2. Of those that a mesh axis runs over, the one named last changes fastest.
Arguments:
- token_ids: int32 [2, 32, 512], P(None, ('rep', 'fsdp')), may hold values from 0 to 30527
- segment_ids: int32 [2, 32, 512], P(None, ('rep', 'fsdp')), may hold values from 0 to 3, never falling along the last dimension, each value on 1 to 256 neighbouring positions
- masked_pos: int32 [2, 32, 128], P(None, ('rep', 'fsdp')), may hold values from 0 to 511, as said below
- labels: int32 [2, 32, 128], P(None, ('rep', 'fsdp')), may hold values from 0 to 30527
- blocks: float32 [32, 512, 512], P(None, 'fsdp')
- gains: float32 [6, 512], P(None, 'fsdp'), may hold values from 0.5 to 1.5
- embed: float32 [30528, 512], P('fsdp'), may hold values from -0.54 to 0.54
- embed_m: float32 [30528, 512], P('fsdp'), may hold values from -0.3 to 0.3
- embed_v: float32 [30528, 512], P('fsdp'), may hold values from 0.0005 to 0.05
- gains_m: float32 [6, 512], P(None, 'fsdp'), may hold values from -3 to 3
- gains_v: float32 [6, 512], P(None, 'fsdp'), may hold values from 0.01 to 1
- soap_m: float32 [48, 512, 512], P('fsdp'), may hold values from -0.3 to 0.3
- soap_v: float32 [48, 512, 512], P('fsdp'), may hold values from 0.0005 to 0.05
- left_basis: float32 [48, 512, 512], P('fsdp'), may hold values from -0.25 to 0.25
- right_basis: float32 [48, 512, 512], P('fsdp'), may hold values from -0.25 to 0.25
- block_slots: int32 [32], replicated, may hold values from 0 to 47, as said below
- step_count: int32 [1], replicated, may hold values from 1 to 20
Outputs:
- loss: float32 [1], replicated
- grad_norm: float32 [1], replicated
- blocks_new: float32 [32, 512, 512], P(None, 'fsdp')
- gains_new: float32 [6, 512], P(None, 'fsdp')
- embed_new: float32 [30528, 512], P('fsdp')
- embed_m_new: float32 [30528, 512], P('fsdp')
- embed_v_new: float32 [30528, 512], P('fsdp')
- gains_m_new: float32 [6, 512], P(None, 'fsdp')
- gains_v_new: float32 [6, 512], P(None, 'fsdp')
- soap_m_new: float32 [48, 512, 512], P('fsdp')
- soap_v_new: float32 [48, 512, 512], P('fsdp')
- blocks_new_low: bfloat16 [32, 512, 512], P(None, 'fsdp')
- embed_new_low: bfloat16 [30528, 512], P('fsdp')
Inputs may be any that keep to these rules, and one draw needn't show every extreme that they name: `segment_ids`: never falling along a pack; every value present in every pack. `masked_pos`: the 128 positions of a pack are distinct. `block_slots`: distinct; slot sl belongs to fsdp index sl // 6; no fsdp index gets more than 6 blocks, and one gets exactly 6.
All inputs are finite; a program needn't handle non-finite values.
Results may differ from a plain program's by a relative error of at most 0.003.
The roundings to bfloat16 on the way count: a program that leaves them out, or rounds other values in their place, can miss the bound.
Values may be sent and summed in bfloat16 or wider, within the bound.
A program may use at most 448 MiB of HBM per device.

v0:
```python
from functools import partial
import math

import jax
import jax.numpy as jnp
from jax import lax
from jax.sharding import PartitionSpec as P

HEADS = 8
FF = 2048
LAYERS = 2


norm_epsilon = 1e-05
beta_first = 0.9
beta_second = 0.99
adam_epsilon = 1e-08
step_rate = 0.04
weight_decay = 0.1
clip_ratio = 12.0
masked_score = -1e30
highest = lax.Precision.HIGHEST


def merged(value, axis, join):
    pieces = jax.tree.map(lambda part: lax.all_gather(part, axis), value)
    head = jax.tree.map(lambda part: part[0], pieces)
    tail = jax.tree.map(lambda part: part[1:], pieces)
    running, _ = lax.scan(lambda running, share: (join(running, share), None), head, tail)
    return running


def layer_norm(inputs, gain_row):
    centre = inputs - jnp.mean(inputs, axis=-1, keepdims=True)
    spread = jnp.mean(centre * centre, axis=-1, keepdims=True)
    return centre * lax.rsqrt(spread + norm_epsilon) * gain_row


def adam_moments(moment_old, second_old, gradient, first_fix, second_fix):
    moment_new = beta_first * moment_old + (1.0 - beta_first) * gradient
    second_new = beta_second * second_old + (1.0 - beta_second) * gradient * gradient
    step_value = moment_new / first_fix / (jnp.sqrt(second_new / second_fix) + adam_epsilon)
    return (moment_new, second_new, step_value)


def head_slopes(head_count):
    return 2.0 ** (-8.0 * (jnp.arange(head_count, dtype=jnp.float32) + 1.0) / head_count)


def merge_totals(first_part, second_part):
    top_first, sum_first, hit_first = first_part
    top_second, sum_second, hit_second = second_part
    top_both = jnp.maximum(top_first, top_second)
    summed = sum_first * jnp.exp(top_first - top_both) + sum_second * jnp.exp(top_second - top_both)
    return (top_both, summed, hit_first + hit_second)


def block_scores(query_rows, keys_all, same_rows, distance_rows, slopes, score_scale):
    scores = (
        jnp.einsum("qhd,khd->hqk", query_rows, keys_all, preferred_element_type=jnp.float32)
        * score_scale
    )
    scores = scores - slopes[:, None, None] * distance_rows[None]
    return jnp.where(same_rows[None], scores, masked_score)


def split_heads(mixed_rows, head_count):
    length_rows, three, model_width = mixed_rows.shape
    head_dim = model_width // head_count
    return (
        mixed_rows[:, 0].reshape(length_rows, head_count, head_dim),
        mixed_rows[:, 1].reshape(length_rows, head_count, head_dim),
        mixed_rows[:, 2].reshape(length_rows, head_count, head_dim),
    )


def attention_forward(stream, gain_row, projections, output_matrix, same_doc, distance, head_count):
    length_rows, model_width = stream.shape
    score_scale = (model_width // head_count) ** (-0.5)
    normed = layer_norm(stream, gain_row).astype(jnp.bfloat16)
    mixed_rows = jnp.einsum(
        "td,bde->tbe", normed, projections, preferred_element_type=jnp.float32
    ).astype(jnp.bfloat16)
    queries, keys_all, values_all = split_heads(mixed_rows, head_count)
    slopes = head_slopes(head_count)
    scores = block_scores(queries, keys_all, same_doc, distance, slopes, score_scale)
    top_value = jnp.max(scores, axis=-1, keepdims=True)
    shifted = jnp.exp(scores - top_value)
    exp_total = jnp.sum(shifted, axis=-1, keepdims=True)
    probs_low = (shifted / exp_total).astype(jnp.bfloat16)
    outputs = jnp.einsum("hqk,khd->qhd", probs_low, values_all, preferred_element_type=jnp.float32)
    log_sums = top_value + jnp.log(exp_total)
    attended = outputs.reshape(length_rows, model_width).astype(jnp.bfloat16)
    result = stream + jnp.dot(attended, output_matrix, preferred_element_type=jnp.float32)
    return (result, (normed, mixed_rows, log_sums, attended))


def attention_backward(
    grad_out,
    stream,
    gain_row,
    projections,
    output_matrix,
    same_doc,
    distance,
    head_count,
    kept_state,
):
    normed, mixed_rows, log_sums, attended = kept_state
    length_rows, model_width = stream.shape
    head_dim = model_width // head_count
    score_scale = head_dim ** (-0.5)
    grad_low = grad_out.astype(jnp.bfloat16)
    grad_output_matrix = jnp.einsum(
        "td,te->de", attended, grad_low, preferred_element_type=jnp.float32
    )
    grad_attended = jnp.einsum(
        "te,de->td", grad_low, output_matrix, preferred_element_type=jnp.float32
    )
    grad_attended = grad_attended.astype(jnp.bfloat16).reshape(length_rows, head_count, head_dim)
    queries, keys_all, values_all = split_heads(mixed_rows, head_count)
    slopes = head_slopes(head_count)
    scores = block_scores(queries, keys_all, same_doc, distance, slopes, score_scale)
    probs_block = jnp.exp(scores - log_sums)
    probs_low = probs_block.astype(jnp.bfloat16)
    grad_probs = jnp.einsum(
        "qhd,khd->hqk", grad_attended, values_all, preferred_element_type=jnp.float32
    )
    inner_sum = jnp.sum(probs_block * grad_probs, axis=-1, keepdims=True)
    grad_scores = (probs_block * (grad_probs - inner_sum)).astype(jnp.bfloat16)
    grad_queries = (
        jnp.einsum("hqk,khd->qhd", grad_scores, keys_all, preferred_element_type=jnp.float32)
        * score_scale
    )
    grad_keys = (
        jnp.einsum("hqk,qhd->khd", grad_scores, queries, preferred_element_type=jnp.float32)
        * score_scale
    )
    grad_values = jnp.einsum(
        "hqk,qhd->khd", probs_low, grad_attended, preferred_element_type=jnp.float32
    )
    grad_mixed = jnp.stack(
        [
            grad_queries.reshape(length_rows, model_width),
            grad_keys.reshape(length_rows, model_width),
            grad_values.reshape(length_rows, model_width),
        ],
        axis=1,
    ).astype(jnp.bfloat16)
    grad_projections = jnp.einsum(
        "td,tbe->bde", normed, grad_mixed, preferred_element_type=jnp.float32
    )
    grad_normed = jnp.einsum(
        "tbe,bde->td", grad_mixed, projections, preferred_element_type=jnp.float32
    )
    unused, norm_pull = jax.vjp(layer_norm, stream, gain_row)
    grad_stream, grad_gain = norm_pull(grad_normed)
    return (grad_out + grad_stream, grad_gain, grad_projections, grad_output_matrix)


def activation(mixed_float, pieces):
    return jax.nn.gelu(mixed_float[:, :pieces]) * mixed_float[:, pieces:]


def feed_forward(stream, gain_row, gate_up, down_blocks):
    pieces = down_blocks.shape[0]
    normed = layer_norm(stream, gain_row).astype(jnp.bfloat16)
    mixed_rows = jnp.einsum(
        "td,bde->tbe", normed, gate_up, preferred_element_type=jnp.float32
    ).astype(jnp.bfloat16)
    hidden = activation(mixed_rows.astype(jnp.float32), pieces).astype(jnp.bfloat16)
    result = stream + jnp.einsum(
        "tbf,bfd->td", hidden, down_blocks, preferred_element_type=jnp.float32
    )
    return (result, (normed, mixed_rows, hidden))


def feed_backward(grad_out, stream, gain_row, gate_up, down_blocks, kept_state):
    normed, mixed_rows, hidden = kept_state
    pieces = down_blocks.shape[0]
    grad_low = grad_out.astype(jnp.bfloat16)
    grad_down = jnp.einsum("tbf,td->bfd", hidden, grad_low, preferred_element_type=jnp.float32)
    grad_hidden = jnp.einsum(
        "td,bfd->tbf", grad_low, down_blocks, preferred_element_type=jnp.float32
    )
    unused, act_pull = jax.vjp(partial(activation, pieces=pieces), mixed_rows.astype(jnp.float32))
    grad_mixed = act_pull(grad_hidden)[0].astype(jnp.bfloat16)
    grad_gate_up = jnp.einsum("td,tbe->bde", normed, grad_mixed, preferred_element_type=jnp.float32)
    grad_normed = jnp.einsum("tbe,bde->td", grad_mixed, gate_up, preferred_element_type=jnp.float32)
    unused_norm, norm_pull = jax.vjp(layer_norm, stream, gain_row)
    grad_stream, grad_gain = norm_pull(grad_normed)
    return (grad_out + grad_stream, grad_gain, grad_gate_up, grad_down)


def body(
    token_ids,
    segment_ids,
    masked_pos,
    labels,
    blocks,
    gains,
    embed,
    embed_m,
    embed_v,
    gains_m,
    gains_v,
    soap_m,
    soap_v,
    left_basis,
    right_basis,
    block_slots,
    step_count,
):
    groups = lax.axis_size("fsdp")
    member = lax.axis_index("fsdp")
    micro_count = token_ids.shape[0]
    pack_length = token_ids.shape[2]
    pick_count = masked_pos.shape[2]
    vocab_rows, model_width = embed.shape
    block_count = blocks.shape[0]
    gain_count = gains.shape[0]
    pieces = FF // model_width
    per_layer = 4 + 3 * pieces
    table_low = embed.astype(jnp.bfloat16)
    blocks_low = blocks.astype(jnp.bfloat16)
    gains_low = gains.astype(jnp.bfloat16)
    places = jnp.arange(pack_length, dtype=jnp.float32)
    distance = jnp.abs(places[:, None] - places[None, :])
    grad_blocks = jnp.zeros((block_count, blocks.shape[1], model_width), jnp.float32)
    grad_gains = jnp.zeros((gain_count, gains.shape[1]), jnp.float32)
    grad_table = jnp.zeros((vocab_rows, model_width), jnp.float32)
    loss_local = jnp.zeros((), jnp.float32)
    columns = jnp.arange(vocab_rows, dtype=jnp.int32)
    for micro_index in range(micro_count):
        full_blocks, full_gains = (
            lax.all_gather(blocks_low, "fsdp", axis=1, tiled=True),
            lax.all_gather(gains_low, "fsdp", axis=1, tiled=True),
        )
        gain_rows = full_gains.astype(jnp.float32)
        pack_ids = token_ids[micro_index, 0]
        pack_segments = segment_ids[micro_index, 0]
        pack_positions = masked_pos[micro_index, 0]
        pack_labels = labels[micro_index, 0]
        same_doc = pack_segments[:, None] == pack_segments[None, :]
        all_ids, all_labels = (
            lax.all_gather(pack_ids, "fsdp", axis=0, tiled=True),
            lax.all_gather(pack_labels, "fsdp", axis=0, tiled=True),
        )
        local_ids = all_ids - member * vocab_rows
        inside = (local_ids >= 0) & (local_ids < vocab_rows)
        looked = jnp.take(table_low, jnp.clip(local_ids, 0, vocab_rows - 1), axis=0)
        looked = jnp.where(inside[:, None], looked, jnp.zeros((), jnp.bfloat16))
        embedded = lax.psum_scatter(
            looked.astype(jnp.float32).astype(jnp.bfloat16), "fsdp", scatter_dimension=0, tiled=True
        ).astype(jnp.float32)
        stream, first_pull = jax.vjp(layer_norm, embedded, gain_rows[0])
        saved_layers = []
        for layer_index in range(LAYERS):
            base_index = layer_index * per_layer
            matrices = full_blocks[base_index : base_index + per_layer]
            before_attention = stream
            stream, attention_kept = attention_forward(
                stream,
                gain_rows[1 + 2 * layer_index],
                matrices[0:3],
                matrices[3],
                same_doc,
                distance,
                HEADS,
            )
            before_feed = stream
            stream, feed_kept = feed_forward(
                stream,
                gain_rows[2 + 2 * layer_index],
                matrices[4 : 4 + 2 * pieces],
                matrices[4 + 2 * pieces :],
            )
            saved_layers.append((before_attention, attention_kept, before_feed, feed_kept))
        final_rows, final_pull = jax.vjp(layer_norm, stream, gain_rows[gain_count - 1])
        picked = jnp.take(final_rows, pack_positions, axis=0).astype(jnp.bfloat16)
        all_picked = lax.all_gather(picked, "fsdp", axis=0, tiled=True)
        logits = jnp.einsum("td,vd->tv", all_picked, table_low, preferred_element_type=jnp.float32)
        top_value = jnp.max(logits, axis=-1)
        exp_total = jnp.sum(jnp.exp(logits - top_value[:, None]), axis=-1)
        label_local = all_labels - member * vocab_rows
        label_hits = columns[None, :] == label_local[:, None]
        target = jnp.sum(jnp.where(label_hits, logits, 0.0), axis=-1)
        top_all, total_all, target_all = merged(
            (top_value, exp_total, target), "fsdp", merge_totals
        )
        entropy = top_all + jnp.log(total_all) - target_all
        loss_local = loss_local + jnp.sum(
            lax.dynamic_slice_in_dim(entropy, member * pick_count, pick_count)
        )
        grad_logits = (
            jnp.exp(logits - top_all[:, None]) / total_all[:, None] - label_hits.astype(jnp.float32)
        ).astype(jnp.bfloat16)
        grad_table = grad_table + jnp.einsum(
            "tv,td->vd", grad_logits, all_picked, preferred_element_type=jnp.float32
        )
        grad_picked = lax.psum_scatter(
            jnp.einsum("tv,vd->td", grad_logits, table_low, preferred_element_type=jnp.float32),
            "fsdp",
            scatter_dimension=0,
            tiled=True,
        )
        grad_final = (
            jnp.zeros((pack_length, model_width), jnp.float32).at[pack_positions].add(grad_picked)
        )
        grad_stream, grad_final_gain = final_pull(grad_final)
        gain_grads = [None] * gain_count
        gain_grads[gain_count - 1] = grad_final_gain
        layer_grads = [None] * LAYERS
        for layer_index in reversed(range(LAYERS)):
            base_index = layer_index * per_layer
            matrices = full_blocks[base_index : base_index + per_layer]
            before_attention, attention_kept, before_feed, feed_kept = saved_layers[layer_index]
            grad_stream, grad_feed_gain, grad_gate_up, grad_down = feed_backward(
                grad_stream,
                before_feed,
                gain_rows[2 + 2 * layer_index],
                matrices[4 : 4 + 2 * pieces],
                matrices[4 + 2 * pieces :],
                feed_kept,
            )
            grad_stream, grad_attention_gain, grad_projections, grad_output_matrix = (
                attention_backward(
                    grad_stream,
                    before_attention,
                    gain_rows[1 + 2 * layer_index],
                    matrices[0:3],
                    matrices[3],
                    same_doc,
                    distance,
                    HEADS,
                    attention_kept,
                )
            )
            gain_grads[1 + 2 * layer_index] = grad_attention_gain
            gain_grads[2 + 2 * layer_index] = grad_feed_gain
            layer_grads[layer_index] = jnp.concatenate(
                [grad_projections, grad_output_matrix[None], grad_gate_up, grad_down], axis=0
            )
        grad_embedded, grad_first_gain = first_pull(grad_stream)
        gain_grads[0] = grad_first_gain
        all_grad_rows = lax.all_gather(
            grad_embedded.astype(jnp.bfloat16), "fsdp", axis=0, tiled=True
        )
        target_rows = jnp.where(inside, local_ids, vocab_rows)
        grad_table = (
            grad_table
            + jax.ops.segment_sum(
                all_grad_rows.astype(jnp.float32), target_rows, num_segments=vocab_rows + 1
            )[:vocab_rows]
        )
        step_blocks = jnp.concatenate(layer_grads, axis=0)
        step_gains = jnp.stack(gain_grads, axis=0)
        shard_blocks, shard_gains = (
            lax.psum_scatter(step_blocks, "fsdp", scatter_dimension=1, tiled=True),
            lax.psum_scatter(step_gains, "fsdp", scatter_dimension=1, tiled=True),
        )
        grad_blocks = grad_blocks + shard_blocks
        grad_gains = grad_gains + shard_gains
    grad_blocks, grad_gains, grad_table, loss_local = lax.psum(
        (grad_blocks, grad_gains, grad_table, loss_local), "rep"
    )
    squares = (
        jnp.sum(grad_blocks * grad_blocks)
        + jnp.sum(grad_gains * grad_gains)
        + jnp.sum(grad_table * grad_table)
    )
    squares_all, loss_all = lax.psum((squares, loss_local), "fsdp")
    grad_norm = jnp.sqrt(squares_all)
    position_count = micro_count * lax.axis_size("rep") * groups * pick_count
    clip_limit = clip_ratio * math.sqrt(position_count)
    factor = jnp.minimum(1.0, clip_limit / grad_norm)
    steps_done = step_count[0].astype(jnp.float32)
    first_fix = 1.0 - beta_first**steps_done
    second_fix = 1.0 - beta_second**steps_done
    embed_m_new, embed_v_new, table_step = adam_moments(
        embed_m, embed_v, factor * grad_table, first_fix, second_fix
    )
    embed_new = embed - step_rate * (table_step + weight_decay * embed)
    gains_m_new, gains_v_new, gain_step = adam_moments(
        gains_m, gains_v, factor * grad_gains, first_fix, second_fix
    )
    gains_new = gains - step_rate * gain_step
    slot_cap = soap_m.shape[0]
    slot_total = slot_cap * groups
    select = (jnp.arange(slot_total, dtype=jnp.int32)[:, None] == block_slots[None, :]).astype(
        jnp.float32
    )
    clipped = factor * grad_blocks
    outgoing = jnp.einsum("sb,bri->sri", select, clipped, precision=highest)
    owned_grads = lax.all_to_all(outgoing, "fsdp", split_axis=0, concat_axis=1, tiled=True)
    rotated = jnp.einsum("bji,bjk->bik", left_basis, owned_grads, precision=highest)
    rotated = jnp.einsum("bik,bkl->bil", rotated, right_basis, precision=highest)
    moment_first, moment_second, rotated_step = adam_moments(
        soap_m, soap_v, rotated, first_fix, second_fix
    )
    my_slots = member * slot_cap + jnp.arange(slot_cap, dtype=jnp.int32)
    live_slots = jnp.any(my_slots[:, None] == block_slots[None, :], axis=1)[:, None, None]
    soap_m_new = jnp.where(live_slots, moment_first, soap_m)
    soap_v_new = jnp.where(live_slots, moment_second, soap_v)
    turned = jnp.einsum("bij,bjk->bik", left_basis, rotated_step, precision=highest)
    turned = jnp.einsum("bik,blk->bil", turned, right_basis, precision=highest)
    returned = lax.all_to_all(turned, "fsdp", split_axis=1, concat_axis=0, tiled=True)
    update = jnp.einsum("sb,sri->bri", select, returned, precision=highest)
    blocks_new = blocks - step_rate * (update + weight_decay * blocks)
    loss = (loss_all / position_count).reshape(1)
    return (
        loss,
        grad_norm.reshape(1),
        blocks_new,
        gains_new,
        embed_new,
        embed_m_new,
        embed_v_new,
        gains_m_new,
        gains_v_new,
        soap_m_new,
        soap_v_new,
        blocks_new.astype(jnp.bfloat16),
        embed_new.astype(jnp.bfloat16),
    )


def solution(mesh):
    placed = (
        P(None, ("rep", "fsdp"), None),
        P(None, ("rep", "fsdp"), None),
        P(None, ("rep", "fsdp"), None),
        P(None, ("rep", "fsdp"), None),
        P(None, "fsdp", None),
        P(None, "fsdp"),
        P("fsdp", None),
        P("fsdp", None),
        P("fsdp", None),
        P(None, "fsdp"),
        P(None, "fsdp"),
        P("fsdp", None, None),
        P("fsdp", None, None),
        P("fsdp", None, None),
        P("fsdp", None, None),
        P(),
        P(),
    )
    return jax.shard_map(
        body,
        mesh=mesh,
        in_specs=placed,
        out_specs=(
            P(),
            P(),
            P(None, "fsdp", None),
            P(None, "fsdp"),
            P("fsdp", None),
            P("fsdp", None),
            P("fsdp", None),
            P(None, "fsdp"),
            P(None, "fsdp"),
            P("fsdp", None, None),
            P("fsdp", None, None),
            P(None, "fsdp", None),
            P("fsdp", None),
        ),
        check_vma=False,
    )
```

profile of v0, /device:TPU:25, one launch (start us, length us, event | category | flops | bytes accessed | tf_op | source)
XLA Modules:
  0.0 2645.1 jit_solution(2109789570997067371)
XLA Ops:
  7.9 17.9 all-gather.5
  25.8 21.5 all-gather
  53.6 20.1 gather_fusion.2
  85.5 20.1 gather_fusion
  122.8 22.5 all-gather.10
  149.4 33.9 %reduce-scatter.11.cloned.1.call-done = bf16[512,512]{0,1:T(8,128)(2,1)} async-done(((bf16[4096,512]{0,1:T(8,128)(2,1)}), bf16[512,512]{0,1:T(8,128)(2,1)}) %reduce-scatter.11.cloned.1.call-update) | async-done | bytes 524304 | tf_op jit(solution)/shard_map/reduce_scatter | solution.py:253
  184.5 91.4 %reduce-scatter.9.cloned.1.call-done = bf16[512,512]{0,1:T(8,128)(2,1)} async-done(((bf16[4096,512]{0,1:T(8,128)(2,1)}), bf16[512,512]{0,1:T(8,128)(2,1)}) %reduce-scatter.9.cloned.1.call-update) | async-done | bytes 524304 | tf_op jit(solution)/shard_map/reduce_scatter | solution.py:253
  282.9 222.0 %all-gather.17.cloned.1.call-done = bf16[32,512,512]{2,0,1:T(8,128)(2,1)} async-done(((bf16[32,64,512]{2,0,1:T(8,128)(2,1)}), bf16[32,512,512]{2,0,1:T(8,128)(2,1)}) %all-gather.17.cloned.1.call-update) | async-done | bytes 16777232 | tf_op jit(solution)/shard_map/all_gather | solution.py:236
  647.9 14.0 all-gather.3
  685.5 23.7 all-gather.4
  709.2 24.0 all-gather.1
  733.2 24.4 all-gather.2
  769.9 24.2 all-gather.9
  794.1 24.2 all-gather.6
  818.4 24.2 all-gather.7
  878.5 89.3 %reduce-scatter.13.cloned.1.call-done = f32[128,512]{1,0:T(8,128)} async-done(((f32[1024,512]{1,0:T(8,128)}), f32[128,512]{1,0:T(8,128)}) %reduce-scatter.13.cloned.1.call-update) | async-done | bytes 262160 | tf_op jit(solution)/shard_map/reduce_scatter | solution.py:301
  973.0 66.3 %reduce-scatter.15.cloned.1.call-done = f32[128,512]{1,0:T(8,128)} async-done(((f32[1024,512]{1,0:T(8,128)}), f32[128,512]{1,0:T(8,128)}) %reduce-scatter.15.cloned.1.call-update) | async-done | bytes 262160 | tf_op jit(solution)/shard_map/reduce_scatter | solution.py:301
  1253.7 33.4 %add.526 = f32[32,512,512]{1,2,0:T(8,128)} add(f32[32,512,512]{1,2,0:T(8,128)} %convolution_dynamic-update-slice_fusion.2, f32[32,512,512]{1,2,0:T(8,128)} %convolution_dynamic-update-slice_fusion) | non-fusion elementwise | flops 8388608 | bytes 100663296 | tf_op jit(solution)/shard_map/add | solution.py:362
  1287.1 39.9 %copy.637 = f32[32,512,512]{2,0,1:T(8,128)} copy(f32[32,512,512]{1,2,0:T(8,128)} %add.526) | data formatting | bytes 67108864 | tf_op jit(solution)/shard_map/add | solution.py:362
  1346.5 30.4 %scatter_custom_fusion.3 = f32[3817,512]{1,0:T(8,128)} fusion(s32[4096]{0:T(1024)} %get-tuple-element.314, f32[4096,512]{1,0:T(8,128)} %copy.645, f32[]{:T(128)} %constant.159.clone.1), kind=kCustom, calls=%fused_computation.152 | custom fusion | flops 2097152 | bytes 7817728 | tf_op jit(solution)/shard_map/scatter-add | solution.py:352
  1384.1 30.3 %scatter_custom_fusion.2 = f32[3817,512]{1,0:T(8,128)} fusion(s32[4096]{0:T(1024)} %get-tuple-element.312, f32[4096,512]{1,0:T(8,128)} %copy.644, f32[]{:T(128)} %constant.159.clone.1), kind=kCustom, calls=%fused_computation.154 | custom fusion | flops 2097152 | bytes 7817728 | tf_op jit(solution)/shard_map/scatter-add | solution.py:352
  1414.5 15.3 slice_add_fusion
  1429.8 452.1 %reduce-scatter.17.cloned.1.call-done = f32[32,64,512]{2,0,1:T(8,128)} async-done(((f32[32,512,512]{2,0,1:T(8,128)}), f32[32,64,512]{2,0,1:T(8,128)}) %reduce-scatter.17.cloned.1.call-update) | async-done | bytes 4194320 | tf_op jit(solution)/shard_map/reduce_scatter | solution.py:359
  1885.4 58.5 %reduce-scatter.19.cloned.1.call-done = f32[64,6]{1,0:T(8,128)} async-done(((f32[512,6]{1,0:T(8,128)}), f32[64,6]{1,0:T(8,128)}) %reduce-scatter.19.cloned.1.call-update) | async-done | bytes 1552
  1953.6 207.2 %all-reduce.13.cloned.1.call-done = (f32[32,64,512]{2,0,1:T(8,128)}, f32[3816,512]{1,0:T(8,128)}) async-done(((f32[32,64,512]{2,0,1:T(8,128)}, f32[3816,512]{1,0:T(8,128)}), (f32[32,64,512]{2,0,1:T(8,128)}, f32[3816,512]{1,0:T(8,128)})) %all-reduce.13.cloned.1.call-update) | async-done | bytes 12009488 | tf_op jit(solution)/shard_map/psum | solution.py:364
  2170.5 14.0 all-reduce.8
  2207.5 136.4 %all-to-all-done = f32[48,64,512]{2,1,0:T(8,128)} async-done(((f32[48,64,512]{2,1,0:T(8,128)}), f32[48,64,512]{2,1,0:T(8,128)}, u32[]{:S(2)}, u32[]{:S(2)}) %all-to-all-start) | async-done | bytes 6291488 | tf_op jit(solution)/shard_map/all_to_all | solution.py:395
  2348.6 12.7 fusion.328
  2361.3 23.2 fusion.24
  2384.5 21.2 fusion.17
  2430.6 21.7 fusion.291
  2452.4 159.2 %all-to-all-done.1 = f32[6,512,512]{2,0,1:T(8,128)} async-done(((f32[6,512,512]{2,0,1:T(8,128)}), f32[6,512,512]{2,0,1:T(8,128)}, u32[]{:S(2)}, u32[]{:S(2)}) %all-to-all-start.1) | async-done | bytes 6291488 | tf_op jit(solution)/shard_map/all_to_all | solution.py:407
  (949 shorter events, 599.9 us)
Async XLA Ops:
  7.2 176.1 %reduce-scatter.11.cloned.1.call-start = ((), (), s32[]{:S(2)}) async-start(), calls=%async_computation.11 | async-start | bytes 4718592 | tf_op jit(solution)/shard_map/reduce_scatter | solution.py:253
  84.8 191.0 %reduce-scatter.9.cloned.1.call-start = ((), (), s32[]{:S(2)}) async-start(), calls=%async_computation.8 | async-start | bytes 4718592 | tf_op jit(solution)/shard_map/reduce_scatter | solution.py:253
  116.8 388.1 %all-gather.17.cloned.1.call-start = ((), (), s32[]{:S(2)}) async-start(), calls=%async_computation.9 | async-start | bytes 18874368 | tf_op jit(solution)/shard_map/all_gather | solution.py:236
  122.8 550.6 %all-gather.19.cloned.1.call-start = ((), (), s32[]{:S(2)}) async-start(), calls=%async_computation.10 | async-start | bytes 1179648 | tf_op jit(solution)/shard_map/all_gather | solution.py:281
  148.3 379.3 %copy-start.206 = (f32[1,512]{1,0:T(1,128)}, f32[1,512]{1,0:T(1,128)S(1)}, u32[]{:S(2)}) copy-start(f32[1,512]{1,0:T(1,128)S(1)} %get-tuple-element.320) | copy-start | bytes 6148
  148.3 450.7 %copy-start.163 = (f32[1,512]{1,0:T(1,128)}, f32[1,512]{1,0:T(1,128)S(1)}, u32[]{:S(2)}) copy-start(f32[1,512]{1,0:T(1,128)S(1)} %get-tuple-element.321) | copy-start | bytes 6148
  148.3 451.5 %copy-start.169 = (f32[1,512]{1,0:T(1,128)}, f32[1,512]{1,0:T(1,128)S(1)}, u32[]{:S(2)}) copy-start(f32[1,512]{1,0:T(1,128)S(1)} %get-tuple-element.319) | copy-start | bytes 6148
  277.0 322.0 %copy-start.161 = (f32[512]{0:T(512)}, f32[512]{0:T(512)S(1)}, u32[]{:S(2)}) copy-start(f32[512]{0:T(512)S(1)} %broadcast_multiply_fusion.5) | copy-start | bytes 6148
  278.2 275.2 %copy-start.159 = (f32[512]{0:T(512)}, f32[512]{0:T(512)S(1)}, u32[]{:S(2)}) copy-start(f32[512]{0:T(512)S(1)} %broadcast_multiply_fusion.11) | copy-start | bytes 6148
  279.5 319.5 %copy-start.167 = (f32[512]{0:T(512)}, f32[512]{0:T(512)S(1)}, u32[]{:S(2)}) copy-start(f32[512]{0:T(512)S(1)} %fusion.244) | copy-start | bytes 6148
  279.5 273.9 %copy-start.165 = (f32[512]{0:T(512)}, f32[512]{0:T(512)S(1)}, u32[]{:S(2)}) copy-start(f32[512]{0:T(512)S(1)} %fusion.238) | copy-start | bytes 6148
  281.1 242.6 %copy-start.193 = (f32[512]{0:T(512)}, f32[512]{0:T(512)S(1)}, u32[]{:S(2)}) copy-start(f32[512]{0:T(512)S(1)} %broadcast_multiply_fusion.4) | copy-start | bytes 6148
  281.1 246.5 %copy-start.191 = (f32[512]{0:T(512)}, f32[512]{0:T(512)S(1)}, u32[]{:S(2)}) copy-start(f32[512]{0:T(512)S(1)} %broadcast_multiply_fusion.10) | copy-start | bytes 6148
  282.8 232.6 %copy-start.220 = (f32[512]{0:T(512)}, f32[512]{0:T(512)S(1)}, u32[]{:S(2)}) copy-start(f32[512]{0:T(512)S(1)} %get-tuple-element.216) | copy-start | bytes 6148
  282.8 232.6 %copy-start.222 = (f32[512]{0:T(512)}, f32[512]{0:T(512)S(1)}, u32[]{:S(2)}) copy-start(f32[512]{0:T(512)S(1)} %get-tuple-element.215) | copy-start | bytes 6148
  282.9 240.8 %copy-start.210 = (f32[512]{0:T(512)}, f32[512]{0:T(512)S(1)}, u32[]{:S(2)}) copy-start(f32[512]{0:T(512)S(1)} %fusion.245) | copy-start | bytes 6148
  282.9 244.7 %copy-start.208 = (f32[512]{0:T(512)}, f32[512]{0:T(512)S(1)}, u32[]{:S(2)}) copy-start(f32[512]{0:T(512)S(1)} %fusion.239) | copy-start | bytes 6148
  580.9 497.0 %copy-start.23 = (f32[512,512]{0,1:T(8,128)}, f32[512,512]{0,1:T(8,128)S(1)}, u32[]{:S(2)}) copy-start(f32[512,512]{0,1:T(8,128)S(1)} %get-tuple-element.371) | copy-start | bytes 3145732
  619.5 460.6 %copy-start.13 = (f32[512,512]{0,1:T(8,128)}, f32[512,512]{0,1:T(8,128)S(1)}, u32[]{:S(2)}) copy-start(f32[512,512]{0,1:T(8,128)S(1)} %get-tuple-element.359) | copy-start | bytes 3145732
  619.5 460.6 %copy-start.171 = (f32[512]{0:T(512)}, f32[512]{0:T(512)S(1)}, u32[]{:S(2)}) copy-start(f32[512]{0:T(512)S(1)} %broadcast_multiply_fusion.1) | copy-start | bytes 6148
  619.7 460.4 %copy-start.179 = (f32[512]{0:T(512)}, f32[512]{0:T(512)S(1)}, u32[]{:S(2)}) copy-start(f32[512]{0:T(512)S(1)} %fusion.248) | copy-start | bytes 6148
  636.3 121.4 %all-gather.21.cloned.1.call-start = ((), (), s32[]{:S(2)}) async-start(), calls=%async_computation.12 | async-start | bytes 1179648 | tf_op jit(solution)/shard_map/all_gather | solution.py:281
  666.8 301.0 %reduce-scatter.13.cloned.1.call-start = ((), (), s32[]{:S(2)}) async-start(), calls=%async_computation.13 | async-start | bytes 2359296 | tf_op jit(solution)/shard_map/reduce_scatter | solution.py:301
  860.3 179.0 %reduce-scatter.15.cloned.1.call-start = ((), (), s32[]{:S(2)}) async-start(), calls=%async_computation.14 | async-start | bytes 2359296 | tf_op jit(solution)/shard_map/reduce_scatter | solution.py:301
  878.3 166.4 %copy-start.200 = (f32[512]{0:T(512)S(1)}, f32[512]{0:T(512)}, u32[]{:S(2)}) copy-start(f32[512]{0:T(512)} %copy-done.199) | copy-start | bytes 6148
  878.3 461.1 %all-gather.25.cloned.1.call-start = ((), (), s32[]{:S(2)}) async-start(), calls=%async_computation.16 | async-start | bytes 4718592 | tf_op jit(solution)/shard_map/all_gather | solution.py:346
  1189.8 187.1 %all-gather.23.cloned.1.call-start = ((), (), s32[]{:S(2)}) async-start(), calls=%async_computation.15 | async-start | bytes 4718592 | tf_op jit(solution)/shard_map/all_gather | solution.py:346
  1190.5 691.4 %reduce-scatter.17.cloned.1.call-start = ((), (), s32[]{:S(2)}) async-start(), calls=%async_computation.17 | async-start | bytes 37748736 | tf_op jit(solution)/shard_map/reduce_scatter | solution.py:359
  1327.1 616.7 %reduce-scatter.19.cloned.1.call-start = ((), (), s32[]{:S(2)}) async-start(), calls=%async_computation.18 | async-start | bytes 294912
  1338.9 821.9 %all-reduce.13.cloned.1.call-start = ((), (), s32[]{:S(2)}) async-start(), calls=%async_computation.19 | async-start | bytes 24018944 | tf_op jit(solution)/shard_map/psum | solution.py:364
  2197.2 146.8 %all-to-all-start = ((f32[48,64,512]{2,1,0:T(8,128)}), f32[48,64,512]{2,1,0:T(8,128)}, u32[]{:S(2)}, u32[]{:S(2)}) async-start(f32[48,64,512]{2,1,0:T(8,128)} %copy.646), calls=%async_computation.4 | async-start | bytes 12582912 | tf_op jit(solution)/shard_map/all_to_all | solution.py:395
  2424.2 187.4 %all-to-all-start.1 = ((f32[6,512,512]{2,0,1:T(8,128)}), f32[6,512,512]{2,0,1:T(8,128)}, u32[]{:S(2)}, u32[]{:S(2)}) async-start(f32[6,512,512]{2,0,1:T(8,128)} %copy.652), calls=%async_computation.5 | async-start | bytes 16777216 | tf_op jit(solution)/shard_map/all_to_all | solution.py:407
  (273 other events, 2993.3 us)
Sparse Core Ops, SparseCore 0:
  84.9 98.3 reduce-scatter.10
  187.5 88.2 reduce-scatter.8
  278.5 226.3 all-gather.16
  636.4 36.9 all-gather.18
  675.9 39.0 all-gather.20
  860.4 107.3 reduce-scatter.12
  971.9 67.3 reduce-scatter.14
  1189.9 74.5 all-gather.24
  1266.5 72.7 all-gather.22
  1343.0 538.9 reduce-scatter.16
  1885.9 57.9 reduce-scatter.18
  1946.9 213.9 all-reduce.12
where the time goes:
time: 2660 us; the launch traced here: 2650 us
  waiting for transfers between devices  1520 us (57%)
  matrix products  340 us (13%)
  blocking collectives  255 us (10%)
  local copies, waits for them, and re-layouts  251 us (9%)
  other arithmetic  232 us (9%)
    reduce_scatter x1, waiting for transfers between devices, body(): lax.psum_scatter(step_blocks, 'fsdp', scatter_dimension=1, tiled=True)  452 us
    all_gather x1, waiting for transfers between devices, body(): lax.all_gather(blocks_low, 'fsdp', axis=1, tiled=True)  222 us
    psum x1, waiting for transfers between devices, body(): lax.psum((grad_blocks, grad_gains, grad_table, loss_local), 'rep')  207 us
    all_to_all x1, waiting for transfers between devices, body(): lax.all_to_all(turned, 'fsdp', split_axis=1, concat_axis=0, tiled=True)  159 us
    reduce_scatter x2, waiting for transfers between devices, body(): lax.psum_scatter(jnp.einsum('tv,vd->td', grad_logits, table_low, preferre...  156 us
    all_gather x6, blocking collectives, merged(): pieces = jax.tree.map(lambda part: lax.all_gather(part, axis), value)  145 us
    all_to_all x1, waiting for transfers between devices, body(): lax.all_to_all(outgoing, 'fsdp', split_axis=0, concat_axis=1, tiled=True)  136 us
    reduce_scatter x2, waiting for transfers between devices, body(): lax.psum_scatter(looked.astype(jnp.float32).astype(jnp.bfloat16), 'fsdp',...  125 us
  transfers between devices with their start and end apart: 14, of which 11 were waited for; matrix products, arithmetic and copies ran while one was open for 13% of the time, Pallas kernels for 0%

commit v1 on v0

v1 whole, which is shorter than its diff:
```python
from functools import partial
import math

import jax
import jax.numpy as jnp
from jax import lax
from jax.experimental import pallas as pl
from jax.experimental.pallas import tpu as pltpu
from jax.sharding import PartitionSpec as P

HEADS = 8
FF = 2048
LAYERS = 2

norm_epsilon = 1e-05
beta_first = 0.9
beta_second = 0.99
adam_epsilon = 1e-08
step_rate = 0.04
weight_decay = 0.1
clip_ratio = 12.0
masked_score = -1e30
bf16 = jnp.bfloat16
f32 = jnp.float32
highest = lax.Precision.HIGHEST
high = lax.Precision.HIGH
MESH = pl.DeviceIdType.MESH
ANY = pl.BlockSpec(memory_space=pl.ANY)
VMEM = pl.BlockSpec(memory_space=pltpu.VMEM)
CAPACITY = 128


def pick(table, index):
    out = jnp.int32(table[0])
    for k in range(1, len(table)):
        out = jnp.where(index == k, jnp.int32(table[k]), out)
    return out


def ring_order(n):
    nz = 4
    nx = n // nz
    order = []
    for x in range(nx):
        zs = range(1, nz) if x % 2 == 0 else range(nz - 1, 0, -1)
        order += [z * nx + x for z in zs]
    order += [x for x in range(nx - 1, -1, -1)]
    return order


class Place:
    def __init__(self, n_rep, n_fsdp):
        self.r = lax.axis_index("rep")
        self.f = lax.axis_index("fsdp")
        self.n_rep, self.n = n_rep, n_fsdp
        self.c = lax.rem(self.r, 2)
        self.y = self.r // 2
        self.order = ring_order(n_fsdp)
        spot = [self.order.index(k) for k in range(n_fsdp)]
        self.pos = pick(spot, self.f)
        self.core = (self.r + 1 - 2 * self.c, self.f)
        self.next = (self.r, self.at(1))
        self.prev = (self.r, self.at(-1))

    def at(self, step):
        return pick(self.order, lax.rem(self.pos + step + 2 * self.n, self.n))


def enter(peers):
    barrier = pltpu.get_barrier_semaphore()
    for peer in peers:
        pl.semaphore_signal(barrier, inc=1, device_id=peer, device_id_type=MESH)
    pl.semaphore_wait(barrier, len(peers))


def remote(src, dst, send, recv, peer):
    return pltpu.make_async_remote_copy(
        src_ref=src, dst_ref=dst, send_sem=send, recv_sem=recv, device_id=peer, device_id_type=MESH
    )


def params(cid, limit=None):
    return pltpu.CompilerParams(
        collective_id=cid, has_side_effects=True, vmem_limit_bytes=limit
    )


def group_kernel(n_rep, n, spread, x_ref, o_ref, send, recv):
    here = Place(n_rep, n)
    me = here.f
    others = [lax.rem(me + k, n) for k in range(1, n)]
    enter([(here.r, o) for o in others])
    copies = []
    for k, o in enumerate(others):
        src = x_ref.at[o] if spread else x_ref
        cp = remote(src, o_ref.at[me], send.at[k], recv.at[k], (here.r, o))
        cp.start()
        copies.append(cp)
    o_ref[me] = x_ref[me] if spread else x_ref[...]
    for cp in copies:
        cp.wait()


def group_exchange(mesh_sizes, cid, x, spread):
    n_rep, n = mesh_sizes
    shape = x.shape if spread else (n,) + x.shape
    return pl.pallas_call(
        partial(group_kernel, n_rep, n, spread),
        out_shape=jax.ShapeDtypeStruct(shape, x.dtype),
        in_specs=[VMEM],
        out_specs=VMEM,
        scratch_shapes=[pltpu.SemaphoreType.DMA((n - 1,)), pltpu.SemaphoreType.DMA((n - 1,))],
        compiler_params=params(cid),
        name=f"group_{cid}",
    )(x)


def ask_kernel(n_rep, n, w_ref, facts_ref, gains_ref, asked, facts, gains, most, held, got, send, recv, send2, recv2):
    here = Place(n_rep, n)
    ypeer = (lax.rem(here.r + 2, 4), here.f)
    me = here.f
    others = [lax.rem(me + k, n) for k in range(1, n)]
    enter([(here.r, o) for o in others] + [here.core, ypeer])
    copies = []
    for k, o in enumerate(others):
        peer = (here.r, o)
        copies.append(remote(facts_ref, facts.at[me], send.at[0, k], recv.at[0, k], peer))
        copies.append(remote(w_ref.at[o], asked.at[me], send.at[1, k], recv.at[1, k], peer))
        copies.append(remote(gains_ref, gains.at[me], send.at[2, k], recv.at[2, k], peer))
    for cp in copies:
        cp.start()
    asked[me] = w_ref[me]
    facts[me] = facts_ref[...]
    gains[me] = gains_ref[...]
    for cp in copies:
        cp.wait_recv()
    top = facts[0]
    for k in range(1, n):
        top = jnp.maximum(top, facts[k])
    held[0] = top
    first = remote(held.at[0], got.at[0], send2.at[0], recv2.at[0], here.core)
    first.start()
    first.wait_recv()
    held[1] = jnp.maximum(top, got[0])
    second = remote(held.at[1], got.at[1], send2.at[1], recv2.at[1], ypeer)
    second.start()
    second.wait_recv()
    most[...] = jnp.maximum(held[1], got[1])
    first.wait_send()
    second.wait_send()
    for cp in copies:
        cp.wait_send()


def ask_group(mesh_sizes, cid, wanted, facts, gains):
    n_rep, n = mesh_sizes
    dma = pltpu.SemaphoreType.DMA
    return pl.pallas_call(
        partial(ask_kernel, n_rep, n),
        out_shape=[
            jax.ShapeDtypeStruct(wanted.shape, wanted.dtype),
            jax.ShapeDtypeStruct((n,) + facts.shape, facts.dtype),
            jax.ShapeDtypeStruct((n,) + gains.shape, gains.dtype),
            jax.ShapeDtypeStruct(facts.shape, facts.dtype),
        ],
        in_specs=[VMEM] * 3,
        out_specs=[VMEM] * 4,
        scratch_shapes=[pltpu.VMEM((2,) + facts.shape, facts.dtype)] * 2
        + [dma((3, n - 1)), dma((3, n - 1)), dma((2,)), dma((2,))],
        compiler_params=params(cid),
        name="ask_group",
    )(wanted, facts, gains)


def weights_kernel(n_rep, n, half, shared, x_ref, o_ref, ring_s, ring_r, core_s, core_r, y_s, y_r, over_s, over_r):
    here = Place(n_rep, n)
    ypeer = (lax.rem(here.r + 2, 4), here.f)
    rows = x_ref.shape[1]
    alone = (half - shared) // 2
    enter([here.next, here.prev, here.core, ypeer])
    mine = pl.ds(here.c * half + here.y * alone, alone + shared)
    given = pl.ds(here.c * half + here.y * (alone + shared), alone)
    taken = pl.ds(here.c * half + (1 - here.y) * (alone + shared), alone)
    hops = n // 2
    copies, sends = [], []

    def rows_of(origin, way, s):
        if s == hops - 1:
            return pl.ds(pl.multiple_of(origin * rows + way * (rows // 2), rows // 2), rows // 2)
        return pl.ds(pl.multiple_of(origin * rows, rows), rows)

    own = remote(
        x_ref, o_ref.at[:, rows_of(here.f, 0, -1)], core_s.at[0, 0], core_r.at[0, 0], here.core
    )
    own.start()
    copies.append(own)
    waiting = [None, None]
    across = []

    def pass_on(way, s):
        waiting[way].wait_recv()
        where = rows_of(here.at(-s - 1 if way == 0 else s + 1), way, s)
        held = o_ref.at[given, where]
        cp = remote(held, held, y_s.at[way, s], y_r.at[way, s], ypeer)
        cp.start()
        across.append((cp, o_ref.at[taken, where], way, s))
        held = o_ref.at[mine, where]
        cp = remote(held, held, core_s.at[way, s + 1], core_r.at[way, s + 1], here.core)
        cp.start()
        copies.append(cp)

    for s in range(hops):
        for way in range(2):
            if s > 0:
                pass_on(way, s - 1)
            origin = here.at(-s if way == 0 else s)
            where = rows_of(origin, way, s)
            if s == 0:
                src = x_ref.at[mine]
            else:
                src = o_ref.at[mine, where]
            cp = remote(
                src,
                o_ref.at[mine, where],
                ring_s.at[way, s],
                ring_r.at[way, s],
                here.next if way == 0 else here.prev,
            )
            cp.start()
            waiting[way] = cp
            sends.append(cp)
    for way in range(2):
        pass_on(way, hops - 1)
    for cp, held, way, s in across:
        cp.wait_recv()
        over = remote(held, held, over_s.at[way, s], over_r.at[way, s], here.core)
        over.start()
        copies.append(over)
        sends.append(cp)
    for cp in sends:
        cp.wait_send()
    for cp in copies:
        cp.wait()


def gather_weights(mesh_sizes, cid, shard):
    n_rep, n = mesh_sizes
    count, rows, width = shard.shape
    half = count // 2
    dma = pltpu.SemaphoreType.DMA
    return pl.pallas_call(
        partial(weights_kernel, n_rep, n, half, half - 2 * (half // 3)),
        out_shape=jax.ShapeDtypeStruct((count, rows * n, width), shard.dtype),
        in_specs=[ANY],
        out_specs=ANY,
        scratch_shapes=[
            dma((2, n // 2)),
            dma((2, n // 2)),
            dma((2, n // 2 + 1)),
            dma((2, n // 2 + 1)),
            dma((2, n // 2)),
            dma((2, n // 2)),
            dma((2, n // 2)),
            dma((2, n // 2)),
        ],
        compiler_params=params(cid),
        name="gather_weights",
    )(shard)


def ring_rows_kernel(n_rep, n, x_ref, o_ref, send, recv):
    here = Place(n_rep, n)
    enter([here.next, here.prev])
    rows = x_ref.shape[0]
    hops = n // 2
    copies = []
    waiting = [None, None]
    for s in range(hops):
        for way in range(2):
            peer = here.next if way == 0 else here.prev
            origin = here.at(-s if way == 0 else s)
            if s > 0:
                waiting[way].wait_recv()
            window = pl.ds(0, rows)
            if s == hops - 1:
                window = pl.ds(way * (rows // 2), rows // 2)
            src = x_ref.at[window] if s == 0 else o_ref.at[origin, window]
            cp = remote(src, o_ref.at[origin, window], send.at[way, s], recv.at[way, s], peer)
            cp.start()
            waiting[way] = cp
            copies.append(cp)
    o_ref[here.f] = x_ref[...]
    for way in range(2):
        waiting[way].wait_recv()
    for cp in copies:
        cp.wait_send()


def ring_rows(mesh_sizes, cid, x):
    n_rep, n = mesh_sizes
    return pl.pallas_call(
        partial(ring_rows_kernel, n_rep, n),
        out_shape=jax.ShapeDtypeStruct((n,) + x.shape, x.dtype),
        in_specs=[VMEM],
        out_specs=VMEM,
        scratch_shapes=[pltpu.SemaphoreType.DMA((2, n // 2)), pltpu.SemaphoreType.DMA((2, n // 2))],
        compiler_params=params(cid),
        name="ring_rows",
    )(x)


def reduce_kernel(
    n_rep, n, half, table_rows, each, *refs
):
    g_refs, refs = refs[: 2 * each], refs[2 * each :]
    (
    t_ref, o_ref, to_ref, sq_ref,
    own, part, got, fin, ysend, ygot, town, tpart, tsend, tgot,
    load_s, core_s, core_r, ring_s, ring_r, y_s, y_r, tload, tcs, tcr, tys, tyr, tos, tor,
    ) = refs
    here = Place(n_rep, n)
    c, y = here.c, here.y
    ypeer = (lax.rem(here.r + 2, 4), here.f)
    other_c, other_y = 1 - c, 1 - y
    enter([here.next, here.prev, here.core, ypeer])
    far = n // 2

    tl = pltpu.make_async_copy(t_ref.at[pl.ds(c * 2, 2)], town, tload)
    tl.start()
    tc = remote(t_ref.at[pl.ds(other_c * 2, 2)], tpart, tcs, tcr, here.core)
    tc.start()

    spots = {(0, far): 0, (1, far): 0}
    for d in range(far - 1, 0, -1):
        spots[0, d] = 1 + 2 * (far - 1 - d)
        spots[1, d] = 2 + 2 * (far - 1 - d)
    spots[0, 0] = spots[1, 0] = n - 1
    loads, cores = {}, {}
    done = set()
    for (way, d), spot in sorted(spots.items(), key=lambda item: item[1]):
        if spot in done:
            continue
        done.add(spot)
        to = here.f if d == 0 else here.at(d if way == 0 else -d)
        for h in (way, 1 - way):
            loads[spot, h], cores[spot, h] = [], []
            for j in range(each):
                g_ref = g_refs[h * each + j]
                into = pl.ds(j * (half // each), half // each)
                ld = pltpu.make_async_copy(g_ref.at[:, to, :, c], own.at[spot, h, into], load_s.at[spot, h, j])
                ld.start()
                loads[spot, h].append(ld)
                cp = remote(
                    g_ref.at[:, to, :, other_c],
                    part.at[spot, h, into],
                    core_s.at[spot, h, j],
                    core_r.at[spot, h, j],
                    here.core,
                )
                cp.start()
                cores[spot, h].append(cp)

    def ready(spot, h):
        for j in range(each):
            loads[spot, h][j].wait()
            cores[spot, h][j].wait_recv()

    ring = {}

    def came(way, h, s):
        return got.at[way, h, s]

    def lane(way, h, s):
        d = far - s
        spot = spots[way, d]
        ready(spot, h)
        before = ring.get((way, h, s - 1))
        if before is not None:
            before.wait_recv()
        target = own.at[spot, h]

        @pl.loop(0, half)
        def _(b):
            for k in range(2):
                total = own[spot, h, b, k].astype(f32) + part[spot, h, b, k].astype(f32)
                if before is not None:
                    total = total + came(way, h, s - 1)[b, k].astype(f32)
                target[b, k] = total.astype(target.dtype)

        cp = remote(
            target, came(way, h, s), ring_s.at[way, h, s], ring_r.at[way, h, s], here.next if way == 0 else here.prev
        )
        cp.start()
        ring[way, h, s] = cp

    step_rows = 48
    for s in range(far):
        for h_turn in range(2):
            for way in range(2):
                h = way if h_turn == 1 else 1 - way
                if s == 0 and h_turn == 0:
                    continue
                if s == 1 and h_turn == 0:
                    continue
                lane(way, h, s)
        if s == 0:
            for way in range(2):
                lane(way, 1 - way, 1)
            tl.wait()
            tc.wait_recv()

            @pl.loop(0, table_rows // step_rows)
            def _(i):
                at = pl.ds(pl.multiple_of(i * step_rows, step_rows), step_rows)
                town[y, at] = town[y, at] + tpart[y, at]
                tsend[at] = (town[other_y, at] + tpart[other_y, at]).astype(bf16)

            ty = remote(tsend, tgot, tys, tyr, ypeer)
            ty.start()
        if s == 2:
            ty.wait_recv()

            def add(i, acc):
                at = pl.ds(pl.multiple_of(i * step_rows, step_rows), step_rows)
                total = town[y, at] + tgot[at].astype(f32)
                town[y, at] = total
                square = total * total
                for k in range(step_rows // 8):
                    acc = acc + square[k * 8 : k * 8 + 8]
                return acc

            sq_ref[0] = lax.fori_loop(0, table_rows // step_rows, add, jnp.zeros((8, tgot.shape[1]), f32))
            mine = c * 2 + y
            near = c * 2 + other_y
            tkeep = pltpu.make_async_copy(town.at[y], to_ref.at[mine], tload)
            tkeep.start()
            t0 = remote(town.at[y], to_ref.at[mine], tos.at[0], tor.at[0], ypeer)
            t1 = remote(town.at[y], to_ref.at[mine], tos.at[1], tor.at[1], here.core)
            t0.start()
            t1.start()
    t0.wait_recv()
    t2 = remote(to_ref.at[near], to_ref.at[near], tos.at[2], tor.at[2], here.core)
    t2.start()
    ys = []
    spot = spots[0, 0]
    for h in range(2):
        ready(spot, h)
        for way in range(2):
            ring[way, h, far - 1].wait_recv()

        @pl.loop(0, half)
        def _(b, h=h):
            for keep in range(2):
                k = y if keep else other_y
                total = own[spot, h, b, k].astype(f32) + part[spot, h, b, k].astype(f32)
                for way in range(2):
                    total = total + got[way, h, far - 1, b, k].astype(f32)
                if keep:
                    fin[h, b] = total
                else:
                    ysend[h, b] = total.astype(bf16)

        cp = remote(ysend.at[h], ygot.at[h], y_s.at[h], y_r.at[h], ypeer)
        cp.start()
        ys.append(cp)

    acc = jnp.zeros((8, fin.shape[-1]), f32)
    for h in range(2):
        ys[h].wait_recv()

        def last(b, acc, h=h):
            total = fin[h, b] + ygot[h, b].astype(f32)
            o_ref[h * half + b] = total
            square = total * total
            return acc + square[:8] + square[8:]

        acc = lax.fori_loop(0, half, last, acc)
    sq_ref[1] = acc
    for cp in ys:
        cp.wait_send()
    for cp in ring.values():
        cp.wait_send()
    for group in cores.values():
        for cp in group:
            cp.wait_send()
    tc.wait_send()
    ty.wait_send()
    tkeep.wait()
    t0.wait_send()
    t1.wait()
    t2.wait()


def reduce_gradients(mesh_sizes, cid, grads, table):
    n_rep, n = mesh_sizes
    _, depth, width = grads[0].shape
    count = sum(g.shape[0] for g in grads)
    half = count // 2
    each = len(grads) // 2
    far = n // 2
    table_rows = table.shape[1]
    views = [g.reshape(g.shape[0], n, 2, 2, 16, width) for g in grads]
    dma = pltpu.SemaphoreType.DMA
    piece = (half, 2, 16, width)
    return pl.pallas_call(
        partial(reduce_kernel, n_rep, n, half, table_rows, each),
        out_shape=[
            jax.ShapeDtypeStruct((count, 16, width), f32),
            jax.ShapeDtypeStruct(table.shape, f32),
            jax.ShapeDtypeStruct((2, 8, width), f32),
        ],
        in_specs=[ANY] * (2 * each + 1),
        out_specs=[VMEM, ANY, VMEM],
        scratch_shapes=[
            pltpu.VMEM((n, 2) + piece, bf16),
            pltpu.VMEM((n, 2) + piece, bf16),
            pltpu.VMEM((2, 2, far) + piece, bf16),
            pltpu.VMEM((2, half, 16, width), f32),
            pltpu.VMEM((2, half, 16, width), bf16),
            pltpu.VMEM((2, half, 16, width), bf16),
            pltpu.VMEM((2, table_rows, width), f32),
            pltpu.VMEM((2, table_rows, width), f32),
            pltpu.VMEM((table_rows, width), bf16),
            pltpu.VMEM((table_rows, width), bf16),
            dma((n, 2, each)),
            dma((n, 2, each)),
            dma((n, 2, each)),
            dma((2, 2, far)),
            dma((2, 2, far)),
            dma((2,)),
            dma((2,)),
            dma,
            dma,
            dma,
            dma,
            dma,
            dma((3,)),
            dma((3,)),
        ],
        compiler_params=params(cid, 60 << 20),
        name="reduce_gradients",
    )(*views, table)


def rows_kernel(n_rep, n, x_ref, o_ref, held, got, send, recv):
    here = Place(n_rep, n)
    enter([here.next, here.prev])
    far = n // 2
    rows = x_ref.shape[1] // 2
    ring = {}

    def lane(way, h, s):
        d = far - s
        q = here.at(d if way == 0 else -d)
        before = ring.get((way, h, s - 1))
        if before is None:
            source = x_ref.at[q, pl.ds(h * rows, rows)]
        else:
            before.wait_recv()
            total = x_ref[q, pl.ds(h * rows, rows)].astype(f32) + got[way, h, s - 1].astype(f32)
            held[way, h, s - 1] = total.astype(held.dtype)
            source = held.at[way, h, s - 1]
        cp = remote(
            source, got.at[way, h, s], send.at[way, h, s], recv.at[way, h, s], here.next if way == 0 else here.prev
        )
        cp.start()
        ring[way, h, s] = cp

    for s in range(far):
        for turn in range(2):
            for way in range(2):
                h = way if turn == 1 else 1 - way
                if turn == 0 and s < 2:
                    continue
                lane(way, h, s)
        if s == 0:
            for way in range(2):
                lane(way, 1 - way, 1)
    for h in range(2):
        for way in range(2):
            ring[way, h, far - 1].wait_recv()
        at = pl.ds(h * rows, rows)
        total = x_ref[here.f, at].astype(f32)
        for way in range(2):
            total = total + got[way, h, far - 1].astype(f32)
        o_ref[at] = total
    for cp in ring.values():
        cp.wait_send()


def reduce_rows(mesh_sizes, cid, x):
    n_rep, n = mesh_sizes
    _, rows, width = x.shape
    far = n // 2
    dma = pltpu.SemaphoreType.DMA
    return pl.pallas_call(
        partial(rows_kernel, n_rep, n),
        out_shape=jax.ShapeDtypeStruct((rows, width), f32),
        in_specs=[VMEM],
        out_specs=VMEM,
        scratch_shapes=[
            pltpu.VMEM((2, 2, far - 1, rows // 2, width), x.dtype),
            pltpu.VMEM((2, 2, far, rows // 2, width), x.dtype),
            dma((2, 2, far)),
            dma((2, 2, far)),
        ],
        compiler_params=params(cid, 24 << 20),
        name="reduce_rows",
    )(x)


def total_kernel(n_rep, n, x_ref, o_ref, core_got, both, y_got, four, got, send, recv):
    here = Place(n_rep, n)
    ypeer = (lax.rem(here.r + 2, 4), here.f)
    others = [lax.rem(here.f + k, n) for k in range(1, n)]
    enter([(here.r, o) for o in others] + [here.core, ypeer])
    first = remote(x_ref, core_got, send.at[0], recv.at[0], here.core)
    first.start()
    first.wait_recv()
    both[...] = x_ref[...] + core_got[...]
    second = remote(both, y_got, send.at[1], recv.at[1], ypeer)
    second.start()
    second.wait_recv()
    four[...] = both[...] + y_got[...]
    copies = []
    for k, o in enumerate(others):
        cp = remote(four, got.at[here.f], send.at[2 + k], recv.at[2 + k], (here.r, o))
        cp.start()
        copies.append(cp)
    got[here.f] = four[...]
    for cp in copies:
        cp.wait_recv()
    total = got[0]
    for k in range(1, n):
        total = total + got[k]
    o_ref[...] = total
    first.wait_send()
    second.wait_send()
    for cp in copies:
        cp.wait_send()


def total_everyone(mesh_sizes, cid, x):
    n_rep, n = mesh_sizes
    dma = pltpu.SemaphoreType.DMA
    like = pltpu.VMEM(x.shape, x.dtype)
    return pl.pallas_call(
        partial(total_kernel, n_rep, n),
        out_shape=jax.ShapeDtypeStruct(x.shape, x.dtype),
        in_specs=[VMEM],
        out_specs=VMEM,
        scratch_shapes=[like] * 4 + [pltpu.VMEM((n,) + x.shape, x.dtype), dma((n + 1,)), dma((n + 1,))],
        compiler_params=params(cid),
        name=f"total_{cid}",
    )(x)


def slots_kernel(n_rep, n, to_slots, x_ref, o_ref, keep, a_s, a_r, f_s, f_r):
    here = Place(n_rep, n)
    ypeer = (lax.rem(here.r + 2, 4), here.f)
    me = here.f
    others = [lax.rem(me + k, n) for k in range(1, n)]
    enter([(here.r, o) for o in others] + [here.core, ypeer])

    def spot(source, r):
        return o_ref.at[:, source, r] if to_slots else o_ref.at[source, :, r]

    copies = []
    for k, o in enumerate(others):
        cp = remote(x_ref.at[o], spot(me, here.r), a_s.at[k], a_r.at[k], (here.r, o))
        cp.start()
        copies.append(cp)
    own = pltpu.make_async_copy(x_ref.at[me], spot(me, here.r), keep)
    own.start()
    sends, far = [], []
    for k in range(n):
        source = me if k == 0 else lax.rem(me - k + n, n)
        if k == 0:
            own.wait()
        else:
            copies[k - 1].wait_recv()
        held = spot(source, here.r)
        over = remote(held, held, f_s.at[0, k], f_r.at[0, k], ypeer)
        over.start()
        beside = remote(held, held, f_s.at[1, k], f_r.at[1, k], here.core)
        beside.start()
        far.append((over, source))
        sends.append(beside)
    yr = lax.rem(here.r + 2, 4)
    for k, (over, source) in enumerate(far):
        over.wait_recv()
        src = me if k == 0 else lax.rem(me - k + n, n)
        held = spot(src, yr)
        beside = remote(held, held, f_s.at[2, k], f_r.at[2, k], here.core)
        beside.start()
        sends.append(beside)
    for cp in copies:
        cp.wait_send()
    for over, _ in far:
        over.wait_send()
    for cp in sends:
        cp.wait()


def exchange_slots(mesh_sizes, cid, x, to_slots):
    n_rep, n = mesh_sizes
    _, cap, rows, width = x.shape
    shape = (cap, n, 4, rows, width) if to_slots else (n, cap, 4, rows, width)
    dma = pltpu.SemaphoreType.DMA
    return pl.pallas_call(
        partial(slots_kernel, n_rep, n, to_slots),
        out_shape=jax.ShapeDtypeStruct(shape, x.dtype),
        in_specs=[VMEM],
        out_specs=ANY,
        scratch_shapes=[dma, dma((n - 1,)), dma((n - 1,)), dma((3, n)), dma((3, n))],
        compiler_params=params(cid),
        name=f"slots_{cid}",
    )(x)


def layer_norm(inputs, gain_row):
    centre = inputs - jnp.mean(inputs, axis=-1, keepdims=True)
    spread = jnp.mean(centre * centre, axis=-1, keepdims=True)
    return centre * lax.rsqrt(spread + norm_epsilon) * gain_row


def adam_moments(moment_old, second_old, gradient, first_fix, second_fix):
    moment_new = beta_first * moment_old + (1.0 - beta_first) * gradient
    second_new = beta_second * second_old + (1.0 - beta_second) * gradient * gradient
    step_value = moment_new / first_fix / (jnp.sqrt(second_new / second_fix) + adam_epsilon)
    return (moment_new, second_new, step_value)


def head_slopes(head_count):
    return 2.0 ** (-8.0 * (jnp.arange(head_count, dtype=f32) + 1.0) / head_count)


NT = (((1,), (1,)), ((), ()))
TN = (((0,), (0,)), ((), ()))
masked_distance = 1e33


def mm(a, b, dims=None):
    if dims is None:
        return jnp.dot(a, b, preferred_element_type=f32)
    return lax.dot_general(a, b, dims, preferred_element_type=f32)


def norm_parts(x):
    centre = x - jnp.mean(x, axis=-1, keepdims=True)
    spread = jnp.mean(centre * centre, axis=-1, keepdims=True)
    rstd = lax.rsqrt(spread + norm_epsilon)
    return centre * rstd, rstd


def norm_back(x, gain, grad):
    hat, rstd = norm_parts(x)
    inner = grad * gain
    back = inner - jnp.mean(inner, axis=-1, keepdims=True) - hat * jnp.mean(inner * hat, axis=-1, keepdims=True)
    return rstd * back, grad * hat


def fold8(x):
    total = x[:8]
    for k in range(1, x.shape[0] // 8):
        total = total + x[k * 8 : k * 8 + 8]
    return total


def pair_bias(seg_row, seg_col, bias):
    length = bias.shape[0]
    i = lax.broadcasted_iota(jnp.int32, (length, length), 0)
    j = lax.broadcasted_iota(jnp.int32, (length, length), 1)
    apart = jnp.abs(i - j).astype(f32)
    bias[...] = jnp.where(seg_col == seg_row, apart, masked_distance)


def attend_kernel(slopes, x, gain, w, seg_row, seg_col, y, a, qkv, o, lse, bias):
    pair = pl.program_id(1)
    length, width = x.shape
    half = width // HEADS
    two = 2 * half
    rows = ROWS

    @pl.when(pair == 0)
    def _():
        pair_bias(seg_row[0], seg_col[0], bias)

        @pl.loop(0, length // rows)
        def _(i):
            at = pl.ds(pl.multiple_of(i * rows, rows), rows)
            hat, _ = norm_parts(x[at])
            low = (hat * gain[...]).astype(bf16)
            a[at] = low
            for k in range(3):
                part = mm(low, w[k])
                if k == 0:
                    part = part.astype(bf16).astype(f32) * half ** (-0.5)
                qkv[at, k * width : (k + 1) * width] = part.astype(bf16)

    lanes = pl.ds(pl.multiple_of(pair * two, two), two)
    q = qkv[:, pl.ds(pl.multiple_of(pair * two, two), two)]
    k = qkv[:, pl.ds(pl.multiple_of(width + pair * two, two), two)]
    v = qkv[:, pl.ds(pl.multiple_of(2 * width + pair * two, two), two)]
    v_t = v.astype(f32).T.astype(bf16)
    left = lax.broadcasted_iota(jnp.int32, (length, two), 1) < half
    zero = jnp.zeros_like(q)
    out = []
    for e in range(2):
        slope = slopes[2 * pair + e]
        q_e = jnp.where(left, q, zero) if e == 0 else jnp.where(left, zero, q)
        s = mm(k, q_e, NT) - slope * bias[...]
        top = jnp.max(s, axis=0, keepdims=True)
        p = jnp.exp(s - top)
        total = jnp.sum(p, axis=0, keepdims=True)
        low = (p * (1.0 / total)).astype(bf16)
        out.append(mm(v_t, low))
        lse[0, pl.ds(2 * pair + e, 1)] = top + jnp.log(total)
    upper = lax.broadcasted_iota(jnp.int32, (two, length), 0) < half
    o[:, lanes] = jnp.where(upper, out[0], out[1]).T.astype(bf16)

    @pl.when(pair == pl.num_programs(1) - 1)
    def _():
        @pl.loop(0, length // rows)
        def _(i):
            at = pl.ds(pl.multiple_of(i * rows, rows), rows)
            y[at] = x[at] + mm(o[at], w[3])


def attend(x, gain, weights, layer, seg):
    packs, length = seg.shape
    tokens, width = x.shape
    per_layer4 = weights.shape[0] // LAYERS // 4
    slopes = head_slopes(HEADS)
    whole = lambda shape: pl.BlockSpec(shape, lambda m, p: (m,) + (0,) * (len(shape) - 1))
    fixed = lambda shape, at: pl.BlockSpec(shape, lambda m, p: at)
    return pl.pallas_call(
        attend_kernel,
        grid=(packs, HEADS // 2),
        in_specs=[
            pl.BlockSpec(memory_space=pltpu.SMEM),
            whole((length, width)),
            fixed((1, width), (0, 0)),
            fixed((4, width, width), (per_layer4 * layer, 0, 0)),
            whole((1, 1, length)),
            whole((1, length, 1)),
        ],
        out_specs=[
            whole((length, width)),
            whole((length, width)),
            whole((length, 3 * width)),
            whole((length, width)),
            whole((1, HEADS, length)),
        ],
        out_shape=[
            jax.ShapeDtypeStruct((tokens, width), f32),
            jax.ShapeDtypeStruct((tokens, width), bf16),
            jax.ShapeDtypeStruct((tokens, 3 * width), bf16),
            jax.ShapeDtypeStruct((tokens, width), bf16),
            jax.ShapeDtypeStruct((packs, HEADS, length), f32),
        ],
        scratch_shapes=[pltpu.VMEM((length, length), f32)],
        compiler_params=pltpu.CompilerParams(vmem_limit_bytes=48 << 20),
        name="attend",
    )(slopes, x, gain.reshape(1, width), weights, seg.reshape(packs, 1, length), seg.reshape(packs, length, 1))


def attend_back_kernel(
    slopes, dx, x, gain, w, a, qkv, o, lse, seg_row, seg_col, new, dgain, gw, bias, do, dqkv, acc
):
    pack, pair = pl.program_id(0), pl.program_id(1)
    length, width = x.shape
    half = width // HEADS
    two = 2 * half
    rows = ROWS

    @pl.when(pair == 0)
    def _():
        pair_bias(seg_row[0], seg_col[0], bias)

        @pl.loop(0, length // rows)
        def _(i):
            at = pl.ds(pl.multiple_of(i * rows, rows), rows)
            do[at] = mm(dx[at].astype(bf16), w[3], NT).astype(bf16)

        part = mm(o[...], dx[...].astype(bf16), TN)

        @pl.when(pack == 0)
        def _():
            acc[3] = part

        @pl.when(pack > 0)
        def _():
            acc[3] += part

    lanes = [pl.ds(pl.multiple_of(n * width + pair * two, two), two) for n in range(3)]
    q, k, v = [qkv[:, at] for at in lanes]
    do_p = do[:, lanes[0]]
    k_t = k.astype(f32).T.astype(bf16)
    left = lax.broadcasted_iota(jnp.int32, (length, two), 1) < half
    upper = lax.broadcasted_iota(jnp.int32, (two, length), 0) < half
    zero = jnp.zeros_like(q)
    dq, dk, dv = [], [], []
    for e in range(2):
        slope = slopes[2 * pair + e]
        keep = (lambda t: jnp.where(left, t, zero)) if e == 0 else (lambda t: jnp.where(left, zero, t))
        s = mm(k, keep(q), NT) - slope * bias[...]
        p = jnp.exp(s - lse[0, pl.ds(2 * pair + e, 1)])
        dp = mm(v, keep(do_p), NT)
        inner = jnp.sum(p * dp, axis=0, keepdims=True)
        ds = (p * (dp - inner)).astype(bf16)
        dv.append(mm(p.astype(bf16), do_p))
        dk.append(mm(ds, q))
        dq.append(mm(k_t, ds))
    dqkv[:, lanes[0]] = (jnp.where(upper, dq[0], dq[1]).T * half ** (-0.5)).astype(bf16)
    dqkv[:, lanes[1]] = jnp.where(left, dk[0], dk[1]).astype(bf16)
    dqkv[:, lanes[2]] = jnp.where(left, dv[0], dv[1]).astype(bf16)

    @pl.when(pair == pl.num_programs(1) - 1)
    def _():
        def chunk(i, total):
            at = pl.ds(pl.multiple_of(i * rows, rows), rows)
            da = mm(dqkv[at, :width], w[0], NT)
            da = da + mm(dqkv[at, width : 2 * width], w[1], NT)
            da = da + mm(dqkv[at, 2 * width :], w[2], NT)
            back, extra = norm_back(x[at], gain[...], da)
            new[at] = dx[at] + back
            return total + fold8(extra)

        dgain[0] = lax.fori_loop(0, length // rows, chunk, jnp.zeros((8, width), f32))
        for n in range(3):
            part = mm(a[...], dqkv[:, n * width : (n + 1) * width], TN)

            @pl.when(pack == 0)
            def _(part=part, n=n):
                acc[n] = part

            @pl.when(pack > 0)
            def _(part=part, n=n):
                acc[n] += part

    @pl.when((pair == pl.num_programs(1) - 1) & (pack == pl.num_programs(0) - 1))
    def _():
        for n in range(4):
            gw[n] = acc[n].astype(bf16)


def attend_back(dx, x, gain, weights, layer, seg, kept):
    a, qkv, o, lse = kept
    packs, length = seg.shape
    tokens, width = x.shape
    per_layer4 = weights.shape[0] // LAYERS // 4
    whole = lambda shape: pl.BlockSpec(shape, lambda m, p: (m,) + (0,) * (len(shape) - 1))
    fixed = lambda shape, at: pl.BlockSpec(shape, lambda m, p: at)
    return pl.pallas_call(
        attend_back_kernel,
        grid=(packs, HEADS // 2),
        in_specs=[
            pl.BlockSpec(memory_space=pltpu.SMEM),
            whole((length, width)),
            whole((length, width)),
            fixed((1, width), (0, 0)),
            fixed((4, width, width), (per_layer4 * layer, 0, 0)),
            whole((length, width)),
            whole((length, 3 * width)),
            whole((length, width)),
            whole((1, HEADS, length)),
            whole((1, 1, length)),
            whole((1, length, 1)),
        ],
        out_specs=[
            whole((length, width)),
            whole((1, 8, width)),
            fixed((4, width, width), (0, 0, 0)),
        ],
        out_shape=[
            jax.ShapeDtypeStruct((tokens, width), f32),
            jax.ShapeDtypeStruct((packs, 8, width), f32),
            jax.ShapeDtypeStruct((4, width, width), bf16),
        ],
        scratch_shapes=[
            pltpu.VMEM((length, length), f32),
            pltpu.VMEM((length, width), bf16),
            pltpu.VMEM((length, 3 * width), bf16),
            pltpu.VMEM((4, width, width), f32),
        ],
        compiler_params=pltpu.CompilerParams(vmem_limit_bytes=56 << 20),
        name="attend_back",
    )(
        head_slopes(HEADS),
        dx,
        x,
        gain.reshape(1, width),
        weights,
        a,
        qkv,
        o,
        lse,
        seg.reshape(packs, 1, length),
        seg.reshape(packs, length, 1),
    )


ROWS = 512
gelu_c = math.sqrt(2.0 / math.pi)


def feed_kernel(x, gain, wg, wu, wd, y, f, gate, up):
    k = pl.program_id(0)
    tokens = x.shape[0]
    rows = ROWS

    @pl.loop(0, tokens // rows)
    def _(i):
        at = pl.ds(pl.multiple_of(i * rows, rows), rows)

        @pl.when(k == 0)
        def _():
            hat, _ = norm_parts(x[at])
            f[at] = (hat * gain[...]).astype(bf16)
            y[at] = x[at]

        low = f[at]
        g = mm(low, wg[0]).astype(bf16)
        u = mm(low, wu[0]).astype(bf16)
        gate[0, at] = g
        up[0, at] = u
        g, u = g.astype(f32), u.astype(f32)
        cdf = 0.5 * (1.0 + jnp.tanh(gelu_c * (g + 0.044715 * (g * g * g))))
        hidden = (g * cdf * u).astype(bf16)
        y[at] += mm(hidden, wd[0])


def feed(x, gain, weights, layer):
    tokens, width = x.shape
    per_layer = weights.shape[0] // LAYERS
    pieces = FF // width
    fixed = lambda shape: pl.BlockSpec(shape, lambda k: (0,) * len(shape))
    block = lambda skip: pl.BlockSpec((1, width, width), lambda k: (per_layer * layer + skip + k, 0, 0))
    each = pl.BlockSpec((1, tokens, width), lambda k: (k, 0, 0))
    return pl.pallas_call(
        feed_kernel,
        grid=(pieces,),
        in_specs=[fixed((tokens, width)), fixed((1, width)), block(4), block(4 + pieces), block(4 + 2 * pieces)],
        out_specs=[fixed((tokens, width)), fixed((tokens, width)), each, each],
        out_shape=[
            jax.ShapeDtypeStruct((tokens, width), f32),
            jax.ShapeDtypeStruct((tokens, width), bf16),
            jax.ShapeDtypeStruct((pieces, tokens, width), bf16),
            jax.ShapeDtypeStruct((pieces, tokens, width), bf16),
        ],
        compiler_params=pltpu.CompilerParams(vmem_limit_bytes=48 << 20),
        name="feed",
    )(x, gain.reshape(1, width), weights, weights, weights)


def feed_back_kernel(dx, x, gain, wg, wu, wd, f, gate, up, new, dgain, gg, gu, gd, f_t, dz, hid, dg, du):
    k = pl.program_id(0)
    tokens, width = x.shape
    rows = ROWS
    last = pl.num_programs(0) - 1

    @pl.when(k == 0)
    def _():
        @pl.loop(0, tokens // rows)
        def _(i):
            at = pl.ds(pl.multiple_of(i * rows, rows), rows)
            f_t[:, at] = f[at].astype(f32).T.astype(bf16)
            dz[at] = dx[at].astype(bf16)
            new[at] = jnp.zeros((rows, width), f32)

    def chunk(i, total):
        at = pl.ds(pl.multiple_of(i * rows, rows), rows)
        dh = mm(dz[at], wd[0], NT)
        g, u = gate[0, at].astype(f32), up[0, at].astype(f32)
        square = g * g
        t = jnp.tanh(gelu_c * (g + 0.044715 * (square * g)))
        cdf = 0.5 * (1.0 + t)
        act = g * cdf
        slope = cdf + 0.5 * g * (1.0 - t * t) * (gelu_c * (1.0 + 3 * 0.044715 * square))
        hid[at] = (act * u).astype(bf16)
        dgate = (dh * u * slope).astype(bf16)
        dup = (dh * act).astype(bf16)
        dg[at] = dgate
        du[at] = dup
        new[at] += mm(dgate, wg[0], NT) + mm(dup, wu[0], NT)
        return total

    lax.fori_loop(0, tokens // rows, chunk, 0)
    gg[0] = mm(f_t[...], dg[...]).astype(bf16)
    gu[0] = mm(f_t[...], du[...]).astype(bf16)
    gd[0] = mm(hid[...], dz[...], TN).astype(bf16)

    @pl.when(k == last)
    def _():
        def finish(i, total):
            at = pl.ds(pl.multiple_of(i * rows, rows), rows)
            back, extra = norm_back(x[at], gain[...], new[at])
            new[at] = dx[at] + back
            return total + fold8(extra)

        dgain[...] = lax.fori_loop(0, tokens // rows, finish, jnp.zeros((8, width), f32))


def feed_back(dx, x, gain, weights, layer, kept):
    f, gate, up = kept
    tokens, width = x.shape
    per_layer = weights.shape[0] // LAYERS
    pieces = FF // width
    fixed = lambda shape: pl.BlockSpec(shape, lambda k: (0,) * len(shape))
    block = lambda skip: pl.BlockSpec((1, width, width), lambda k: (per_layer * layer + skip + k, 0, 0))
    each = pl.BlockSpec((1, tokens, width), lambda k: (k, 0, 0))
    grad = pl.BlockSpec((1, width, width), lambda k: (k, 0, 0))
    return pl.pallas_call(
        feed_back_kernel,
        grid=(pieces,),
        in_specs=[
            fixed((tokens, width)),
            fixed((tokens, width)),
            fixed((1, width)),
            block(4),
            block(4 + pieces),
            block(4 + 2 * pieces),
            fixed((tokens, width)),
            each,
            each,
        ],
        out_specs=[fixed((tokens, width)), fixed((8, width)), grad, grad, grad],
        out_shape=[
            jax.ShapeDtypeStruct((tokens, width), f32),
            jax.ShapeDtypeStruct((8, width), f32),
        ]
        + [jax.ShapeDtypeStruct((pieces, width, width), bf16)] * 3,
        scratch_shapes=[
            pltpu.VMEM((width, tokens), bf16),
            pltpu.VMEM((tokens, width), bf16),
            pltpu.VMEM((tokens, width), bf16),
            pltpu.VMEM((tokens, width), bf16),
            pltpu.VMEM((tokens, width), bf16),
        ],
        compiler_params=pltpu.CompilerParams(vmem_limit_bytes=56 << 20),
        name="feed_back",
    )(dx, x, gain.reshape(1, width), weights, weights, weights, f, gate, up)


def two_parts(x):
    top = x.astype(bf16)
    return top, (x - top.astype(f32)).astype(bf16)


def mm3(a, b, dims=None):
    (a1, a2), (b1, b2) = a, b
    return mm(a1, b1, dims) + (mm(a1, b2, dims) + mm(a2, b1, dims))


def turn_kernel(scalars, numbers, left, right, some, grad, m, v, m_new, v_new, turned):
    slot = pl.program_id(0)
    factor, first_fix, second_fix = numbers[0], numbers[1], numbers[2]
    bases = two_parts(right[0])
    left_top, left_rest = two_parts(left[0])
    rotated = mm(left_top, grad[0], TN) + mm(left_rest, grad[0], TN)
    rotated = factor * mm3(two_parts(rotated), bases)
    moment, second, step = adam_moments(m[0], v[0], rotated, first_fix, second_fix)
    live = scalars[1 + slot] > 0
    m_new[0] = jnp.where(live, moment, m[0])
    v_new[0] = jnp.where(live, second, v[0])
    groups, _, rows, width = turned.shape
    rows_here = some[...].reshape(groups * rows, width)
    out = mm3(two_parts(rows_here), two_parts(step))
    out = mm3(two_parts(out), bases, NT)
    turned[...] = out.astype(turned.dtype).reshape(turned.shape)


def turn_slots(replica, live, numbers, left, right, grads, m, v):
    cap, width, _ = left.shape
    groups = width // 64
    scalars = jnp.concatenate([replica.reshape(1), live.astype(jnp.int32)])
    view = left.reshape(cap, groups, 4, 16, width)
    whole = pl.BlockSpec((1, width, width), lambda s, scalars: (s, 0, 0))
    grid_spec = pltpu.PrefetchScalarGridSpec(
        num_scalar_prefetch=1,
        grid=(cap,),
        in_specs=[
            pl.BlockSpec(memory_space=pltpu.SMEM),
            whole,
            whole,
            pl.BlockSpec((1, groups, 1, 16, width), lambda s, scalars: (s, 0, scalars[0], 0, 0)),
            whole,
            whole,
            whole,
        ],
        out_specs=[whole, whole, pl.BlockSpec((groups, 1, 16, width), lambda s, scalars: (0, s, 0, 0))],
    )
    return pl.pallas_call(
        turn_kernel,
        grid_spec=grid_spec,
        out_shape=[
            jax.ShapeDtypeStruct(m.shape, f32),
            jax.ShapeDtypeStruct(v.shape, f32),
            jax.ShapeDtypeStruct((groups, cap, 16, width), bf16),
        ],
        compiler_params=pltpu.CompilerParams(vmem_limit_bytes=56 << 20),
        name="turn_slots",
    )(scalars, numbers, left, right, view, grads, m, v)


class Transport:
    def __init__(self, n_rep, n_fsdp, shard_rows):
        self.sizes = (n_rep, n_fsdp)
        self.kernels = n_rep == 4 and n_fsdp == 8 and shard_rows == 64

    def ask(self, cid, wanted, facts, gains):
        if self.kernels:
            return ask_group(self.sizes, cid, wanted, facts, gains)
        asked = lax.all_to_all(wanted, "fsdp", split_axis=0, concat_axis=0, tiled=True)
        return asked, lax.all_gather(facts, "fsdp"), lax.all_gather(gains, "fsdp"), lax.pmax(facts, ("rep", "fsdp"))

    def spread(self, cid, x):
        if self.kernels:
            return group_exchange(self.sizes, cid, x, True)
        return lax.all_to_all(x, "fsdp", split_axis=0, concat_axis=0, tiled=True)

    def share(self, cid, x):
        if self.kernels:
            return group_exchange(self.sizes, cid, x, False)
        return lax.all_gather(x, "fsdp")

    def share_rows(self, cid, x):
        if self.kernels:
            return ring_rows(self.sizes, cid, x)
        return lax.all_gather(x, "fsdp")

    def sum_rows(self, cid, x):
        if self.kernels:
            return reduce_rows(self.sizes, cid, x)
        return lax.psum_scatter(x.astype(f32), "fsdp", scatter_dimension=0)

    def weights(self, cid, shard):
        if self.kernels:
            return gather_weights(self.sizes, cid, shard)
        return lax.all_gather(shard, "fsdp", axis=1, tiled=True)


def body(
    token_ids,
    segment_ids,
    masked_pos,
    labels,
    blocks,
    gains,
    embed,
    embed_m,
    embed_v,
    gains_m,
    gains_v,
    soap_m,
    soap_v,
    left_basis,
    right_basis,
    block_slots,
    step_count,
):
    groups = lax.axis_size("fsdp")
    replicas = lax.axis_size("rep")
    member = lax.axis_index("fsdp")
    replica = lax.axis_index("rep")
    micro_count = token_ids.shape[0]
    pack_length = token_ids.shape[2]
    pick_count = masked_pos.shape[2]
    vocab_rows, model_width = embed.shape
    block_count, shard_rows, _ = blocks.shape
    gain_count = gains.shape[0]
    tokens = micro_count * pack_length
    picks = micro_count * pick_count
    move = Transport(replicas, groups, shard_rows)
    table_low = embed.astype(bf16)

    ids = token_ids.reshape(tokens)
    index = jnp.arange(tokens, dtype=jnp.int32)
    owner = ids // vocab_rows
    local = ids - owner * vocab_rows
    first_at = jnp.min(jnp.where(ids[:, None] == ids[None, :], index[None, :], tokens), axis=1)
    is_first = first_at == index
    ahead = is_first[None, :] & (owner[:, None] == owner[None, :]) & (index[None, :] < first_at[:, None])
    rank = jnp.sum(ahead.astype(jnp.int32), axis=1)
    most = jnp.max(rank) + 1

    my_labels = labels.reshape(picks // 128, 128)
    facts = jnp.concatenate(
        [my_labels, jnp.full((8 - picks // 128, 128), most, jnp.int32)], axis=0
    )
    gain_pad = jnp.pad(gains, ((0, 8 - gain_count), (0, 128 - gains.shape[1])))
    slots = groups * CAPACITY
    most_rounds = (tokens + CAPACITY - 1) // CAPACITY
    slot_index = jnp.arange(slots, dtype=jnp.int32)

    def slot_of(k):
        here = rank - k * CAPACITY
        return jnp.where((here >= 0) & (here < CAPACITY), owner * CAPACITY + here, -1)

    def wanted_in(slot):
        wanted = jnp.where((slot[None, :] == slot_index[:, None]) & is_first[None, :], local[None, :], 0)
        return jnp.sum(wanted, axis=1).reshape(groups, 1, CAPACITY)

    def rows_for(cid, slot, asked):
        rows = jnp.take(table_low, asked.reshape(slots), axis=0)
        rows = move.spread(cid, rows.reshape(groups, CAPACITY, model_width)).reshape(slots, model_width)
        return jnp.dot((slot[:, None] == slot_index[None, :]).astype(bf16), rows, preferred_element_type=f32)

    slot = slot_of(0)
    asked, group_facts, gain_rows, most_facts = move.ask(0, wanted_in(slot), facts, gain_pad)
    rounds = (most_facts[7, 0] + CAPACITY - 1) // CAPACITY
    all_labels = group_facts[:, : picks // 128].reshape(groups * picks)
    gain_rows = gain_rows[:, :gain_count, : gains.shape[1]].transpose(1, 0, 2).reshape(gain_count, model_width)
    gain_rows = lax.reduce_precision(gain_rows, exponent_bits=8, mantissa_bits=7)
    embedded = rows_for(2, slot, asked)
    asked_all = jnp.zeros((most_rounds, slots), jnp.int32).at[0].set(asked.reshape(slots))

    def look(state):
        k, rows_so_far, asked_all = state
        slot = slot_of(k)
        asked = move.spread(1, wanted_in(slot))
        asked_all = lax.dynamic_update_index_in_dim(asked_all, asked.reshape(slots), k, 0)
        return k + 1, rows_so_far + rows_for(12, slot, asked), asked_all

    _, embedded, asked_all = lax.while_loop(lambda s: s[0] < rounds, look, (jnp.int32(1), embedded, asked_all))

    full_blocks = move.weights(3, blocks.astype(bf16))

    segments = segment_ids.reshape(micro_count, pack_length)
    stream, first_pull = jax.vjp(layer_norm, embedded, gain_rows[0])
    saved_layers = []
    for layer in range(LAYERS):
        middle, *attention_kept = attend(stream, gain_rows[1 + 2 * layer], full_blocks, layer, segments)
        after, *feed_kept = feed(middle, gain_rows[2 + 2 * layer], full_blocks, layer)
        saved_layers.append((stream, attention_kept, middle, feed_kept))
        stream = after
    final_rows, final_pull = jax.vjp(layer_norm, stream, gain_rows[gain_count - 1])

    positions = masked_pos.reshape(micro_count, pick_count)
    flat_positions = (positions + jnp.arange(micro_count, dtype=jnp.int32)[:, None] * pack_length).reshape(picks)
    picked = jnp.take(final_rows, flat_positions, axis=0).astype(bf16)
    all_picked = move.share_rows(4, picked).reshape(groups * picks, model_width)
    logits = jnp.einsum("td,vd->tv", all_picked, table_low, preferred_element_type=f32)
    top_value = jnp.max(logits, axis=-1)
    exp_total = jnp.sum(jnp.exp(logits - top_value[:, None]), axis=-1)
    label_local = all_labels - member * vocab_rows
    columns = jnp.arange(vocab_rows, dtype=jnp.int32)
    label_hits = columns[None, :] == label_local[:, None]
    target = jnp.sum(jnp.where(label_hits, logits, 0.0), axis=-1)
    stats = move.share(5, jnp.stack([top_value, exp_total, target]))
    top_all = jnp.max(stats[:, 0], axis=0)
    total_all = jnp.sum(stats[:, 1] * jnp.exp(stats[:, 0] - top_all[None]), axis=0)
    target_all = jnp.sum(stats[:, 2], axis=0)
    entropy = top_all + jnp.log(total_all) - target_all
    loss_local = jnp.sum(lax.dynamic_slice_in_dim(entropy, member * picks, picks))
    grad_logits = (
        jnp.exp(logits - top_all[:, None]) / total_all[:, None] - label_hits.astype(f32)
    ).astype(bf16)
    grad_table = jnp.einsum("tv,td->vd", grad_logits, all_picked, preferred_element_type=f32)
    grad_picked = jnp.einsum("tv,vd->td", grad_logits, table_low, preferred_element_type=f32)
    grad_picked = move.sum_rows(6, grad_picked.astype(bf16).reshape(groups, picks, model_width))

    match = flat_positions[None, :] == index[:, None]
    place = jnp.sum(jnp.where(match, jnp.arange(picks, dtype=jnp.int32)[None, :] + 1, 0), axis=1)
    grad_final = jnp.where(
        (place > 0)[:, None], jnp.take(grad_picked, jnp.maximum(place - 1, 0), axis=0), 0.0
    )
    grad_stream, grad_final_gain = final_pull(grad_final)
    gain_grads = [None] * gain_count
    gain_grads[gain_count - 1] = grad_final_gain
    layer_grads = [None] * LAYERS
    for layer in reversed(range(LAYERS)):
        before, attention_kept, middle, feed_kept = saved_layers[layer]
        grad_stream, feed_gain, *grads_feed = feed_back(
            grad_stream, middle, gain_rows[2 + 2 * layer], full_blocks, layer, feed_kept
        )
        grad_stream, attention_gain, grads_attention = attend_back(
            grad_stream, before, gain_rows[1 + 2 * layer], full_blocks, layer, segments, attention_kept
        )
        gain_grads[1 + 2 * layer] = jnp.sum(attention_gain, axis=(0, 1))
        gain_grads[2 + 2 * layer] = jnp.sum(feed_gain, axis=0)
        layer_grads[layer] = [grads_attention] + grads_feed
    grad_embedded, gain_grads[0] = first_pull(grad_stream)
    grad_rows = grad_embedded.astype(bf16)
    padded_rows = -(-vocab_rows // 384) * 384
    grad_table = jnp.pad(grad_table, ((0, padded_rows - vocab_rows), (0, 0)))
    row_index = jnp.arange(padded_rows, dtype=jnp.int32)

    def given(cid, k, grad_table):
        chosen = (slot_index[:, None] == slot_of(k)[None, :]).astype(bf16)
        rows = jnp.dot(chosen, grad_rows, preferred_element_type=f32).astype(bf16)
        rows = move.spread(cid, rows.reshape(groups, CAPACITY, model_width)).reshape(slots, model_width)
        asked = lax.dynamic_index_in_dim(asked_all, k, 0, keepdims=False)
        target_rows = (row_index[:, None] == asked[None, :]).astype(bf16)
        return grad_table + jnp.dot(target_rows, rows, preferred_element_type=f32)

    grad_table = given(7, 0, grad_table)
    _, grad_table = lax.while_loop(
        lambda s: s[0] < rounds, lambda s: (s[0] + 1, given(13, s[0], s[1])), (jnp.int32(1), grad_table)
    )
    grad_blocks = [g for grads in layer_grads for g in grads]
    grad_gains = jnp.stack(gain_grads, axis=0)

    position_count = micro_count * replicas * groups * pick_count
    clip_limit = clip_ratio * math.sqrt(position_count)
    steps_done = step_count[0].astype(f32)
    first_fix = 1.0 - beta_first**steps_done
    second_fix = 1.0 - beta_second**steps_done
    slot_cap = soap_m.shape[0]
    slot_total = slot_cap * groups
    named = jnp.arange(slot_total, dtype=jnp.int32)[:, None] == block_slots[None, :]
    taken = jnp.any(named, axis=1)
    block_of = jnp.sum(jnp.where(named, jnp.arange(block_count, dtype=jnp.int32)[None, :], 0), axis=1)

    small = jnp.zeros((8, model_width), f32).at[:gain_count].set(grad_gains)
    small = small.at[7, 0].set(loss_local)
    if move.kernels:
        mine, grad_table, squares = reduce_gradients(
            move.sizes, 8, grad_blocks, grad_table.reshape(4, padded_rows // 4, model_width)
        )
        grad_table = grad_table.reshape(padded_rows, model_width)[:vocab_rows]
        small = total_everyone(move.sizes, 9, small.at[6].set(jnp.sum(squares, axis=(0, 1))))
        squares = jnp.sum(small[6])
        outgoing = jnp.where(taken[:, None, None], jnp.take(mine.astype(bf16), block_of, axis=0), 0)
        owned = exchange_slots(move.sizes, 10, outgoing.reshape(groups, slot_cap, 16, model_width), True)
        owned = owned.reshape(slot_cap, model_width, model_width)
    else:
        grad_blocks = jnp.concatenate([g.astype(f32) for g in grad_blocks], axis=0)
        mine = lax.psum_scatter(grad_blocks, "fsdp", scatter_dimension=1, tiled=True)
        mine, grad_table = lax.psum((mine, grad_table[:vocab_rows]), "rep")
        small = lax.psum(small, ("rep", "fsdp"))
        squares = lax.psum(jnp.sum(mine * mine) + jnp.sum(grad_table * grad_table), "fsdp")
        outgoing = jnp.where(taken[:, None, None], jnp.take(mine, block_of, axis=0), 0)
        owned = lax.all_to_all(outgoing, "fsdp", split_axis=0, concat_axis=1, tiled=True)
    loss_all = small[7, 0]
    grad_gains = small[:gain_count]
    grad_norm = jnp.sqrt(squares + jnp.sum(grad_gains * grad_gains))
    factor = jnp.minimum(1.0, clip_limit / grad_norm)
    grad_gains = lax.dynamic_slice_in_dim(grad_gains, member * gains.shape[1], gains.shape[1], axis=1)

    live = lax.dynamic_slice_in_dim(taken, member * slot_cap, slot_cap)
    if move.kernels:
        soap_m_new, soap_v_new, turned = turn_slots(
            replica,
            live,
            jnp.stack([factor, first_fix, second_fix]),
            left_basis,
            right_basis,
            owned,
            soap_m,
            soap_v,
        )
        returned = exchange_slots(move.sizes, 11, turned, False)
        returned = returned.reshape(slot_total, shard_rows, model_width)
    else:
        rotated = jnp.einsum("bji,bjk->bik", left_basis, owned, precision=high)
        rotated = factor * jnp.einsum("bik,bkl->bil", rotated, right_basis, precision=high)
        moment_first, moment_second, rotated_step = adam_moments(soap_m, soap_v, rotated, first_fix, second_fix)
        soap_m_new = jnp.where(live[:, None, None], moment_first, soap_m)
        soap_v_new = jnp.where(live[:, None, None], moment_second, soap_v)
        turned = jnp.einsum("bij,bjk->bik", left_basis, rotated_step, precision=high)
        turned = jnp.einsum("bik,blk->bil", turned, right_basis, precision=high)
        returned = lax.all_to_all(turned, "fsdp", split_axis=1, concat_axis=0, tiled=True)
    update = jnp.take(returned, block_slots, axis=0).astype(f32)
    blocks_new = blocks - step_rate * (update + weight_decay * blocks)

    embed_m_new, embed_v_new, table_step = adam_moments(
        embed_m, embed_v, factor * grad_table, first_fix, second_fix
    )
    embed_new = embed - step_rate * (table_step + weight_decay * embed)
    gains_m_new, gains_v_new, gain_step = adam_moments(
        gains_m, gains_v, factor * grad_gains, first_fix, second_fix
    )
    gains_new = gains - step_rate * gain_step
    loss = (loss_all / position_count).reshape(1)
    return (
        loss,
        grad_norm.reshape(1),
        blocks_new,
        gains_new,
        embed_new,
        embed_m_new,
        embed_v_new,
        gains_m_new,
        gains_v_new,
        soap_m_new,
        soap_v_new,
        blocks_new.astype(bf16),
        embed_new.astype(bf16),
    )


def solution(mesh):
    packs = P(None, ("rep", "fsdp"), None)
    rows = P(None, "fsdp", None)
    columns = P(None, "fsdp")
    table = P("fsdp", None)
    slots = P("fsdp", None, None)
    return jax.shard_map(
        body,
        mesh=mesh,
        in_specs=(packs,) * 4
        + (rows, columns)
        + (table,) * 3
        + (columns,) * 2
        + (slots,) * 4
        + (P(), P()),
        out_specs=(P(), P(), rows, columns)
        + (table,) * 3
        + (columns,) * 2
        + (slots,) * 2
        + (rows, table),
        check_vma=False,
    )
```

time: 2660 us -> 781 us (0.29)
  waiting for transfers between devices: 1520 us -> 0 us
  Pallas kernels: 0 us -> 579 us
  matrix products: 340 us -> 48.6 us
  blocking collectives: 255 us -> 0 us
  local copies, waits for them, and re-layouts: 251 us -> 34.9 us
  other arithmetic: 232 us -> 101 us
    reduce_scatter x5 -> x0, waiting for transfers between devices: 733 us -> none  [the longest x1 452 us: body(): lax.psum_scatter(step_blocks, 'fsdp', scatter_dimension=1, tiled=True)]
    pallas_call x0 -> x20, Pallas kernels: none -> 579 us  [the longest x1 117 us: reduce_gradients(): pl.pallas_call(partial(reduce_kernel, n_rep, n, half, table_rows, each),...]
    all_to_all x2 -> x0, waiting for transfers between devices: 296 us -> none  [the longest x1 159 us: body(): lax.all_to_all(turned, 'fsdp', split_axis=1, concat_axis=0, tiled=True)]
    dot_general x84 -> x6, matrix products: 340 us -> 48.6 us  [the longest x1 17 us: body(): jnp.einsum('td,vd->tv', all_picked, table_low, preferred_element_type=f32)]
    all_gather x11 -> x0, blocking collectives: 232 us -> none  [the longest x6 145 us: merged(): pieces = jax.tree.map(lambda part: lax.all_gather(part, axis), value)]
    all_gather x5 -> x0, waiting for transfers between devices: 229 us -> none  [the longest x1 222 us: body(): lax.all_gather(blocks_low, 'fsdp', axis=1, tiled=True)]
    psum x1 -> x0, waiting for transfers between devices: 207 us -> none  [body(): lax.psum((grad_blocks, grad_gains, grad_table, loss_local), 'rep')]
    scatter-add x4 -> x0, other arithmetic: 66.3 us -> none  [the longest x2 60.7 us: body(): jax.ops.segment_sum(all_grad_rows.astype(jnp.float32), target_rows, num_s...]
  transfers between devices with their start and end apart: 14 -> 0, of which waited for: 11 -> 0; matrix products, arithmetic and copies ran while one was open for 13% -> 0% of each run, Pallas kernels for 0% -> 0%
where the time goes in v1:
time: 781 us; the launch traced here: 772 us
  Pallas kernels  579 us (74%)
  other arithmetic  101 us (13%)
  matrix products  48.6 us (6%)
  local copies, waits for them, and re-layouts  34.9 us (4%)
  between operations  8.35 us (1%)
    pallas_call x1, Pallas kernels, reduce_gradients(): pl.pallas_call(partial(reduce_kernel, n_rep, n, half, table_rows, each),...  117 us
    pallas_call x1, Pallas kernels, gather_weights(): pl.pallas_call(partial(weights_kernel, n_rep, n, half, half - 2 * (half /...  74.3 us
    pallas_call x2, Pallas kernels, exchange_slots(): pl.pallas_call(partial(slots_kernel, n_rep, n, to_slots), out_shape=jax.S...  68 us
    pallas_call x2, Pallas kernels, feed_back(): pl.pallas_call(feed_back_kernel, grid=(pieces,), in_specs=[fixed((tokens,...  58.4 us
    pallas_call x2, Pallas kernels, attend_back(): pl.pallas_call(attend_back_kernel, grid=(packs, HEADS // 2), in_specs=[pl...  55.4 us
    pallas_call x3, Pallas kernels, group_exchange(): pl.pallas_call(partial(group_kernel, n_rep, n, spread), out_shape=jax.Sha...  50.5 us
    pallas_call x2, Pallas kernels, attend(): pl.pallas_call(attend_kernel, grid=(packs, HEADS // 2), in_specs=[pl.Bloc...  35.5 us
    pallas_call x1, Pallas kernels, ring_rows(): pl.pallas_call(partial(ring_rows_kernel, n_rep, n), out_shape=jax.ShapeDt...  28.6 us

profile of v1, /device:TPU:25, one launch (start us, length us, event | category | flops | bytes accessed | tf_op | source)
XLA Modules:
  0.0 772.5 jit_solution(7168555248841209657)
XLA Ops:
  10.5 12.2 %ask_group.1 = (s32[8,1,128]{2,1,0:T(1,128)}, s32[8,8,128]{2,1,0:T(8,128)}, f32[8,8,128]{2,1,0:T(8,128)}, s32[8,128]{1,0:T(8,128)}) custom-call(s32[8,1,128]{2,1,0:T(1,128)} %bitcast.173, s32[8,128]{1,0:T(8,128)} %concatenate.14.facts_ref, f32[8,128]{1,0:T(8,128)} %pad.21.gains_ref), custom_call_target="tpu_custom_call" | custom-call | tf_op jit(solution)/shard_map/ask_group/pallas_call | solution.py:158
  25.2 5.6 convert_element_type.62
  30.9 6.6 gather_fusion.1
  38.7 26.0 %group_2.1 = bf16[8,128,512]{2,1,0:T(8,128)(2,1)} custom-call(bf16[8,128,512]{2,1,0:T(8,128)(2,1)} %broadcast_select_fusion.1.x_ref), custom_call_target="tpu_custom_call" | custom-call | tf_op jit(solution)/shard_map/group_2/pallas_call | solution.py:107
  70.1 3.8 convert_element_type.63.x_ref
  74.0 74.3 %gather_weights.1.w.wg.wu.wd = bf16[32,512,512]{2,1,0:T(8,128)(2,1)} custom-call(bf16[32,64,512]{2,1,0:T(8,128)(2,1)} %convert_element_type.63.x_ref), custom_call_target="tpu_custom_call" | custom-call | tf_op jit(solution)/shard_map/gather_weights/pallas_call | solution.py:251
  148.6 17.8 %attend.2 = (f32[1024,512]{1,0:T(8,128)S(1)}, bf16[1024,512]{1,0:T(8,128)(2,1)S(1)}, bf16[1024,1536]{1,0:T(8,128)(2,1)}, bf16[1024,512]{1,0:T(8,128)(2,1)S(1)}, f32[2,8,512]{2,1,0:T(8,128)S(1)}) custom-call(f32[8]{0:T(128)S(1)} %multiply_power_fusion.slopes, f32[1024,512]{1,0:T(8,128)} %multiply_multiply_fusion.2.x, f32[1,512]{1,0:T(1,128)S(1)} %slice.136.gain, ...), custom_call_target="tpu_custom_call" | custom-call | tf_op jit(solution)/shard_map/attend/pallas_call | solution.py:837
  168.4 12.9 %feed.2 = (f32[1024,512]{1,0:T(8,128)S(1)}, bf16[1024,512]{1,0:T(8,128)(2,1)S(1)}, bf16[4,1024,512]{2,1,0:T(8,128)(2,1)}, bf16[4,1024,512]{2,1,0:T(8,128)(2,1)}) custom-call(f32[1024,512]{1,0:T(8,128)S(1)} %get-tuple-element.214.x, f32[1,512]{1,0:T(1,128)S(1)} %slice.138.gain, bf16[32,512,512]{2,1,0:T(8,128)(2,1)} %gather_weights.1.w.wg.wu.wd, ...), custom_call_target="tpu_custom_call" | custom-call | tf_op jit(solution)/shard_map/feed/pallas_call | solution.py:1041
  183.7 17.7 %attend.3 = (f32[1024,512]{1,0:T(8,128)S(1)}, bf16[1024,512]{1,0:T(8,128)(2,1)S(1)}, bf16[1024,1536]{1,0:T(8,128)(2,1)}, bf16[1024,512]{1,0:T(8,128)(2,1)S(1)}, f32[2,8,512]{2,1,0:T(8,128)S(1)}) custom-call(f32[8]{0:T(128)S(1)} %multiply_power_fusion.slopes, f32[1024,512]{1,0:T(8,128)} %copy-done.4, f32[1,512]{1,0:T(1,128)S(1)} %slice.140.gain, ...), custom_call_target="tpu_custom_call" | custom-call | tf_op jit(solution)/shard_map/attend/pallas_call | solution.py:837
  206.9 12.2 %feed.3 = (f32[1024,512]{1,0:T(8,128)S(1)}, bf16[1024,512]{1,0:T(8,128)(2,1)S(1)}, bf16[4,1024,512]{2,1,0:T(8,128)(2,1)}, bf16[4,1024,512]{2,1,0:T(8,128)(2,1)}) custom-call(f32[1024,512]{1,0:T(8,128)S(1)} %copy-done.3, f32[1,512]{1,0:T(1,128)S(1)} %slice.142.gain, bf16[32,512,512]{2,1,0:T(8,128)(2,1)} %gather_weights.1.w.wg.wu.wd, ...), custom_call_target="tpu_custom_call" | custom-call | tf_op jit(solution)/shard_map/feed/pallas_call | solution.py:1041
  223.4 28.6 %ring_rows.1 = bf16[8,256,512]{2,1,0:T(8,128)(2,1)} custom-call(bf16[256,512]{1,0:T(8,128)(2,1)} %select_convert_fusion.x_ref), custom_call_target="tpu_custom_call" | custom-call | tf_op jit(solution)/shard_map/ring_rows/pallas_call | solution.py:301
  251.9 17.0 %fusion.47 = (f32[2048]{0:T(1024)S(1)}, f32[2048,3816]{0,1:T(8,128)}) fusion(bf16[2048,512]{1,0:T(8,128)(2,1)} %bitcast.145, bf16[3816,512]{1,0:T(8,128)(2,1)} %get-tuple-element.565), kind=kOutput, calls=%fused_computation.160 | convolution fusion | flops 8010545152 | bytes 37273600 | tf_op jit(solution)/shard_map/td,vd->tv/dot_general | solution.py:1344
  269.7 14.3 %exponential_reduce_fusion = (f32[2048]{0:T(1024)S(1)}, f32[2048]{0:T(1024)S(1)}) fusion(f32[2048,3816]{0,1:T(8,128)} %get-tuple-element.392, f32[2048]{0:T(1024)S(1)} %get-tuple-element.391, s32[2048]{0:T(1024)S(1)} %bitcast.155), kind=kLoop, calls=%fused_computation.35 | loop fusion | flops 39071744 | bytes 31293440 | tf_op jit(solution)/shard_map/reduce_sum | solution.py:1346
  284.7 8.5 %group_5.1 = f32[8,3,2048]{2,1,0:T(4,128)} custom-call(f32[3,2048]{1,0:T(4,128)} %pad_maximum_fusion.x_ref), custom_call_target="tpu_custom_call" | custom-call | tf_op jit(solution)/shard_map/group_5/pallas_call | solution.py:107
  295.2 14.8 %subtract_convert_fusion = bf16[2048,3816]{0,1:T(8,128)(2,1)S(1)} fusion(f32[2048,3816]{0,1:T(8,128)} %get-tuple-element.392, f32[2048]{0:T(1024)S(1)} %fusion.29, f32[2048]{0:T(1024)S(1)} %get-tuple-element.328, s32[2048]{0:T(1024)S(1)} %bitcast.156), kind=kLoop, calls=%fused_computation.32 | loop fusion | flops 46891008 | bytes 46915584 | tf_op jit(solution)/shard_map/convert_element_type | solution.py:1359
  310.1 8.6 %convolution_convert_fusion = bf16[2048,512]{1,0:T(8,128)(2,1)S(1)} fusion(bf16[2048,3816]{0,1:T(8,128)(2,1)S(1)} %subtract_convert_fusion, bf16[3816,512]{1,0:T(8,128)(2,1)S(1)} %copy-done.19), kind=kOutput, calls=%fused_computation.59 | convolution fusion | flops 8003780608 | bytes 21635072 | tf_op jit(solution)/shard_map/tv,vd->td/dot_general | solution.py:1361
  318.7 19.1 %reduce_rows.1 = f32[256,512]{1,0:T(8,128)S(1)} custom-call(bf16[8,256,512]{2,1,0:T(8,128)(2,1)S(1)} %bitcast.125), custom_call_target="tpu_custom_call" | custom-call | tf_op jit(solution)/shard_map/reduce_rows/pallas_call | solution.py:596
  338.1 4.9 gather_fusion.3
  349.3 29.1 %feed_back.2 = (f32[1024,512]{1,0:T(8,128)}, f32[8,512]{1,0:T(8,128)}, bf16[4,512,512]{2,1,0:T(8,128)(2,1)}, bf16[4,512,512]{2,1,0:T(8,128)(2,1)}, bf16[4,512,512]{2,1,0:T(8,128)(2,1)}) custom-call(f32[1024,512]{1,0:T(8,128)} %broadcast_add_fusion.dx, f32[1024,512]{1,0:T(8,128)} %copy-done.2, f32[1,512]{1,0:T(1,128)} %copy-done.15, ...), custom_call_target="tpu_custom_call" | custom-call | tf_op jit(solution)/shard_map/feed_back/pallas_call | solution.py:1114
  378.4 27.6 %attend_back.2 = (f32[1024,512]{1,0:T(8,128)}, f32[2,8,512]{2,1,0:T(8,128)}, bf16[4,512,512]{2,1,0:T(8,128)(2,1)}) custom-call(f32[8]{0:T(128)} %copy-done.18, f32[1024,512]{1,0:T(8,128)} %get-tuple-element.222.dx, f32[1024,512]{1,0:T(8,128)} %copy-done.4, f32[1,512]{1,0:T(1,128)} %copy-done.17, bf16[32,512,512]{2,1,0:T(8,128)(2,1)} %gather_weights.1.w.wg.wu.wd, ...), custom_call_target="tpu_custom_call" | custom-call | tf_op jit(solution)/shard_map/attend_back/pallas_call | solution.py:955
  406.0 29.3 %feed_back.3 = (f32[1024,512]{1,0:T(8,128)}, f32[8,512]{1,0:T(8,128)}, bf16[4,512,512]{2,1,0:T(8,128)(2,1)}, bf16[4,512,512]{2,1,0:T(8,128)(2,1)}, bf16[4,512,512]{2,1,0:T(8,128)(2,1)}) custom-call(f32[1024,512]{1,0:T(8,128)} %get-tuple-element.227.dx, f32[1024,512]{1,0:T(8,128)} %copy-done.1, f32[1,512]{1,0:T(1,128)} %copy-done.14, ...), custom_call_target="tpu_custom_call" | custom-call | tf_op jit(solution)/shard_map/feed_back/pallas_call | solution.py:1114
  435.4 27.7 %attend_back.3 = (f32[1024,512]{1,0:T(8,128)}, f32[2,8,512]{2,1,0:T(8,128)}, bf16[4,512,512]{2,1,0:T(8,128)(2,1)}) custom-call(f32[8]{0:T(128)} %copy-done.18, f32[1024,512]{1,0:T(8,128)} %get-tuple-element.231.dx, f32[1024,512]{1,0:T(8,128)} %multiply_multiply_fusion.2.x, f32[1,512]{1,0:T(1,128)} %copy-done.16, ...), custom_call_target="tpu_custom_call" | custom-call | tf_op jit(solution)/shard_map/attend_back/pallas_call | solution.py:955
  469.0 16.1 %group_7.1 = bf16[8,128,512]{2,1,0:T(8,128)(2,1)} custom-call(bf16[8,128,512]{2,1,0:T(8,128)(2,1)} %bitcast.151), custom_call_target="tpu_custom_call" | custom-call | tf_op jit(solution)/shard_map/group_7/pallas_call | solution.py:107
  485.1 11.6 %fusion.48 = f32[3816,512]{1,0:T(8,128)S(1)} fusion(bf16[2048,3816]{0,1:T(8,128)(2,1)} %copy-done.23, bf16[2048,512]{1,0:T(8,128)(2,1)S(1)} %bitcast.146), kind=kOutput, calls=%fused_computation.161 | convolution fusion | flops 8002732032 | bytes 25542656 | tf_op jit(solution)/shard_map/tv,td->vd/dot_general | solution.py:1360
  497.4 6.7 pad_add_fusion
  504.1 117.5 %reduce_gradients.1 = (f32[32,16,512]{2,1,0:T(8,128)}, f32[4,960,512]{2,1,0:T(8,128)}, f32[2,8,512]{2,1,0:T(8,128)}) custom-call(bf16[4,8,2,2,16,512]{5,4,3,2,1,0:T(8,128)(2,1)} %bitcast.144, bf16[4,8,2,2,16,512]{5,4,3,2,1,0:T(8,128)(2,1)} %bitcast.141, bf16[4,8,2,2,16,512]{5,4,3,2,1,0:T(8,128)(2,1)} %bitcast.142, bf16[4,8,2,2,16,512]{5,4,3,2,1,0:T(8,128)(2,1)} %bitcast.143, ...), custom_call_target="tpu_custom_call" | custom-call | tf_op jit(solution)/shard_map/reduce_gradients/pallas_call | solution.py:505
  625.3 12.2 %total_9.1 = f32[8,512]{1,0:T(8,128)} custom-call(f32[8,512]{1,0:T(8,128)} %copy-done.37), custom_call_target="tpu_custom_call" | custom-call | tf_op jit(solution)/shard_map/total_9/pallas_call | solution.py:647
  642.4 22.1 %fusion.39 = (bf16[3816,512]{1,0:T(8,128)(2,1)}, f32[3816,512]{1,0:T(8,128)}, f32[3816,512]{1,0:T(8,128)}, f32[3816,512]{1,0:T(8,128)}) fusion(f32[3816,512]{1,0:T(8,128)} %param.35, f32[]{:T(128)} %bitcast.54, f32[]{:T(128)} %bitcast.53, f32[3840,512]{1,0:T(8,128)} %bitcast.134, f32[]{:T(128)} %min.3, f32[3816,512]{1,0:T(8,128)} %param.37, ...), kind=kLoop, calls=%fused_computation.154 | loop fusion | flops 33214464 | bytes 58613772 | tf_op jit(solution)/shard_map/convert_element_type | solution.py:1490
  667.3 32.4 %slots_10.1 = bf16[6,8,4,16,512]{4,3,2,1,0:T(8,128)(2,1)} custom-call(bf16[8,6,16,512]{3,2,1,0:T(8,128)(2,1)} %select_select_fusion.1.x_ref), custom_call_target="tpu_custom_call" | custom-call | tf_op jit(solution)/shard_map/slots_10/pallas_call | solution.py:710
  701.0 22.7 %turn_slots.1 = (f32[6,512,512]{2,1,0:T(8,128)}, f32[6,512,512]{2,1,0:T(8,128)}, bf16[8,6,16,512]{3,2,1,0:T(8,128)(2,1)}) custom-call(s32[7]{0:T(128)} %pad_add_fusion.1.scalars, f32[3]{0:T(128)} %pad_maximum_fusion.1.numbers, f32[6,512,512]{2,1,0:T(8,128)} %left.1, f32[6,512,512]{2,1,0:T(8,128)} %right.1, f32[6,8,4,16,512]{4,3,2,1,0:T(8,128)} %bitcast.130, ...), custom_call_target="tpu_custom_call" | custom-call | tf_op jit(solution)/shard_map/turn_slots/pallas_call | solution.py:1194
  723.7 35.5 %slots_11.1 = bf16[8,6,4,16,512]{4,3,2,1,0:T(8,128)(2,1)} custom-call(bf16[8,6,16,512]{3,2,1,0:T(8,128)(2,1)} %get-tuple-element.253.x_ref), custom_call_target="tpu_custom_call" | custom-call | tf_op jit(solution)/shard_map/slots_11/pallas_call | solution.py:710
  761.9 6.1 fusion.41
  (212 shorter events, 62.8 us)
Async XLA Ops:
  5.8 58.9 %copy-start.56 = (s32[1024]{0:T(1024)}, s32[1024]{0:T(1024)S(1)}, u32[]{:S(2)}) copy-start(s32[1024]{0:T(1024)S(1)} %get-tuple-element.389) | copy-start | bytes 12292
  70.1 78.4 %copy-start.16 = (f32[1,512]{1,0:T(1,128)}, f32[1,512]{1,0:T(1,128)S(1)}, u32[]{:S(2)}) copy-start(f32[1,512]{1,0:T(1,128)S(1)} %slice.136.gain) | copy-start | bytes 6148
  74.0 74.3 %copy-start.11 = (s32[2,1,512]{2,1,0:T(1,128)S(1)}, s32[2,1,512]{2,1,0:T(1,128)}, u32[]{:S(2)}) copy-start(s32[2,1,512]{2,1,0:T(1,128)} %seg_row.7) | copy-start | bytes 12292
  148.5 35.2 %copy-start = (s32[2,512,1]{2,1,0:T(8,128)}, s32[2,512,1]{2,1,0:T(8,128)S(1)}, u32[]{:S(2)}) copy-start(s32[2,512,1]{2,1,0:T(8,128)S(1)} %reshape_reshape.3.seg_col) | copy-start | bytes 12292
  148.6 35.1 %copy-start.18 = (f32[8]{0:T(128)}, f32[8]{0:T(128)S(1)}, u32[]{:S(2)}) copy-start(f32[8]{0:T(128)S(1)} %multiply_power_fusion.slopes) | copy-start | bytes 100
  168.4 13.0 %copy-start.1 = (f32[1024,512]{1,0:T(8,128)}, f32[1024,512]{1,0:T(8,128)S(1)}, u32[]{:S(2)}) copy-start(f32[1024,512]{1,0:T(8,128)S(1)} %get-tuple-element.214.x) | copy-start | bytes 6291460
  168.4 13.0 %copy-start.12 = (f32[2,8,512]{2,1,0:T(8,128)}, f32[2,8,512]{2,1,0:T(8,128)S(1)}, u32[]{:S(2)}) copy-start(f32[2,8,512]{2,1,0:T(8,128)S(1)} %get-tuple-element.235.lse) | copy-start | bytes 98308
  168.4 12.9 %copy-start.14 = (f32[1,512]{1,0:T(1,128)}, f32[1,512]{1,0:T(1,128)S(1)}, u32[]{:S(2)}) copy-start(f32[1,512]{1,0:T(1,128)S(1)} %slice.138.gain) | copy-start | bytes 6148
  183.7 17.7 %copy-start.17 = (f32[1,512]{1,0:T(1,128)}, f32[1,512]{1,0:T(1,128)S(1)}, u32[]{:S(2)}) copy-start(f32[1,512]{1,0:T(1,128)S(1)} %slice.140.gain) | copy-start | bytes 6148
  206.9 12.2 %copy-start.15 = (f32[1,512]{1,0:T(1,128)}, f32[1,512]{1,0:T(1,128)S(1)}, u32[]{:S(2)}) copy-start(f32[1,512]{1,0:T(1,128)S(1)} %slice.142.gain) | copy-start | bytes 6148
  295.2 14.9 %copy-start.36 = (f32[2048]{0:T(1024)}, f32[2048]{0:T(1024)S(1)}, u32[]{:S(2)}) copy-start(f32[2048]{0:T(1024)S(1)} %get-tuple-element.328) | copy-start | bytes 24580
  295.2 14.8 %copy-start.40 = (f32[2048]{0:T(1024)}, f32[2048]{0:T(1024)S(1)}, u32[]{:S(2)}) copy-start(f32[2048]{0:T(1024)S(1)} %fusion.29) | copy-start | bytes 24580
  295.2 14.8 %copy-start.19 = (bf16[3816,512]{1,0:T(8,128)(2,1)S(1)}, bf16[3816,512]{1,0:T(8,128)(2,1)}, u32[]{:S(2)}) copy-start(bf16[3816,512]{1,0:T(8,128)(2,1)} %get-tuple-element.565) | copy-start | bytes 11722756
  310.1 8.6 %copy-start.23 = (bf16[2048,3816]{0,1:T(8,128)(2,1)}, bf16[2048,3816]{0,1:T(8,128)(2,1)S(1)}, u32[]{:S(2)}) copy-start(bf16[2048,3816]{0,1:T(8,128)(2,1)S(1)} %subtract_convert_fusion) | copy-start | bytes 46891012
  435.3 27.8 %copy-start.21 = (f32[1024,512]{1,0:T(8,128)S(1)}, f32[1024,512]{1,0:T(8,128)}, u32[]{:S(2)}) copy-start(f32[1024,512]{1,0:T(8,128)} %copy-done.20) | copy-start | bytes 6291460
  435.3 27.8 %copy-start.34 = (f32[1024]{0:T(1024)S(1)}, f32[1024]{0:T(1024)}, u32[]{:S(2)}) copy-start(f32[1024]{0:T(1024)} %copy-done.33) | copy-start | bytes 12292
  435.4 27.8 %copy-start.39 = (f32[1024]{0:T(1024)S(1)}, f32[1024]{0:T(1024)}, u32[]{:S(2)}) copy-start(f32[1024]{0:T(1024)} %copy-done.38) | copy-start | bytes 12292
  435.4 27.8 %copy-start.45 = (f32[512]{0:T(512)S(1)}, f32[512]{0:T(512)}, u32[]{:S(2)}) copy-start(f32[512]{0:T(512)} %copy-done.44) | copy-start | bytes 6148
  466.7 18.3 %copy-start.25 = (bf16[8,256,512]{2,1,0:T(8,128)(2,1)S(1)}, bf16[8,256,512]{2,1,0:T(8,128)(2,1)}, u32[]{:S(2)}) copy-start(bf16[8,256,512]{2,1,0:T(8,128)(2,1)} %ring_rows.1) | copy-start | bytes 6291460
  485.1 12.4 %copy-start.28 = (bf16[8,128,512]{2,1,0:T(8,128)(2,1)S(1)}, bf16[8,128,512]{2,1,0:T(8,128)(2,1)}, u32[]{:S(2)}) copy-start(bf16[8,128,512]{2,1,0:T(8,128)(2,1)} %group_7.1) | copy-start | bytes 3145732
  497.4 6.7 copy-start.30
  497.4 6.7 copy-start.32
  504.1 119.7 %copy-start.47 = (f32[2,8,512]{2,1,0:T(8,128)S(1)}, f32[2,8,512]{2,1,0:T(8,128)}, u32[]{:S(2)}) copy-start(f32[2,8,512]{2,1,0:T(8,128)} %get-tuple-element.237) | copy-start | bytes 98308
  504.1 119.7 %copy-start.51 = (f32[8,512]{1,0:T(8,128)S(1)}, f32[8,512]{1,0:T(8,128)}, u32[]{:S(2)}) copy-start(f32[8,512]{1,0:T(8,128)} %get-tuple-element.238) | copy-start | bytes 49156
  504.1 119.7 %copy-start.46 = (f32[2,8,512]{2,1,0:T(8,128)S(1)}, f32[2,8,512]{2,1,0:T(8,128)}, u32[]{:S(2)}) copy-start(f32[2,8,512]{2,1,0:T(8,128)} %get-tuple-element.239) | copy-start | bytes 98308
  504.1 119.7 %copy-start.50 = (f32[8,512]{1,0:T(8,128)S(1)}, f32[8,512]{1,0:T(8,128)}, u32[]{:S(2)}) copy-start(f32[8,512]{1,0:T(8,128)} %get-tuple-element.240) | copy-start | bytes 49156
  504.1 119.7 %copy-start.52 = (f32[512]{0:T(512)S(1)}, f32[512]{0:T(512)}, u32[]{:S(2)}) copy-start(f32[512]{0:T(512)} %get-tuple-element.323) | copy-start | bytes 6148
  642.3 22.1 %copy-start.49 = (f32[6,64]{1,0:T(8,128)S(1)}, f32[6,64]{1,0:T(8,128)}, u32[]{:S(2)}) copy-start(f32[6,64]{1,0:T(8,128)} %param.34) | copy-start | bytes 4612
  642.3 22.1 %copy-start.53 = (f32[6,64]{1,0:T(8,128)S(1)}, f32[6,64]{1,0:T(8,128)}, u32[]{:S(2)}) copy-start(f32[6,64]{1,0:T(8,128)} %param.39) | copy-start | bytes 4612
  642.3 22.1 %copy-start.54 = (f32[6,64]{1,0:T(8,128)S(1)}, f32[6,64]{1,0:T(8,128)}, u32[]{:S(2)}) copy-start(f32[6,64]{1,0:T(8,128)} %param.38) | copy-start | bytes 4612
  642.4 22.8 %copy-start.27 = (f32[32,16,512]{2,1,0:T(8,128)S(1)}, f32[32,16,512]{2,1,0:T(8,128)}, u32[]{:S(2)}) copy-start(f32[32,16,512]{2,1,0:T(8,128)} %get-tuple-element.252) | copy-start | bytes 3145732
  642.4 22.9 %copy-start.58 = (s32[32]{0:T(128)S(1)}, s32[32]{0:T(128)}, u32[]{:S(2)}) copy-start(s32[32]{0:T(128)} %param.44) | copy-start | bytes 388
  (26 other events, 63.3 us)

commit v2 on v1

--- a/solution.py
+++ b/solution.py
@@ -115,69 +115,29 @@
     )(x)
 
 
-def ask_kernel(n_rep, n, w_ref, facts_ref, gains_ref, asked, facts, gains, most, held, got, send, recv, send2, recv2):
+def opening_kernel(
+    n_rep, n, half, shared, x_ref, t_ref, w_ref, facts_ref, gains_ref, o_ref, rows_ref, asked, facts, gains, most,
+    table, index, stage, ready, held, got,
+    t_s, ring_s, ring_r, core_s, core_r, y_s, y_r, over_s, over_r, ask_s, ask_r, top_s, top_r, rows_s, rows_r,
+):
     here = Place(n_rep, n)
+    me = here.f
     ypeer = (lax.rem(here.r + 2, 4), here.f)
-    me = here.f
     others = [lax.rem(me + k, n) for k in range(1, n)]
+    rows = x_ref.shape[1]
+    alone = (half - shared) // 2
     enter([(here.r, o) for o in others] + [here.core, ypeer])
-    copies = []
+    load = pltpu.make_async_copy(t_ref, table, t_s.at[0])
+    load.start()
+    asks = []
     for k, o in enumerate(others):
         peer = (here.r, o)
-        copies.append(remote(facts_ref, facts.at[me], send.at[0, k], recv.at[0, k], peer))
-        copies.append(remote(w_ref.at[o], asked.at[me], send.at[1, k], recv.at[1, k], peer))
-        copies.append(remote(gains_ref, gains.at[me], send.at[2, k], recv.at[2, k], peer))
-    for cp in copies:
+        asks.append(remote(w_ref.at[o], asked.at[me], ask_s.at[0, k], ask_r.at[0, k], peer))
+        asks.append(remote(facts_ref, facts.at[me], ask_s.at[1, k], ask_r.at[1, k], peer))
+        asks.append(remote(gains_ref, gains.at[me], ask_s.at[2, k], ask_r.at[2, k], peer))
+    for cp in asks:
         cp.start()
-    asked[me] = w_ref[me]
-    facts[me] = facts_ref[...]
-    gains[me] = gains_ref[...]
-    for cp in copies:
-        cp.wait_recv()
-    top = facts[0]
-    for k in range(1, n):
-        top = jnp.maximum(top, facts[k])
-    held[0] = top
-    first = remote(held.at[0], got.at[0], send2.at[0], recv2.at[0], here.core)
-    first.start()
-    first.wait_recv()
-    held[1] = jnp.maximum(top, got[0])
-    second = remote(held.at[1], got.at[1], send2.at[1], recv2.at[1], ypeer)
-    second.start()
-    second.wait_recv()
-    most[...] = jnp.maximum(held[1], got[1])
-    first.wait_send()
-    second.wait_send()
-    for cp in copies:
-        cp.wait_send()
-
-
-def ask_group(mesh_sizes, cid, wanted, facts, gains):
-    n_rep, n = mesh_sizes
-    dma = pltpu.SemaphoreType.DMA
-    return pl.pallas_call(
-        partial(ask_kernel, n_rep, n),
-        out_shape=[
-            jax.ShapeDtypeStruct(wanted.shape, wanted.dtype),
-            jax.ShapeDtypeStruct((n,) + facts.shape, facts.dtype),
-            jax.ShapeDtypeStruct((n,) + gains.shape, gains.dtype),
-            jax.ShapeDtypeStruct(facts.shape, facts.dtype),
-        ],
-        in_specs=[VMEM] * 3,
-        out_specs=[VMEM] * 4,
-        scratch_shapes=[pltpu.VMEM((2,) + facts.shape, facts.dtype)] * 2
-        + [dma((3, n - 1)), dma((3, n - 1)), dma((2,)), dma((2,))],
-        compiler_params=params(cid),
-        name="ask_group",
-    )(wanted, facts, gains)
-
-
-def weights_kernel(n_rep, n, half, shared, x_ref, o_ref, ring_s, ring_r, core_s, core_r, y_s, y_r, over_s, over_r):
-    here = Place(n_rep, n)
-    ypeer = (lax.rem(here.r + 2, 4), here.f)
-    rows = x_ref.shape[1]
-    alone = (half - shared) // 2
-    enter([here.next, here.prev, here.core, ypeer])
+
     mine = pl.ds(here.c * half + here.y * alone, alone + shared)
     given = pl.ds(here.c * half + here.y * (alone + shared), alone)
     taken = pl.ds(here.c * half + (1 - here.y) * (alone + shared), alone)
@@ -189,9 +149,7 @@
             return pl.ds(pl.multiple_of(origin * rows + way * (rows // 2), rows // 2), rows // 2)
         return pl.ds(pl.multiple_of(origin * rows, rows), rows)
 
-    own = remote(
-        x_ref, o_ref.at[:, rows_of(here.f, 0, -1)], core_s.at[0, 0], core_r.at[0, 0], here.core
-    )
+    own = remote(x_ref, o_ref.at[:, rows_of(here.f, 0, -1)], core_s.at[0, 0], core_r.at[0, 0], here.core)
     own.start()
     copies.append(own)
     waiting = [None, None]
@@ -200,60 +158,112 @@
     def pass_on(way, s):
         waiting[way].wait_recv()
         where = rows_of(here.at(-s - 1 if way == 0 else s + 1), way, s)
-        held = o_ref.at[given, where]
-        cp = remote(held, held, y_s.at[way, s], y_r.at[way, s], ypeer)
+        kept = o_ref.at[given, where]
+        cp = remote(kept, kept, y_s.at[way, s], y_r.at[way, s], ypeer)
         cp.start()
         across.append((cp, o_ref.at[taken, where], way, s))
-        held = o_ref.at[mine, where]
-        cp = remote(held, held, core_s.at[way, s + 1], core_r.at[way, s + 1], here.core)
+        kept = o_ref.at[mine, where]
+        cp = remote(kept, kept, core_s.at[way, s + 1], core_r.at[way, s + 1], here.core)
         cp.start()
         copies.append(cp)
 
-    for s in range(hops):
+    def hop(way, s):
+        where = rows_of(here.at(-s if way == 0 else s), way, s)
+        src = x_ref.at[mine] if s == 0 else o_ref.at[mine, where]
+        cp = remote(
+            src, o_ref.at[mine, where], ring_s.at[way, s], ring_r.at[way, s], here.next if way == 0 else here.prev
+        )
+        cp.start()
+        waiting[way] = cp
+        sends.append(cp)
+
+    for way in range(2):
+        hop(way, 0)
+
+    asked[me] = w_ref[me]
+    facts[me] = facts_ref[...]
+    gains[me] = gains_ref[...]
+    for cp in asks:
+        cp.wait_recv()
+    listed = pltpu.make_async_copy(asked, index, t_s.at[1])
+    listed.start()
+    top = facts[0]
+    for k in range(1, n):
+        top = jnp.maximum(top, facts[k])
+    held[0] = top
+    first = remote(held.at[0], got.at[0], top_s.at[0], top_r.at[0], here.core)
+    first.start()
+    listed.wait()
+    load.wait()
+    places = rows_ref.shape[1]
+
+    def collect(o):
+        def one(i, carry):
+            stage[pl.ds(i, 1)] = table[pl.ds(index[o, 0, i], 1)]
+            return carry
+
+        lax.fori_loop(0, places, one, 0, unroll=8)
+        return stage[...].astype(bf16)
+
+    for k, o in enumerate(others):
+        ready[o] = collect(o)
+        cp = remote(ready.at[o], rows_ref.at[me], rows_s.at[k], rows_r.at[k], (here.r, o))
+        cp.start()
+        asks.append(cp)
+    rows_ref[me] = collect(me)
+    first.wait_recv()
+    held[1] = jnp.maximum(top, got[0])
+    second = remote(held.at[1], got.at[1], top_s.at[1], top_r.at[1], ypeer)
+    second.start()
+
+    for s in range(1, hops):
         for way in range(2):
-            if s > 0:
-                pass_on(way, s - 1)
-            origin = here.at(-s if way == 0 else s)
-            where = rows_of(origin, way, s)
-            if s == 0:
-                src = x_ref.at[mine]
-            else:
-                src = o_ref.at[mine, where]
-            cp = remote(
-                src,
-                o_ref.at[mine, where],
-                ring_s.at[way, s],
-                ring_r.at[way, s],
-                here.next if way == 0 else here.prev,
-            )
-            cp.start()
-            waiting[way] = cp
-            sends.append(cp)
+            pass_on(way, s - 1)
+            hop(way, s)
+    second.wait_recv()
+    most[...] = jnp.maximum(held[1], got[1])
     for way in range(2):
         pass_on(way, hops - 1)
-    for cp, held, way, s in across:
+    for cp, kept, way, s in across:
         cp.wait_recv()
-        over = remote(held, held, over_s.at[way, s], over_r.at[way, s], here.core)
+        over = remote(kept, kept, over_s.at[way, s], over_r.at[way, s], here.core)
         over.start()
         copies.append(over)
         sends.append(cp)
-    for cp in sends:
+    for cp in asks[3 * (n - 1) :]:
+        cp.wait_recv()
+    for cp in asks + [first, second] + sends:
         cp.wait_send()
     for cp in copies:
         cp.wait()
 
 
-def gather_weights(mesh_sizes, cid, shard):
+def open_step(mesh_sizes, cid, shard, table, wanted, facts, gains):
     n_rep, n = mesh_sizes
     count, rows, width = shard.shape
     half = count // 2
+    places = wanted.shape[2]
     dma = pltpu.SemaphoreType.DMA
     return pl.pallas_call(
-        partial(weights_kernel, n_rep, n, half, half - 2 * (half // 3)),
-        out_shape=jax.ShapeDtypeStruct((count, rows * n, width), shard.dtype),
-        in_specs=[ANY],
-        out_specs=ANY,
+        partial(opening_kernel, n_rep, n, half, half - 2 * (half // 3)),
+        out_shape=[
+            jax.ShapeDtypeStruct((count, rows * n, width), shard.dtype),
+            jax.ShapeDtypeStruct((n, places, width), bf16),
+            jax.ShapeDtypeStruct(wanted.shape, wanted.dtype),
+            jax.ShapeDtypeStruct((n,) + facts.shape, facts.dtype),
+            jax.ShapeDtypeStruct((n,) + gains.shape, gains.dtype),
+            jax.ShapeDtypeStruct(facts.shape, facts.dtype),
+        ],
+        in_specs=[ANY, ANY] + [VMEM] * 3,
+        out_specs=[ANY] + [VMEM] * 5,
         scratch_shapes=[
+            pltpu.VMEM(table.shape, table.dtype),
+            pltpu.SMEM(wanted.shape, wanted.dtype),
+            pltpu.VMEM((places, width), table.dtype),
+            pltpu.VMEM((n, places, width), bf16),
+            pltpu.VMEM((2,) + facts.shape, facts.dtype),
+            pltpu.VMEM((2,) + facts.shape, facts.dtype),
+            dma((2,)),
             dma((2, n // 2)),
             dma((2, n // 2)),
             dma((2, n // 2 + 1)),
@@ -262,10 +272,16 @@
             dma((2, n // 2)),
             dma((2, n // 2)),
             dma((2, n // 2)),
-        ],
-        compiler_params=params(cid),
-        name="gather_weights",
-    )(shard)
+            dma((3, n - 1)),
+            dma((3, n - 1)),
+            dma((2,)),
+            dma((2,)),
+            dma((n - 1,)),
+            dma((n - 1,)),
+        ],
+        compiler_params=params(cid, 24 << 20),
+        name="open_step",
+    )(shard, table, wanted, facts, gains)
 
 
 def ring_rows_kernel(n_rep, n, x_ref, o_ref, send, recv):
@@ -309,20 +325,28 @@
     )(x)
 
 
+def squares_row(square):
+    row = jnp.sum(square, axis=0, keepdims=True)
+    return jnp.where(lax.broadcasted_iota(jnp.int32, square.shape, 0) == 6, row, 0.0)
+
+
 def reduce_kernel(
     n_rep, n, half, table_rows, each, *refs
 ):
     g_refs, refs = refs[: 2 * each], refs[2 * each :]
     (
-    t_ref, o_ref, to_ref, sq_ref,
+    t_ref, small_ref, block_of, taken, o_ref, to_ref, sum_ref, mine, outgoing, held, hgot, four, fours, squares,
     own, part, got, fin, ysend, ygot, town, tpart, tsend, tgot,
     load_s, core_s, core_r, ring_s, ring_r, y_s, y_r, tload, tcs, tcr, tys, tyr, tos, tor,
+    keep, a_s, a_r, f_s, f_r, sum_s, sum_r,
     ) = refs
     here = Place(n_rep, n)
     c, y = here.c, here.y
     ypeer = (lax.rem(here.r + 2, 4), here.f)
     other_c, other_y = 1 - c, 1 - y
-    enter([here.next, here.prev, here.core, ypeer])
+    me = here.f
+    others = [lax.rem(me + k, n) for k in range(1, n)]
+    enter([(here.r, o) for o in others] + [here.core, ypeer])
     far = n // 2
 
     tl = pltpu.make_async_copy(t_ref.at[pl.ds(c * 2, 2)], town, tload)
@@ -429,18 +453,15 @@
                     acc = acc + square[k * 8 : k * 8 + 8]
                 return acc
 
-            sq_ref[0] = lax.fori_loop(0, table_rows // step_rows, add, jnp.zeros((8, tgot.shape[1]), f32))
-            mine = c * 2 + y
+            squares[...] = lax.fori_loop(0, table_rows // step_rows, add, jnp.zeros((8, tgot.shape[1]), f32))
+            quarter = c * 2 + y
             near = c * 2 + other_y
-            tkeep = pltpu.make_async_copy(town.at[y], to_ref.at[mine], tload)
+            tkeep = pltpu.make_async_copy(town.at[y], to_ref.at[quarter], tload)
             tkeep.start()
-            t0 = remote(town.at[y], to_ref.at[mine], tos.at[0], tor.at[0], ypeer)
-            t1 = remote(town.at[y], to_ref.at[mine], tos.at[1], tor.at[1], here.core)
+            t0 = remote(town.at[y], to_ref.at[quarter], tos.at[0], tor.at[0], ypeer)
+            t1 = remote(town.at[y], to_ref.at[quarter], tos.at[1], tor.at[1], here.core)
             t0.start()
             t1.start()
-    t0.wait_recv()
-    t2 = remote(to_ref.at[near], to_ref.at[near], tos.at[2], tor.at[2], here.core)
-    t2.start()
     ys = []
     spot = spots[0, 0]
     for h in range(2):
@@ -470,12 +491,79 @@
 
         def last(b, acc, h=h):
             total = fin[h, b] + ygot[h, b].astype(f32)
-            o_ref[h * half + b] = total
+            mine[h * half + b] = total.astype(bf16)
             square = total * total
             return acc + square[:8] + square[8:]
 
         acc = lax.fori_loop(0, half, last, acc)
-    sq_ref[1] = acc
+
+    held[0] = small_ref[...] + squares_row(acc + squares[...])
+    first = remote(held.at[0], hgot.at[0], sum_s.at[0], sum_r.at[0], here.core)
+    first.start()
+
+    cap = o_ref.shape[0]
+
+    @pl.loop(0, n * cap)
+    def _(k):
+        value = mine[block_of[k]]
+        outgoing[k] = jnp.where(taken[k] > 0, value, jnp.zeros_like(value))
+
+    def spot_of(source, r):
+        return o_ref.at[:, source, r]
+
+    moves = []
+    for k, o in enumerate(others):
+        cp = remote(outgoing.at[pl.ds(o * cap, cap)], spot_of(me, here.r), a_s.at[k], a_r.at[k], (here.r, o))
+        cp.start()
+        moves.append(cp)
+    kept = pltpu.make_async_copy(outgoing.at[pl.ds(me * cap, cap)], spot_of(me, here.r), keep)
+    kept.start()
+    first.wait_recv()
+    held[1] = held[0] + hgot[0]
+    second = remote(held.at[1], hgot.at[1], sum_s.at[1], sum_r.at[1], ypeer)
+    second.start()
+    t0.wait_recv()
+    t2 = remote(to_ref.at[near], to_ref.at[near], tos.at[2], tor.at[2], here.core)
+    t2.start()
+    second.wait_recv()
+    four[...] = held[1] + hgot[1]
+    totals = []
+    for k, o in enumerate(others):
+        cp = remote(four, fours.at[me], sum_s.at[2 + k], sum_r.at[2 + k], (here.r, o))
+        cp.start()
+        totals.append(cp)
+    fours[me] = four[...]
+    beside, distant = [], []
+    for k in range(n):
+        source = me if k == 0 else lax.rem(me - k + n, n)
+        if k == 0:
+            kept.wait()
+        else:
+            moves[k - 1].wait_recv()
+        piece = spot_of(source, here.r)
+        over = remote(piece, piece, f_s.at[0, k], f_r.at[0, k], ypeer)
+        over.start()
+        cp = remote(piece, piece, f_s.at[1, k], f_r.at[1, k], here.core)
+        cp.start()
+        distant.append((over, source))
+        beside.append(cp)
+    for cp in totals:
+        cp.wait_recv()
+    total = fours[0]
+    for k in range(1, n):
+        total = total + fours[k]
+    sum_ref[...] = total
+    yr = lax.rem(here.r + 2, 4)
+    for k, (over, source) in enumerate(distant):
+        over.wait_recv()
+        piece = spot_of(source, yr)
+        cp = remote(piece, piece, f_s.at[2, k], f_r.at[2, k], here.core)
+        cp.start()
+        beside.append(cp)
+    for cp in moves + totals + [first, second] + [over for over, _ in distant]:
+        cp.wait_send()
+    for cp in beside:
+        cp.wait()
     for cp in ys:
         cp.wait_send()
     for cp in ring.values():
@@ -491,7 +579,7 @@
     t2.wait()
 
 
-def reduce_gradients(mesh_sizes, cid, grads, table):
+def settle_gradients(mesh_sizes, cid, grads, table, small, block_of, taken, cap):
     n_rep, n = mesh_sizes
     _, depth, width = grads[0].shape
     count = sum(g.shape[0] for g in grads)
@@ -502,16 +590,25 @@
     views = [g.reshape(g.shape[0], n, 2, 2, 16, width) for g in grads]
     dma = pltpu.SemaphoreType.DMA
     piece = (half, 2, 16, width)
+    smem = pl.BlockSpec(memory_space=pltpu.SMEM)
+    like = small.shape
     return pl.pallas_call(
         partial(reduce_kernel, n_rep, n, half, table_rows, each),
         out_shape=[
-            jax.ShapeDtypeStruct((count, 16, width), f32),
+            jax.ShapeDtypeStruct((cap, n, 4, 16, width), bf16),
             jax.ShapeDtypeStruct(table.shape, f32),
-            jax.ShapeDtypeStruct((2, 8, width), f32),
-        ],
-        in_specs=[ANY] * (2 * each + 1),
-        out_specs=[VMEM, ANY, VMEM],
+            jax.ShapeDtypeStruct(like, f32),
+        ],
+        in_specs=[ANY] * (2 * each + 1) + [VMEM, smem, smem],
+        out_specs=[ANY, ANY, VMEM],
         scratch_shapes=[
+            pltpu.VMEM((count, 16, width), bf16),
+            pltpu.VMEM((n * cap, 16, width), bf16),
+            pltpu.VMEM((2,) + like, f32),
+            pltpu.VMEM((2,) + like, f32),
+            pltpu.VMEM(like, f32),
+            pltpu.VMEM((n,) + like, f32),
+            pltpu.VMEM(like, f32),
             pltpu.VMEM((n, 2) + piece, bf16),
             pltpu.VMEM((n, 2) + piece, bf16),
             pltpu.VMEM((2, 2, far) + piece, bf16),
@@ -536,10 +633,17 @@
             dma,
             dma((3,)),
             dma((3,)),
-        ],
-        compiler_params=params(cid, 60 << 20),
-        name="reduce_gradients",
-    )(*views, table)
+            dma,
+            dma((n - 1,)),
+            dma((n - 1,)),
+            dma((3, n)),
+            dma((3, n)),
+            dma((n + 1,)),
+            dma((n + 1,)),
+        ],
+        compiler_params=params(cid, 56 << 20),
+        name="settle_gradients",
+    )(*views, table, small, block_of, taken)
 
 
 def rows_kernel(n_rep, n, x_ref, o_ref, held, got, send, recv):
@@ -606,52 +710,6 @@
         ],
         compiler_params=params(cid, 24 << 20),
         name="reduce_rows",
-    )(x)
-
-
-def total_kernel(n_rep, n, x_ref, o_ref, core_got, both, y_got, four, got, send, recv):
-    here = Place(n_rep, n)
-    ypeer = (lax.rem(here.r + 2, 4), here.f)
-    others = [lax.rem(here.f + k, n) for k in range(1, n)]
-    enter([(here.r, o) for o in others] + [here.core, ypeer])
-    first = remote(x_ref, core_got, send.at[0], recv.at[0], here.core)
-    first.start()
-    first.wait_recv()
-    both[...] = x_ref[...] + core_got[...]
-    second = remote(both, y_got, send.at[1], recv.at[1], ypeer)
-    second.start()
-    second.wait_recv()
-    four[...] = both[...] + y_got[...]
-    copies = []
-    for k, o in enumerate(others):
-        cp = remote(four, got.at[here.f], send.at[2 + k], recv.at[2 + k], (here.r, o))
-        cp.start()
-        copies.append(cp)
-    got[here.f] = four[...]
-    for cp in copies:
-        cp.wait_recv()
-    total = got[0]
-    for k in range(1, n):
-        total = total + got[k]
-    o_ref[...] = total
-    first.wait_send()
-    second.wait_send()
-    for cp in copies:
-        cp.wait_send()
-
-
-def total_everyone(mesh_sizes, cid, x):
-    n_rep, n = mesh_sizes
-    dma = pltpu.SemaphoreType.DMA
-    like = pltpu.VMEM(x.shape, x.dtype)
-    return pl.pallas_call(
-        partial(total_kernel, n_rep, n),
-        out_shape=jax.ShapeDtypeStruct(x.shape, x.dtype),
-        in_specs=[VMEM],
-        out_specs=VMEM,
-        scratch_shapes=[like] * 4 + [pltpu.VMEM((n,) + x.shape, x.dtype), dma((n + 1,)), dma((n + 1,))],
-        compiler_params=params(cid),
-        name=f"total_{cid}",
     )(x)
 
 
@@ -1209,11 +1267,20 @@
         self.sizes = (n_rep, n_fsdp)
         self.kernels = n_rep == 4 and n_fsdp == 8 and shard_rows == 64
 
-    def ask(self, cid, wanted, facts, gains):
+    def open(self, cid, shard, table, wanted, facts, gains):
         if self.kernels:
-            return ask_group(self.sizes, cid, wanted, facts, gains)
+            return open_step(self.sizes, cid, shard, table, wanted, facts, gains)
         asked = lax.all_to_all(wanted, "fsdp", split_axis=0, concat_axis=0, tiled=True)
-        return asked, lax.all_gather(facts, "fsdp"), lax.all_gather(gains, "fsdp"), lax.pmax(facts, ("rep", "fsdp"))
+        rows = jnp.take(table.astype(bf16), asked.reshape(-1), axis=0)
+        rows = rows.reshape(wanted.shape[0], wanted.shape[2], table.shape[1])
+        return (
+            lax.all_gather(shard, "fsdp", axis=1, tiled=True),
+            self.spread(cid, rows),
+            asked,
+            lax.all_gather(facts, "fsdp"),
+            lax.all_gather(gains, "fsdp"),
+            lax.pmax(facts, ("rep", "fsdp")),
+        )
 
     def spread(self, cid, x):
         if self.kernels:
@@ -1234,11 +1301,6 @@
         if self.kernels:
             return reduce_rows(self.sizes, cid, x)
         return lax.psum_scatter(x.astype(f32), "fsdp", scatter_dimension=0)
-
-    def weights(self, cid, shard):
-        if self.kernels:
-            return gather_weights(self.sizes, cid, shard)
-        return lax.all_gather(shard, "fsdp", axis=1, tiled=True)
 
 
 def body(
@@ -1302,18 +1364,19 @@
         wanted = jnp.where((slot[None, :] == slot_index[:, None]) & is_first[None, :], local[None, :], 0)
         return jnp.sum(wanted, axis=1).reshape(groups, 1, CAPACITY)
 
-    def rows_for(cid, slot, asked):
-        rows = jnp.take(table_low, asked.reshape(slots), axis=0)
-        rows = move.spread(cid, rows.reshape(groups, CAPACITY, model_width)).reshape(slots, model_width)
-        return jnp.dot((slot[:, None] == slot_index[None, :]).astype(bf16), rows, preferred_element_type=f32)
+    def placed(slot, rows):
+        chosen = (slot[:, None] == slot_index[None, :]).astype(bf16)
+        return jnp.dot(chosen, rows.reshape(slots, model_width), preferred_element_type=f32)
 
     slot = slot_of(0)
-    asked, group_facts, gain_rows, most_facts = move.ask(0, wanted_in(slot), facts, gain_pad)
+    full_blocks, rows, asked, group_facts, gain_rows, most_facts = move.open(
+        0, blocks.astype(bf16), embed, wanted_in(slot), facts, gain_pad
+    )
     rounds = (most_facts[7, 0] + CAPACITY - 1) // CAPACITY
     all_labels = group_facts[:, : picks // 128].reshape(groups * picks)
     gain_rows = gain_rows[:, :gain_count, : gains.shape[1]].transpose(1, 0, 2).reshape(gain_count, model_width)
     gain_rows = lax.reduce_precision(gain_rows, exponent_bits=8, mantissa_bits=7)
-    embedded = rows_for(2, slot, asked)
+    embedded = placed(slot, rows)
     asked_all = jnp.zeros((most_rounds, slots), jnp.int32).at[0].set(asked.reshape(slots))
 
     def look(state):
@@ -1321,11 +1384,10 @@
         slot = slot_of(k)
         asked = move.spread(1, wanted_in(slot))
         asked_all = lax.dynamic_update_index_in_dim(asked_all, asked.reshape(slots), k, 0)
-        return k + 1, rows_so_far + rows_for(12, slot, asked), asked_all
+        rows = jnp.take(table_low, asked.reshape(slots), axis=0).reshape(groups, CAPACITY, model_width)
+        return k + 1, rows_so_far + placed(slot, move.spread(2, rows)), asked_all
 
     _, embedded, asked_all = lax.while_loop(lambda s: s[0] < rounds, look, (jnp.int32(1), embedded, asked_all))
-
-    full_blocks = move.weights(3, blocks.astype(bf16))
 
     segments = segment_ids.reshape(micro_count, pack_length)
     stream, first_pull = jax.vjp(layer_norm, embedded, gain_rows[0])
@@ -1416,14 +1478,18 @@
     small = jnp.zeros((8, model_width), f32).at[:gain_count].set(grad_gains)
     small = small.at[7, 0].set(loss_local)
     if move.kernels:
-        mine, grad_table, squares = reduce_gradients(
-            move.sizes, 8, grad_blocks, grad_table.reshape(4, padded_rows // 4, model_width)
+        owned, grad_table, small = settle_gradients(
+            move.sizes,
+            8,
+            grad_blocks,
+            grad_table.reshape(4, padded_rows // 4, model_width),
+            small,
+            block_of,
+            taken.astype(jnp.int32),
+            slot_cap,
         )
         grad_table = grad_table.reshape(padded_rows, model_width)[:vocab_rows]
-        small = total_everyone(move.sizes, 9, small.at[6].set(jnp.sum(squares, axis=(0, 1))))
         squares = jnp.sum(small[6])
-        outgoing = jnp.where(taken[:, None, None], jnp.take(mine.astype(bf16), block_of, axis=0), 0)
-        owned = exchange_slots(move.sizes, 10, outgoing.reshape(groups, slot_cap, 16, model_width), True)
         owned = owned.reshape(slot_cap, model_width, model_width)
     else:
         grad_blocks = jnp.concatenate([g.astype(f32) for g in grad_blocks], axis=0)

time: 781 us -> 745 us (0.954)
  Pallas kernels: 579 us -> 552 us
    pallas_call x4 -> x2, Pallas kernels: 216 us -> 251 us  [the longest x1 151 us: settle_gradients(): pl.pallas_call(partial(reduce_kernel, n_rep, n, half, table_rows, each),...]
    pallas_call x2 -> x1, Pallas kernels: 68 us -> 34.9 us  [exchange_slots(): pl.pallas_call(partial(slots_kernel, n_rep, n, to_slots), out_shape=jax.S...]
    pallas_call x3 -> x2, Pallas kernels: 50.5 us -> 24.5 us  [group_exchange(): pl.pallas_call(partial(group_kernel, n_rep, n, spread), out_shape=jax.Sha...]
    unnamed x116 -> x96, local copies, waits for them, and re-layouts: 11.6 us -> 20.3 us
where the time goes in v2:
time: 745 us; the launch traced here: 737 us
  Pallas kernels  552 us (74%)
  other arithmetic  95 us (13%)
  matrix products  47.1 us (6%)
  local copies, waits for them, and re-layouts  33.8 us (5%)
  between operations  8.21 us (1%)
    pallas_call x1, Pallas kernels, settle_gradients(): pl.pallas_call(partial(reduce_kernel, n_rep, n, half, table_rows, each),...  151 us
    pallas_call x1, Pallas kernels, open_step(): pl.pallas_call(partial(opening_kernel, n_rep, n, half, half - 2 * (half /...  99.3 us
    pallas_call x2, Pallas kernels, feed_back(): pl.pallas_call(feed_back_kernel, grid=(pieces,), in_specs=[fixed((tokens,...  58.3 us
    pallas_call x2, Pallas kernels, attend_back(): pl.pallas_call(attend_back_kernel, grid=(packs, HEADS // 2), in_specs=[pl...  55.4 us
    pallas_call x2, Pallas kernels, attend(): pl.pallas_call(attend_kernel, grid=(packs, HEADS // 2), in_specs=[pl.Bloc...  35.5 us
    pallas_call x1, Pallas kernels, exchange_slots(): pl.pallas_call(partial(slots_kernel, n_rep, n, to_slots), out_shape=jax.S...  34.9 us
    pallas_call x1, Pallas kernels, ring_rows(): pl.pallas_call(partial(ring_rows_kernel, n_rep, n), out_shape=jax.ShapeDt...  26.3 us
    pallas_call x2, Pallas kernels, feed(): pl.pallas_call(feed_kernel, grid=(pieces,), in_specs=[fixed((tokens, widt...  25.1 us

profile of v2, /device:TPU:25, one launch (start us, length us, event | category | flops | bytes accessed | tf_op | source)
XLA Modules:
  0.0 736.6 jit_solution(18321078009669992517)
XLA Ops:
  8.0 2.5 convert_element_type.60.x_ref
  10.6 3.2 copy-done.1
  13.8 99.3 %open_step.1 = (bf16[32,512,512]{2,1,0:T(8,128)(2,1)S(1)}, bf16[8,128,512]{2,1,0:T(8,128)(2,1)S(1)}, s32[8,1,128]{2,1,0:T(1,128)S(1)}, s32[8,8,128]{2,1,0:T(8,12...) custom-call(bf16[32,64,512]{2,1,0:T(8,128)(2,1)S(1)} %convert_element_type.60.x_ref, f32[3816,512]{1,0:T(8,128)S(1)} %copy-done.1, ...), custom_call_target="tpu_custom_call" | custom-call | tf_op jit(solution)/shard_map/open_step/pallas_call | solution.py:247
  113.1 5.8 copy-done
  121.4 5.6 convert_element_type.61
  130.2 17.8 %attend.2 = (f32[1024,512]{1,0:T(8,128)S(1)}, bf16[1024,512]{1,0:T(8,128)(2,1)S(1)}, bf16[1024,1536]{1,0:T(8,128)(2,1)}, bf16[1024,512]{1,0:T(8,128)(2,1)S(1)}, f32[2,8,512]{2,1,0:T(8,128)S(1)}) custom-call(f32[8]{0:T(128)S(1)} %multiply_power_fusion.slopes, f32[1024,512]{1,0:T(8,128)} %multiply_multiply_fusion.2.x, f32[1,512]{1,0:T(1,128)S(1)} %slice.121.gain, ...), custom_call_target="tpu_custom_call" | custom-call | tf_op jit(solution)/shard_map/attend/pallas_call | solution.py:895
  150.1 12.9 %feed.2 = (f32[1024,512]{1,0:T(8,128)S(1)}, bf16[1024,512]{1,0:T(8,128)(2,1)S(1)}, bf16[4,1024,512]{2,1,0:T(8,128)(2,1)}, bf16[4,1024,512]{2,1,0:T(8,128)(2,1)}) custom-call(f32[1024,512]{1,0:T(8,128)S(1)} %get-tuple-element.206.x, f32[1,512]{1,0:T(1,128)S(1)} %slice.123.gain, bf16[32,512,512]{2,1,0:T(8,128)(2,1)} %copy-done, bf16[32,512,512]{2,1,0:T(8,128)(2,1)} %copy-done, ...), custom_call_target="tpu_custom_call" | custom-call | tf_op jit(solution)/shard_map/feed/pallas_call | solution.py:1099
  165.3 17.7 %attend.3 = (f32[1024,512]{1,0:T(8,128)S(1)}, bf16[1024,512]{1,0:T(8,128)(2,1)S(1)}, bf16[1024,1536]{1,0:T(8,128)(2,1)}, bf16[1024,512]{1,0:T(8,128)(2,1)S(1)}, f32[2,8,512]{2,1,0:T(8,128)S(1)}) custom-call(f32[8]{0:T(128)S(1)} %multiply_power_fusion.slopes, f32[1024,512]{1,0:T(8,128)} %copy-done.6, f32[1,512]{1,0:T(1,128)S(1)} %slice.125.gain, ...), custom_call_target="tpu_custom_call" | custom-call | tf_op jit(solution)/shard_map/attend/pallas_call | solution.py:895
  188.6 12.2 %feed.3 = (f32[1024,512]{1,0:T(8,128)S(1)}, bf16[1024,512]{1,0:T(8,128)(2,1)S(1)}, bf16[4,1024,512]{2,1,0:T(8,128)(2,1)}, bf16[4,1024,512]{2,1,0:T(8,128)(2,1)}) custom-call(f32[1024,512]{1,0:T(8,128)S(1)} %copy-done.5, f32[1,512]{1,0:T(1,128)S(1)} %slice.127.gain, bf16[32,512,512]{2,1,0:T(8,128)(2,1)} %copy-done, bf16[32,512,512]{2,1,0:T(8,128)(2,1)} %copy-done, ...), custom_call_target="tpu_custom_call" | custom-call | tf_op jit(solution)/shard_map/feed/pallas_call | solution.py:1099
  205.0 26.3 %ring_rows.1 = bf16[8,256,512]{2,1,0:T(8,128)(2,1)} custom-call(bf16[256,512]{1,0:T(8,128)(2,1)} %select_convert_fusion.x_ref), custom_call_target="tpu_custom_call" | custom-call | tf_op jit(solution)/shard_map/ring_rows/pallas_call | solution.py:317
  231.3 17.0 %fusion.46 = (f32[2048]{0:T(1024)S(1)}, f32[2048,3816]{0,1:T(8,128)}) fusion(bf16[2048,512]{1,0:T(8,128)(2,1)} %bitcast.127, bf16[3816,512]{1,0:T(8,128)(2,1)} %get-tuple-element.557), kind=kOutput, calls=%fused_computation.147 | convolution fusion | flops 8010545152 | bytes 37273600 | tf_op jit(solution)/shard_map/td,vd->tv/dot_general | solution.py:1406
  248.3 14.3 %exponential_reduce_fusion = (f32[2048]{0:T(1024)S(1)}, f32[2048]{0:T(1024)S(1)}) fusion(f32[2048,3816]{0,1:T(8,128)} %get-tuple-element.384, f32[2048]{0:T(1024)S(1)} %get-tuple-element.383, s32[2048]{0:T(1024)S(1)} %bitcast.144), kind=kLoop, calls=%fused_computation.33 | loop fusion | flops 39071744 | bytes 31293440 | tf_op jit(solution)/shard_map/reduce_sum | solution.py:1408
  263.3 8.5 %group_5.1 = f32[8,3,2048]{2,1,0:T(4,128)} custom-call(f32[3,2048]{1,0:T(4,128)} %pad_maximum_fusion.x_ref), custom_call_target="tpu_custom_call" | custom-call | tf_op jit(solution)/shard_map/group_5/pallas_call | solution.py:107
  273.9 14.8 %subtract_convert_fusion = bf16[2048,3816]{0,1:T(8,128)(2,1)S(1)} fusion(f32[2048,3816]{0,1:T(8,128)} %get-tuple-element.384, f32[2048]{0:T(1024)S(1)} %fusion.29, f32[2048]{0:T(1024)S(1)} %get-tuple-element.320, s32[2048]{0:T(1024)S(1)} %bitcast.145), kind=kLoop, calls=%fused_computation.30 | loop fusion | flops 46891008 | bytes 46915584 | tf_op jit(solution)/shard_map/convert_element_type | solution.py:1421
  288.8 8.6 %convolution_convert_fusion = bf16[2048,512]{1,0:T(8,128)(2,1)S(1)} fusion(bf16[2048,3816]{0,1:T(8,128)(2,1)S(1)} %subtract_convert_fusion, bf16[3816,512]{1,0:T(8,128)(2,1)S(1)} %copy-done.21), kind=kOutput, calls=%fused_computation.57 | convolution fusion | flops 8003780608 | bytes 21635072 | tf_op jit(solution)/shard_map/tv,vd->td/dot_general | solution.py:1423
  297.3 18.8 %reduce_rows.1 = f32[256,512]{1,0:T(8,128)S(1)} custom-call(bf16[8,256,512]{2,1,0:T(8,128)(2,1)S(1)} %bitcast.114), custom_call_target="tpu_custom_call" | custom-call | tf_op jit(solution)/shard_map/reduce_rows/pallas_call | solution.py:700
  316.4 4.9 gather_fusion.2
  321.3 2.5 multiply_reduce_fusion
  327.1 29.0 %feed_back.2 = (f32[1024,512]{1,0:T(8,128)}, f32[8,512]{1,0:T(8,128)}, bf16[4,512,512]{2,1,0:T(8,128)(2,1)}, bf16[4,512,512]{2,1,0:T(8,128)(2,1)}, bf16[4,512,512]{2,1,0:T(8,128)(2,1)}) custom-call(f32[1024,512]{1,0:T(8,128)} %broadcast_add_fusion.dx, f32[1024,512]{1,0:T(8,128)} %copy-done.4, f32[1,512]{1,0:T(1,128)} %copy-done.17, ...), custom_call_target="tpu_custom_call" | custom-call | tf_op jit(solution)/shard_map/feed_back/pallas_call | solution.py:1172
  356.1 27.6 %attend_back.2 = (f32[1024,512]{1,0:T(8,128)}, f32[2,8,512]{2,1,0:T(8,128)}, bf16[4,512,512]{2,1,0:T(8,128)(2,1)}) custom-call(f32[8]{0:T(128)} %copy-done.20, f32[1024,512]{1,0:T(8,128)} %get-tuple-element.214.dx, f32[1024,512]{1,0:T(8,128)} %copy-done.6, f32[1,512]{1,0:T(1,128)} %copy-done.19, bf16[32,512,512]{2,1,0:T(8,128)(2,1)} %copy-done, ...), custom_call_target="tpu_custom_call" | custom-call | tf_op jit(solution)/shard_map/attend_back/pallas_call | solution.py:1013
  383.7 29.3 %feed_back.3 = (f32[1024,512]{1,0:T(8,128)}, f32[8,512]{1,0:T(8,128)}, bf16[4,512,512]{2,1,0:T(8,128)(2,1)}, bf16[4,512,512]{2,1,0:T(8,128)(2,1)}, bf16[4,512,512]{2,1,0:T(8,128)(2,1)}) custom-call(f32[1024,512]{1,0:T(8,128)} %get-tuple-element.219.dx, f32[1024,512]{1,0:T(8,128)} %copy-done.3, f32[1,512]{1,0:T(1,128)} %copy-done.16, ...), custom_call_target="tpu_custom_call" | custom-call | tf_op jit(solution)/shard_map/feed_back/pallas_call | solution.py:1172
  413.0 27.7 %attend_back.3 = (f32[1024,512]{1,0:T(8,128)}, f32[2,8,512]{2,1,0:T(8,128)}, bf16[4,512,512]{2,1,0:T(8,128)(2,1)}) custom-call(f32[8]{0:T(128)} %copy-done.20, f32[1024,512]{1,0:T(8,128)} %get-tuple-element.223.dx, f32[1024,512]{1,0:T(8,128)} %multiply_multiply_fusion.2.x, f32[1,512]{1,0:T(1,128)} %copy-done.18, bf16[32,512,512]{2,1,0:T(8,128)(2,1)} %copy-done, ...), custom_call_target="tpu_custom_call" | custom-call | tf_op jit(solution)/shard_map/attend_back/pallas_call | solution.py:1013
  444.2 2.4 fusion.42
  449.1 16.1 %group_7.1 = bf16[8,128,512]{2,1,0:T(8,128)(2,1)} custom-call(bf16[8,128,512]{2,1,0:T(8,128)(2,1)} %bitcast.140), custom_call_target="tpu_custom_call" | custom-call | tf_op jit(solution)/shard_map/group_7/pallas_call | solution.py:107
  465.2 11.4 %fusion.47 = f32[3816,512]{1,0:T(8,128)S(1)} fusion(bf16[2048,3816]{0,1:T(8,128)(2,1)} %copy-done.25, bf16[2048,512]{1,0:T(8,128)(2,1)S(1)} %bitcast.128), kind=kOutput, calls=%fused_computation.148 | convolution fusion | flops 8002732032 | bytes 25542656 | tf_op jit(solution)/shard_map/tv,td->vd/dot_general | solution.py:1422
  477.3 6.6 pad_add_fusion
  485.9 151.3 %settle_gradients.1 = (bf16[6,8,4,16,512]{4,3,2,1,0:T(8,128)(2,1)}, f32[4,960,512]{2,1,0:T(8,128)}, f32[8,512]{1,0:T(8,128)}) custom-call(bf16[4,8,2,2,16,512]{5,4,3,2,1,0:T(8,128)(2,1)} %bitcast.136, bf16[4,8,2,2,16,512]{5,4,3,2,1,0:T(8,128)(2,1)} %bitcast.133, bf16[4,8,2,2,16,512]{5,4,3,2,1,0:T(8,128)(2,1)} %bitcast.134, ...), custom_call_target="tpu_custom_call" | custom-call | tf_op jit(solution)/shard_map/settle_gradients/pallas_call | solution.py:595
  642.0 21.8 %fusion.38 = (bf16[3816,512]{1,0:T(8,128)(2,1)}, f32[3816,512]{1,0:T(8,128)}, f32[3816,512]{1,0:T(8,128)}, f32[3816,512]{1,0:T(8,128)}) fusion(f32[3816,512]{1,0:T(8,128)} %t_ref.1, f32[]{:T(128)} %bitcast.46, f32[]{:T(128)} %bitcast.45, f32[3840,512]{1,0:T(8,128)} %bitcast.125, f32[]{:T(128)} %min.3, f32[3816,512]{1,0:T(8,128)} %param.35, ...), kind=kLoop, calls=%fused_computation.141 | loop fusion | flops 33214464 | bytes 58613772 | tf_op jit(solution)/shard_map/convert_element_type | solution.py:1556
  665.7 22.7 %turn_slots.1 = (f32[6,512,512]{2,1,0:T(8,128)}, f32[6,512,512]{2,1,0:T(8,128)}, bf16[8,6,16,512]{3,2,1,0:T(8,128)(2,1)}) custom-call(s32[7]{0:T(128)} %pad_add_fusion.1.scalars, f32[3]{0:T(128)} %pad_maximum_fusion.1.numbers, f32[6,512,512]{2,1,0:T(8,128)} %left.1, f32[6,512,512]{2,1,0:T(8,128)} %right.1, f32[6,8,4,16,512]{4,3,2,1,0:T(8,128)} %bitcast.122, ...), custom_call_target="tpu_custom_call" | custom-call | tf_op jit(solution)/shard_map/turn_slots/pallas_call | solution.py:1252
  688.4 34.9 %slots_11.1 = bf16[8,6,4,16,512]{4,3,2,1,0:T(8,128)(2,1)} custom-call(bf16[8,6,16,512]{3,2,1,0:T(8,128)(2,1)} %get-tuple-element.245.x_ref), custom_call_target="tpu_custom_call" | custom-call | tf_op jit(solution)/shard_map/slots_11/pallas_call | solution.py:768
  723.4 2.6 gather_fusion.3
  726.0 6.1 fusion.40
  (174 shorter events, 46.2 us)
Async XLA Ops:
  0.6 9.9 %copy-start.39 = (f32[6,64]{1,0:T(8,128)S(1)}, f32[6,64]{1,0:T(8,128)}, u32[]{:S(2)}) copy-start(f32[6,64]{1,0:T(8,128)} %param.32) | copy-start | bytes 4612
  5.8 114.3 %copy-start.46 = (s32[1024]{0:T(1024)}, s32[1024]{0:T(1024)S(1)}, u32[]{:S(2)}) copy-start(s32[1024]{0:T(1024)S(1)} %get-tuple-element.381) | copy-start | bytes 12292
  10.6 3.2 copy-start.1
  113.1 5.9 copy-start
  127.2 2.6 copy-start.22
  127.2 2.6 copy-start.29
  127.3 2.6 copy-start.31
  127.3 2.6 copy-start.33
  127.3 2.6 copy-start.13
  127.9 20.0 %copy-start.35 = (f32[1024]{0:T(1024)}, f32[1024]{0:T(1024)S(1)}, u32[]{:S(2)}) copy-start(f32[1024]{0:T(1024)S(1)} %multiply_reduce_fusion.5) | copy-start | bytes 12292
  129.9 18.1 %copy-start.18 = (f32[1,512]{1,0:T(1,128)}, f32[1,512]{1,0:T(1,128)S(1)}, u32[]{:S(2)}) copy-start(f32[1,512]{1,0:T(1,128)S(1)} %slice.121.gain) | copy-start | bytes 6148
  130.1 35.2 %copy-start.2 = (s32[2,512,1]{2,1,0:T(8,128)}, s32[2,512,1]{2,1,0:T(8,128)S(1)}, u32[]{:S(2)}) copy-start(s32[2,512,1]{2,1,0:T(8,128)S(1)} %reshape_reshape.3.seg_col) | copy-start | bytes 12292
  130.1 35.2 %copy-start.20 = (f32[8]{0:T(128)}, f32[8]{0:T(128)S(1)}, u32[]{:S(2)}) copy-start(f32[8]{0:T(128)S(1)} %multiply_power_fusion.slopes) | copy-start | bytes 100
  150.0 13.0 %copy-start.3 = (f32[1024,512]{1,0:T(8,128)}, f32[1024,512]{1,0:T(8,128)S(1)}, u32[]{:S(2)}) copy-start(f32[1024,512]{1,0:T(8,128)S(1)} %get-tuple-element.206.x) | copy-start | bytes 6291460
  150.0 13.0 %copy-start.14 = (f32[2,8,512]{2,1,0:T(8,128)}, f32[2,8,512]{2,1,0:T(8,128)S(1)}, u32[]{:S(2)}) copy-start(f32[2,8,512]{2,1,0:T(8,128)S(1)} %get-tuple-element.227.lse) | copy-start | bytes 98308
  150.1 12.9 %copy-start.16 = (f32[1,512]{1,0:T(1,128)}, f32[1,512]{1,0:T(1,128)S(1)}, u32[]{:S(2)}) copy-start(f32[1,512]{1,0:T(1,128)S(1)} %slice.123.gain) | copy-start | bytes 6148
  165.3 17.7 %copy-start.19 = (f32[1,512]{1,0:T(1,128)}, f32[1,512]{1,0:T(1,128)S(1)}, u32[]{:S(2)}) copy-start(f32[1,512]{1,0:T(1,128)S(1)} %slice.125.gain) | copy-start | bytes 6148
  188.6 12.2 %copy-start.17 = (f32[1,512]{1,0:T(1,128)}, f32[1,512]{1,0:T(1,128)S(1)}, u32[]{:S(2)}) copy-start(f32[1,512]{1,0:T(1,128)S(1)} %slice.127.gain) | copy-start | bytes 6148
  273.9 14.8 %copy-start.21 = (bf16[3816,512]{1,0:T(8,128)(2,1)S(1)}, bf16[3816,512]{1,0:T(8,128)(2,1)}, u32[]{:S(2)}) copy-start(bf16[3816,512]{1,0:T(8,128)(2,1)} %get-tuple-element.557) | copy-start | bytes 11722756
  288.8 8.6 %copy-start.25 = (bf16[2048,3816]{0,1:T(8,128)(2,1)}, bf16[2048,3816]{0,1:T(8,128)(2,1)S(1)}, u32[]{:S(2)}) copy-start(bf16[2048,3816]{0,1:T(8,128)(2,1)S(1)} %subtract_convert_fusion) | copy-start | bytes 46891012
  321.3 2.6 copy-start.24
  413.0 27.8 %copy-start.23 = (f32[1024,512]{1,0:T(8,128)S(1)}, f32[1024,512]{1,0:T(8,128)}, u32[]{:S(2)}) copy-start(f32[1024,512]{1,0:T(8,128)} %copy-done.22) | copy-start | bytes 6291460
  440.8 3.4 copy-start.36
  444.2 2.7 copy-start.34
  444.2 2.6 copy-start.47
  446.9 18.3 %copy-start.26 = (bf16[8,256,512]{2,1,0:T(8,128)(2,1)S(1)}, bf16[8,256,512]{2,1,0:T(8,128)(2,1)}, u32[]{:S(2)}) copy-start(bf16[8,256,512]{2,1,0:T(8,128)(2,1)} %ring_rows.1) | copy-start | bytes 6291460
  465.2 12.1 %copy-start.28 = (bf16[8,128,512]{2,1,0:T(8,128)(2,1)S(1)}, bf16[8,128,512]{2,1,0:T(8,128)(2,1)}, u32[]{:S(2)}) copy-start(bf16[8,128,512]{2,1,0:T(8,128)(2,1)} %group_7.1) | copy-start | bytes 3145732
  477.3 6.6 copy-start.30
  477.3 6.6 copy-start.32
  641.9 21.8 %copy-start.40 = (f32[6,64]{1,0:T(8,128)S(1)}, f32[6,64]{1,0:T(8,128)}, u32[]{:S(2)}) copy-start(f32[6,64]{1,0:T(8,128)} %param.32) | copy-start | bytes 4612
  641.9 21.8 %copy-start.43 = (f32[6,64]{1,0:T(8,128)S(1)}, f32[6,64]{1,0:T(8,128)}, u32[]{:S(2)}) copy-start(f32[6,64]{1,0:T(8,128)} %param.37) | copy-start | bytes 4612
  642.0 21.8 %copy-start.44 = (f32[6,64]{1,0:T(8,128)S(1)}, f32[6,64]{1,0:T(8,128)}, u32[]{:S(2)}) copy-start(f32[6,64]{1,0:T(8,128)} %param.36) | copy-start | bytes 4612
  (16 other events, 22.2 us)

commit v3 on v2

--- a/solution.py
+++ b/solution.py
@@ -282,47 +282,6 @@
         compiler_params=params(cid, 24 << 20),
         name="open_step",
     )(shard, table, wanted, facts, gains)
-
-
-def ring_rows_kernel(n_rep, n, x_ref, o_ref, send, recv):
-    here = Place(n_rep, n)
-    enter([here.next, here.prev])
-    rows = x_ref.shape[0]
-    hops = n // 2
-    copies = []
-    waiting = [None, None]
-    for s in range(hops):
-        for way in range(2):
-            peer = here.next if way == 0 else here.prev
-            origin = here.at(-s if way == 0 else s)
-            if s > 0:
-                waiting[way].wait_recv()
-            window = pl.ds(0, rows)
-            if s == hops - 1:
-                window = pl.ds(way * (rows // 2), rows // 2)
-            src = x_ref.at[window] if s == 0 else o_ref.at[origin, window]
-            cp = remote(src, o_ref.at[origin, window], send.at[way, s], recv.at[way, s], peer)
-            cp.start()
-            waiting[way] = cp
-            copies.append(cp)
-    o_ref[here.f] = x_ref[...]
-    for way in range(2):
-        waiting[way].wait_recv()
-    for cp in copies:
-        cp.wait_send()
-
-
-def ring_rows(mesh_sizes, cid, x):
-    n_rep, n = mesh_sizes
-    return pl.pallas_call(
-        partial(ring_rows_kernel, n_rep, n),
-        out_shape=jax.ShapeDtypeStruct((n,) + x.shape, x.dtype),
-        in_specs=[VMEM],
-        out_specs=VMEM,
-        scratch_shapes=[pltpu.SemaphoreType.DMA((2, n // 2)), pltpu.SemaphoreType.DMA((2, n // 2))],
-        compiler_params=params(cid),
-        name="ring_rows",
-    )(x)
 
 
 def squares_row(square):
@@ -646,73 +605,6 @@
     )(*views, table, small, block_of, taken)
 
 
-def rows_kernel(n_rep, n, x_ref, o_ref, held, got, send, recv):
-    here = Place(n_rep, n)
-    enter([here.next, here.prev])
-    far = n // 2
-    rows = x_ref.shape[1] // 2
-    ring = {}
-
-    def lane(way, h, s):
-        d = far - s
-        q = here.at(d if way == 0 else -d)
-        before = ring.get((way, h, s - 1))
-        if before is None:
-            source = x_ref.at[q, pl.ds(h * rows, rows)]
-        else:
-            before.wait_recv()
-            total = x_ref[q, pl.ds(h * rows, rows)].astype(f32) + got[way, h, s - 1].astype(f32)
-            held[way, h, s - 1] = total.astype(held.dtype)
-            source = held.at[way, h, s - 1]
-        cp = remote(
-            source, got.at[way, h, s], send.at[way, h, s], recv.at[way, h, s], here.next if way == 0 else here.prev
-        )
-        cp.start()
-        ring[way, h, s] = cp
-
-    for s in range(far):
-        for turn in range(2):
-            for way in range(2):
-                h = way if turn == 1 else 1 - way
-                if turn == 0 and s < 2:
-                    continue
-                lane(way, h, s)
-        if s == 0:
-            for way in range(2):
-                lane(way, 1 - way, 1)
-    for h in range(2):
-        for way in range(2):
-            ring[way, h, far - 1].wait_recv()
-        at = pl.ds(h * rows, rows)
-        total = x_ref[here.f, at].astype(f32)
-        for way in range(2):
-            total = total + got[way, h, far - 1].astype(f32)
-        o_ref[at] = total
-    for cp in ring.values():
-        cp.wait_send()
-
-
-def reduce_rows(mesh_sizes, cid, x):
-    n_rep, n = mesh_sizes
-    _, rows, width = x.shape
-    far = n // 2
-    dma = pltpu.SemaphoreType.DMA
-    return pl.pallas_call(
-        partial(rows_kernel, n_rep, n),
-        out_shape=jax.ShapeDtypeStruct((rows, width), f32),
-        in_specs=[VMEM],
-        out_specs=VMEM,
-        scratch_shapes=[
-            pltpu.VMEM((2, 2, far - 1, rows // 2, width), x.dtype),
-            pltpu.VMEM((2, 2, far, rows // 2, width), x.dtype),
-            dma((2, 2, far)),
-            dma((2, 2, far)),
-        ],
-        compiler_params=params(cid, 24 << 20),
-        name="reduce_rows",
-    )(x)
-
-
 def slots_kernel(n_rep, n, to_slots, x_ref, o_ref, keep, a_s, a_r, f_s, f_r):
     here = Place(n_rep, n)
     ypeer = (lax.rem(here.r + 2, 4), here.f)
@@ -1262,6 +1154,210 @@
     )(scalars, numbers, left, right, view, grads, m, v)
 
 
+def head_kernel(
+    n_rep, n, vocab, tile, x_ref, e_ref, label_ref, picked_ref, table_ref, loss_ref,
+    table, rows_all, logits, stats, shared, held, got,
+    load_s, ring_s, ring_r, stat_s, stat_r, back_s, back_r,
+):
+    here = Place(n_rep, n)
+    me = here.f
+    others = [lax.rem(me + k, n) for k in range(1, n)]
+    enter([(here.r, o) for o in others])
+    picks, width = x_ref.shape
+    half = picks // 2
+    tiles = table.shape[0] // tile
+    far = n // 2
+    load = pltpu.make_async_copy(e_ref, table, load_s)
+    load.start()
+    sends = []
+    waiting = {}
+
+    def hop(way, s):
+        origin = here.at(-s if way == 0 else s)
+        window = pl.ds(way * half, half) if s == far - 1 else pl.ds(0, picks)
+        src = x_ref if s == 0 else rows_all.at[origin, window]
+        cp = remote(
+            src,
+            rows_all.at[origin, window],
+            ring_s.at[way, s],
+            ring_r.at[way, s],
+            here.next if way == 0 else here.prev,
+        )
+        cp.start()
+        sends.append(cp)
+        waiting[way] = cp
+
+    def columns(t):
+        return t * tile + lax.broadcasted_iota(jnp.int32, (picks, tile), 1)
+
+    def span(t):
+        return pl.ds(pl.multiple_of(t * tile, tile), tile)
+
+    def fold(x, join):
+        out = x[:, :128]
+        for k in range(1, tile // 128):
+            out = join(out, x[:, k * 128 : (k + 1) * 128])
+        return out
+
+    def forward(origin):
+        rows = rows_all[origin]
+        label = label_ref[origin]
+
+        def product(t, top):
+            scores = mm(rows, table[span(t)], NT)
+            scores = jnp.where(columns(t) < vocab, scores, masked_score)
+            logits[origin, :, span(t)] = scores
+            return jnp.maximum(top, fold(scores, jnp.maximum))
+
+        top = lax.fori_loop(0, tiles, product, jnp.full((picks, 128), masked_score, f32))
+        top = jnp.max(top, axis=1, keepdims=True)
+
+        def weigh(t, sums):
+            total, target = sums
+            scores = logits[origin, :, span(t)]
+            total = total + fold(jnp.exp(scores - top), jnp.add)
+            hit = jnp.where(columns(t) == label, scores, 0.0)
+            return total, target + fold(hit, jnp.add)
+
+        zero = jnp.zeros((picks, 128), f32)
+        total, target = lax.fori_loop(0, tiles, weigh, (zero, zero))
+        log_sum = top + jnp.log(jnp.sum(total, axis=1, keepdims=True))
+        target = jnp.sum(target, axis=1, keepdims=True)
+        lane = lax.broadcasted_iota(jnp.int32, (picks, 128), 1)
+        both = jnp.where(lane == 0, log_sum, target).T
+        stats[pl.ds(origin, 1)] = both[0:1]
+        stats[pl.ds(n + origin, 1)] = both[1:2]
+
+    rows_all[me] = x_ref[...]
+    for way in range(2):
+        hop(way, 0)
+    load.wait()
+    forward(me)
+    for s in range(far):
+        for way in range(2):
+            waiting[way].wait_recv()
+            if s < far - 1:
+                hop(way, s + 1)
+        if s < far - 1:
+            forward(here.at(-s - 1))
+            forward(here.at(s + 1))
+        else:
+            forward(here.at(far))
+
+    moves = []
+    for k, o in enumerate(others):
+        cp = remote(stats, shared.at[me], stat_s.at[k], stat_r.at[k], (here.r, o))
+        cp.start()
+        moves.append(cp)
+    shared[me] = stats[...]
+    table_ref[...] = jnp.zeros(table_ref.shape, f32)
+    for cp in moves:
+        cp.wait_recv()
+    top = shared[0, :n]
+    for k in range(1, n):
+        top = jnp.maximum(top, shared[k, :n])
+    total = jnp.exp(shared[0, :n] - top)
+    target = shared[0, n:]
+    for k in range(1, n):
+        total = total + jnp.exp(shared[k, :n] - top)
+        target = target + shared[k, n:]
+    log_sum = top + jnp.log(total)
+    for cp in moves:
+        cp.wait_send()
+    stats[:n] = log_sum
+    stats[n:] = log_sum - target
+    mine = stats[pl.ds(n + me, 1)]
+    loss_ref[...] = jnp.broadcast_to(jnp.sum(mine, axis=1, keepdims=True), loss_ref.shape)
+
+    def backward(q):
+        rows = rows_all[q]
+        label = label_ref[q]
+        norm = jnp.broadcast_to(stats[pl.ds(q, 1)], (128, picks)).T
+
+        def product(t, out):
+            scores = logits[q, :, span(t)]
+            parts = [jnp.exp(scores[:, k * 128 : (k + 1) * 128] - norm) for k in range(tile // 128)]
+            soft = jnp.concatenate(parts, axis=1)
+            grad = (soft - jnp.where(columns(t) == label, 1.0, 0.0)).astype(bf16)
+            table_ref[span(t)] += mm(grad, rows, TN)
+            return out + mm(grad, table[span(t)])
+
+        return lax.fori_loop(0, tiles, product, jnp.zeros((picks, width), f32))
+
+    ring = {}
+
+    def lane_send(way, h, s, value):
+        before = ring.get((way, h, s - 1))
+        if before is not None:
+            before.wait_recv()
+            value = value + got[way, h, s - 1].astype(f32)
+        held[way, h, s] = value.astype(bf16)
+        cp = remote(
+            held.at[way, h, s],
+            got.at[way, h, s],
+            back_s.at[way, h, s],
+            back_r.at[way, h, s],
+            here.next if way == 0 else here.prev,
+        )
+        cp.start()
+        ring[way, h, s] = cp
+
+    out = backward(here.at(far))
+    lane_send(0, 0, 0, out[:half])
+    lane_send(1, 1, 0, out[half:])
+    for s in range(1, far):
+        for way in range(2):
+            d = far - s
+            out = backward(here.at(d if way == 0 else -d))
+            for h in (1 - way, way):
+                lane_send(way, h, s, out[h * half : (h + 1) * half])
+    out = backward(me)
+    for h in range(2):
+        total = out[h * half : (h + 1) * half]
+        for way in range(2):
+            ring[way, h, far - 1].wait_recv()
+            total = total + got[way, h, far - 1].astype(f32)
+        picked_ref[pl.ds(h * half, half)] = total
+    for cp in sends + list(ring.values()):
+        cp.wait_send()
+
+
+def head_step(mesh_sizes, cid, picked, table, labels, vocab):
+    n_rep, n = mesh_sizes
+    picks, width = picked.shape
+    padded = table.shape[0]
+    far = n // 2
+    dma = pltpu.SemaphoreType.DMA
+    return pl.pallas_call(
+        partial(head_kernel, n_rep, n, vocab, 256),
+        out_shape=[
+            jax.ShapeDtypeStruct((picks, width), f32),
+            jax.ShapeDtypeStruct((padded, width), f32),
+            jax.ShapeDtypeStruct((8, 128), f32),
+        ],
+        in_specs=[VMEM, ANY, VMEM],
+        out_specs=[VMEM, VMEM, VMEM],
+        scratch_shapes=[
+            pltpu.VMEM((padded, width), bf16),
+            pltpu.VMEM((n, picks, width), bf16),
+            pltpu.VMEM((n, picks, padded), f32),
+            pltpu.VMEM((2 * n, picks), f32),
+            pltpu.VMEM((n, 2 * n, picks), f32),
+            pltpu.VMEM((2, 2, far, picks // 2, width), bf16),
+            pltpu.VMEM((2, 2, far, picks // 2, width), bf16),
+            dma,
+            dma((2, far)),
+            dma((2, far)),
+            dma((n - 1,)),
+            dma((n - 1,)),
+            dma((2, 2, far)),
+            dma((2, 2, far)),
+        ],
+        compiler_params=params(cid, 60 << 20),
+        name="head_step",
+    )(picked, table, labels.reshape(n, picks, 1))
+
+
 class Transport:
     def __init__(self, n_rep, n_fsdp, shard_rows):
         self.sizes = (n_rep, n_fsdp)
@@ -1286,21 +1382,6 @@
         if self.kernels:
             return group_exchange(self.sizes, cid, x, True)
         return lax.all_to_all(x, "fsdp", split_axis=0, concat_axis=0, tiled=True)
-
-    def share(self, cid, x):
-        if self.kernels:
-            return group_exchange(self.sizes, cid, x, False)
-        return lax.all_gather(x, "fsdp")
-
-    def share_rows(self, cid, x):
-        if self.kernels:
-            return ring_rows(self.sizes, cid, x)
-        return lax.all_gather(x, "fsdp")
-
-    def sum_rows(self, cid, x):
-        if self.kernels:
-            return reduce_rows(self.sizes, cid, x)
-        return lax.psum_scatter(x.astype(f32), "fsdp", scatter_dimension=0)
 
 
 def body(
@@ -1335,7 +1416,8 @@
     tokens = micro_count * pack_length
     picks = micro_count * pick_count
     move = Transport(replicas, groups, shard_rows)
-    table_low = embed.astype(bf16)
+    padded_rows = -(-vocab_rows // 768) * 768
+    table_low = jnp.pad(embed.astype(bf16), ((0, padded_rows - vocab_rows), (0, 0)))
 
     ids = token_ids.reshape(tokens)
     index = jnp.arange(tokens, dtype=jnp.int32)
@@ -1402,26 +1484,34 @@
     positions = masked_pos.reshape(micro_count, pick_count)
     flat_positions = (positions + jnp.arange(micro_count, dtype=jnp.int32)[:, None] * pack_length).reshape(picks)
     picked = jnp.take(final_rows, flat_positions, axis=0).astype(bf16)
-    all_picked = move.share_rows(4, picked).reshape(groups * picks, model_width)
-    logits = jnp.einsum("td,vd->tv", all_picked, table_low, preferred_element_type=f32)
-    top_value = jnp.max(logits, axis=-1)
-    exp_total = jnp.sum(jnp.exp(logits - top_value[:, None]), axis=-1)
     label_local = all_labels - member * vocab_rows
-    columns = jnp.arange(vocab_rows, dtype=jnp.int32)
-    label_hits = columns[None, :] == label_local[:, None]
-    target = jnp.sum(jnp.where(label_hits, logits, 0.0), axis=-1)
-    stats = move.share(5, jnp.stack([top_value, exp_total, target]))
-    top_all = jnp.max(stats[:, 0], axis=0)
-    total_all = jnp.sum(stats[:, 1] * jnp.exp(stats[:, 0] - top_all[None]), axis=0)
-    target_all = jnp.sum(stats[:, 2], axis=0)
-    entropy = top_all + jnp.log(total_all) - target_all
-    loss_local = jnp.sum(lax.dynamic_slice_in_dim(entropy, member * picks, picks))
-    grad_logits = (
-        jnp.exp(logits - top_all[:, None]) / total_all[:, None] - label_hits.astype(f32)
-    ).astype(bf16)
-    grad_table = jnp.einsum("tv,td->vd", grad_logits, all_picked, preferred_element_type=f32)
-    grad_picked = jnp.einsum("tv,vd->td", grad_logits, table_low, preferred_element_type=f32)
-    grad_picked = move.sum_rows(6, grad_picked.astype(bf16).reshape(groups, picks, model_width))
+    label_local = jnp.where((label_local >= 0) & (label_local < vocab_rows), label_local, -1)
+    if move.kernels:
+        grad_picked, grad_table, loss_local = head_step(
+            move.sizes, 4, picked, table_low, label_local.reshape(groups, picks), vocab_rows
+        )
+        loss_local = loss_local[0, 0]
+    else:
+        all_picked = lax.all_gather(picked, "fsdp", tiled=True)
+        logits = jnp.einsum("td,vd->tv", all_picked, table_low[:vocab_rows], preferred_element_type=f32)
+        top_value = jnp.max(logits, axis=-1)
+        exp_total = jnp.sum(jnp.exp(logits - top_value[:, None]), axis=-1)
+        label_hits = jnp.arange(vocab_rows, dtype=jnp.int32)[None, :] == label_local[:, None]
+        target = jnp.sum(jnp.where(label_hits, logits, 0.0), axis=-1)
+        stats = lax.all_gather(jnp.stack([top_value, exp_total, target]), "fsdp")
+        top_all = jnp.max(stats[:, 0], axis=0)
+        total_all = jnp.sum(stats[:, 1] * jnp.exp(stats[:, 0] - top_all[None]), axis=0)
+        target_all = jnp.sum(stats[:, 2], axis=0)
+        entropy = top_all + jnp.log(total_all) - target_all
+        loss_local = jnp.sum(lax.dynamic_slice_in_dim(entropy, member * picks, picks))
+        grad_logits = (
+            jnp.exp(logits - top_all[:, None]) / total_all[:, None] - label_hits.astype(f32)
+        ).astype(bf16)
+        grad_table = jnp.einsum("tv,td->vd", grad_logits, all_picked, preferred_element_type=f32)
+        grad_table = jnp.pad(grad_table, ((0, padded_rows - vocab_rows), (0, 0)))
+        grad_picked = jnp.einsum("tv,vd->td", grad_logits, table_low[:vocab_rows], preferred_element_type=f32)
+        grad_picked = grad_picked.reshape(groups, picks, model_width)
+        grad_picked = lax.psum_scatter(grad_picked, "fsdp", scatter_dimension=0)
 
     match = flat_positions[None, :] == index[:, None]
     place = jnp.sum(jnp.where(match, jnp.arange(picks, dtype=jnp.int32)[None, :] + 1, 0), axis=1)
@@ -1445,8 +1535,6 @@
         layer_grads[layer] = [grads_attention] + grads_feed
     grad_embedded, gain_grads[0] = first_pull(grad_stream)
     grad_rows = grad_embedded.astype(bf16)
-    padded_rows = -(-vocab_rows // 384) * 384
-    grad_table = jnp.pad(grad_table, ((0, padded_rows - vocab_rows), (0, 0)))
     row_index = jnp.arange(padded_rows, dtype=jnp.int32)
 
     def given(cid, k, grad_table):

time: 745 us -> 751 us (level)
  Pallas kernels: 552 us -> 619 us
  matrix products: 47.1 us -> 12.4 us
  other arithmetic: 95 us -> 61.8 us
    pallas_call x2 -> x1, Pallas kernels: 45.1 us -> 120 us  [head_step(): pl.pallas_call(partial(head_kernel, n_rep, n, vocab, 256), out_shape=[jax...]
    dot_general x3 -> x0, matrix products: 37 us -> none  [the longest x1 17 us: body(): jnp.einsum('td,vd->tv', all_picked, table_low, preferred_element_type=f32)]
    convert_element_type x2 -> x1, other arithmetic: 20.5 us -> 3.72 us  [body(): embed.astype(bf16)]
    reduce_sum x4 -> x0, other arithmetic: 16.5 us -> none  [the longest x1 14.3 us: body(): exp_total = jnp.sum(jnp.exp(logits - top_value[:, None]), axis=-1)]
    unnamed x96 -> x74, local copies, waits for them, and re-layouts: 20.3 us -> 21.9 us
    pallas_call x2 -> x1, Pallas kernels: 24.5 us -> 23.9 us  [group_exchange(): pl.pallas_call(partial(group_kernel, n_rep, n, spread), out_shape=jax.Sha...]
where the time goes in v3:
time: 751 us; the launch traced here: 741 us
  Pallas kernels  619 us (82%)
  other arithmetic  61.8 us (8%)
  local copies, waits for them, and re-layouts  40.2 us (5%)
  matrix products  12.4 us (2%)
  between operations  8.03 us (1%)
    pallas_call x1, Pallas kernels, settle_gradients(): pl.pallas_call(partial(reduce_kernel, n_rep, n, half, table_rows, each),...  144 us
    pallas_call x1, Pallas kernels, head_step(): pl.pallas_call(partial(head_kernel, n_rep, n, vocab, 256), out_shape=[jax...  120 us
    pallas_call x1, Pallas kernels, open_step(): pl.pallas_call(partial(opening_kernel, n_rep, n, half, half - 2 * (half /...  99.3 us
    pallas_call x2, Pallas kernels, feed_back(): pl.pallas_call(feed_back_kernel, grid=(pieces,), in_specs=[fixed((tokens,...  58.1 us
    pallas_call x2, Pallas kernels, attend_back(): pl.pallas_call(attend_back_kernel, grid=(packs, HEADS // 2), in_specs=[pl...  55.7 us
    pallas_call x2, Pallas kernels, attend(): pl.pallas_call(attend_kernel, grid=(packs, HEADS // 2), in_specs=[pl.Bloc...  35.6 us
    pallas_call x1, Pallas kernels, exchange_slots(): pl.pallas_call(partial(slots_kernel, n_rep, n, to_slots), out_shape=jax.S...  34.6 us
    pallas_call x2, Pallas kernels, feed(): pl.pallas_call(feed_kernel, grid=(pieces,), in_specs=[fixed((tokens, widt...  25.1 us

profile of v3, /device:TPU:25, one launch (start us, length us, event | category | flops | bytes accessed | tf_op | source)
XLA Modules:
  0.0 741.3 jit_solution(4068632147288204300)
XLA Ops:
  0.6 1.5 select_reduce_fusion.2
  2.9 1.5 convert_reduce_fusion
  8.0 2.5 convert_element_type.51.x_ref
  10.6 3.2 copy-done.1
  13.8 99.3 %open_step.1 = (bf16[32,512,512]{2,1,0:T(8,128)(2,1)S(1)}, bf16[8,128,512]{2,1,0:T(8,128)(2,1)S(1)}, s32[8,1,128]{2,1,0:T(1,128)S(1)}, s32[8,8,128]{2,1,0:T(8,12...) custom-call(bf16[32,64,512]{2,1,0:T(8,128)(2,1)S(1)} %convert_element_type.51.x_ref, f32[3816,512]{1,0:T(8,128)S(1)} %copy-done.1, ...), custom_call_target="tpu_custom_call" | custom-call | tf_op jit(solution)/shard_map/open_step/pallas_call | solution.py:247
  113.1 5.7 copy-done
  121.3 3.7 convert_element_type.52
  125.0 2.2 pad.20.e_ref
  128.6 1.7 multiply_multiply_fusion.2.x
  130.6 17.9 %attend.2 = (f32[1024,512]{1,0:T(8,128)S(1)}, bf16[1024,512]{1,0:T(8,128)(2,1)S(1)}, bf16[1024,1536]{1,0:T(8,128)(2,1)}, bf16[1024,512]{1,0:T(8,128)(2,1)S(1)}, f32[2,8,512]{2,1,0:T(8,128)S(1)}) custom-call(f32[8]{0:T(128)S(1)} %multiply_power_fusion.slopes, f32[1024,512]{1,0:T(8,128)} %multiply_multiply_fusion.2.x, f32[1,512]{1,0:T(1,128)S(1)} %slice.114.gain, ...), custom_call_target="tpu_custom_call" | custom-call | tf_op jit(solution)/shard_map/attend/pallas_call | solution.py:787
  151.2 12.9 %feed.2 = (f32[1024,512]{1,0:T(8,128)S(1)}, bf16[1024,512]{1,0:T(8,128)(2,1)S(1)}, bf16[4,1024,512]{2,1,0:T(8,128)(2,1)}, bf16[4,1024,512]{2,1,0:T(8,128)(2,1)}) custom-call(f32[1024,512]{1,0:T(8,128)S(1)} %get-tuple-element.209.x, f32[1,512]{1,0:T(1,128)S(1)} %slice.116.gain, bf16[32,512,512]{2,1,0:T(8,128)(2,1)} %copy-done, bf16[32,512,512]{2,1,0:T(8,128)(2,1)} %copy-done, ...), custom_call_target="tpu_custom_call" | custom-call | tf_op jit(solution)/shard_map/feed/pallas_call | solution.py:991
  166.5 17.7 %attend.3 = (f32[1024,512]{1,0:T(8,128)S(1)}, bf16[1024,512]{1,0:T(8,128)(2,1)S(1)}, bf16[1024,1536]{1,0:T(8,128)(2,1)}, bf16[1024,512]{1,0:T(8,128)(2,1)S(1)}, f32[2,8,512]{2,1,0:T(8,128)S(1)}) custom-call(f32[8]{0:T(128)S(1)} %multiply_power_fusion.slopes, f32[1024,512]{1,0:T(8,128)} %copy-done.6, f32[1,512]{1,0:T(1,128)S(1)} %slice.118.gain, ...), custom_call_target="tpu_custom_call" | custom-call | tf_op jit(solution)/shard_map/attend/pallas_call | solution.py:787
  188.1 1.6 copy-done.5
  189.7 12.2 %feed.3 = (f32[1024,512]{1,0:T(8,128)S(1)}, bf16[1024,512]{1,0:T(8,128)(2,1)S(1)}, bf16[4,1024,512]{2,1,0:T(8,128)(2,1)}, bf16[4,1024,512]{2,1,0:T(8,128)(2,1)}) custom-call(f32[1024,512]{1,0:T(8,128)S(1)} %copy-done.5, f32[1,512]{1,0:T(1,128)S(1)} %slice.120.gain, bf16[32,512,512]{2,1,0:T(8,128)(2,1)} %copy-done, bf16[32,512,512]{2,1,0:T(8,128)(2,1)} %copy-done, ...), custom_call_target="tpu_custom_call" | custom-call | tf_op jit(solution)/shard_map/feed/pallas_call | solution.py:991
  208.3 119.5 %head_step.1 = (f32[256,512]{1,0:T(8,128)}, f32[3840,512]{1,0:T(8,128)}, f32[8,128]{1,0:T(8,128)}) custom-call(bf16[256,512]{1,0:T(8,128)(2,1)} %select_convert_fusion.x_ref, bf16[3840,512]{1,0:T(8,128)(2,1)} %get-tuple-element.555, s32[8,256,1]{2,1,0:T(8,128)} %and_select_fusion.label_ref), custom_call_target="tpu_custom_call" | custom-call | tf_op jit(solution)/shard_map/head_step/pallas_call | solution.py:1331
  328.1 6.3 gather_fusion.2
  334.4 2.5 multiply_reduce_fusion
  339.8 29.0 %feed_back.2 = (f32[1024,512]{1,0:T(8,128)}, f32[8,512]{1,0:T(8,128)}, bf16[4,512,512]{2,1,0:T(8,128)(2,1)}, bf16[4,512,512]{2,1,0:T(8,128)(2,1)}, bf16[4,512,512]{2,1,0:T(8,128)(2,1)}) custom-call(f32[1024,512]{1,0:T(8,128)} %broadcast_add_fusion.dx, f32[1024,512]{1,0:T(8,128)} %copy-done.4, f32[1,512]{1,0:T(1,128)} %copy-done.17, ...), custom_call_target="tpu_custom_call" | custom-call | tf_op jit(solution)/shard_map/feed_back/pallas_call | solution.py:1064
  368.8 27.8 %attend_back.2 = (f32[1024,512]{1,0:T(8,128)}, f32[2,8,512]{2,1,0:T(8,128)}, bf16[4,512,512]{2,1,0:T(8,128)(2,1)}) custom-call(f32[8]{0:T(128)} %copy-done.20, f32[1024,512]{1,0:T(8,128)} %get-tuple-element.218.dx, f32[1024,512]{1,0:T(8,128)} %copy-done.6, f32[1,512]{1,0:T(1,128)} %copy-done.19, bf16[32,512,512]{2,1,0:T(8,128)(2,1)} %copy-done, ...), custom_call_target="tpu_custom_call" | custom-call | tf_op jit(solution)/shard_map/attend_back/pallas_call | solution.py:905
  396.6 29.1 %feed_back.3 = (f32[1024,512]{1,0:T(8,128)}, f32[8,512]{1,0:T(8,128)}, bf16[4,512,512]{2,1,0:T(8,128)(2,1)}, bf16[4,512,512]{2,1,0:T(8,128)(2,1)}, bf16[4,512,512]{2,1,0:T(8,128)(2,1)}) custom-call(f32[1024,512]{1,0:T(8,128)} %get-tuple-element.223.dx, f32[1024,512]{1,0:T(8,128)} %copy-done.3, f32[1,512]{1,0:T(1,128)} %copy-done.16, ...), custom_call_target="tpu_custom_call" | custom-call | tf_op jit(solution)/shard_map/feed_back/pallas_call | solution.py:1064
  425.7 27.9 %attend_back.3 = (f32[1024,512]{1,0:T(8,128)}, f32[2,8,512]{2,1,0:T(8,128)}, bf16[4,512,512]{2,1,0:T(8,128)(2,1)}) custom-call(f32[8]{0:T(128)} %copy-done.20, f32[1024,512]{1,0:T(8,128)} %get-tuple-element.227.dx, f32[1024,512]{1,0:T(8,128)} %multiply_multiply_fusion.2.x, f32[1,512]{1,0:T(1,128)} %copy-done.18, bf16[32,512,512]{2,1,0:T(8,128)(2,1)} %copy-done, ...), custom_call_target="tpu_custom_call" | custom-call | tf_op jit(solution)/shard_map/attend_back/pallas_call | solution.py:905
  453.7 2.3 multiply_reduce_fusion.1
  458.1 2.4 fusion.38
  461.2 2.2 fusion.26
  463.4 23.9 %group_7.1 = bf16[8,128,512]{2,1,0:T(8,128)(2,1)} custom-call(bf16[8,128,512]{2,1,0:T(8,128)(2,1)} %bitcast.112), custom_call_target="tpu_custom_call" | custom-call | tf_op jit(solution)/shard_map/group_7/pallas_call | solution.py:107
  487.3 8.9 %fusion.19 = f32[3840,512]{1,0:T(8,128)} fusion(f32[3840,512]{1,0:T(8,128)} %get-tuple-element.240, bf16[1024,512]{1,0:T(8,128)(2,1)} %bitcast.111, s32[1024]{0:T(1024)S(1)} %bitcast.127), kind=kOutput, calls=%fused_computation.38 | convolution fusion | flops 4032430080 | bytes 16781312 | tf_op jit(solution)/shard_map/dot_general | solution.py:1546
  498.1 144.0 %settle_gradients.1 = (bf16[6,8,4,16,512]{4,3,2,1,0:T(8,128)(2,1)}, f32[4,960,512]{2,1,0:T(8,128)}, f32[8,512]{1,0:T(8,128)}) custom-call(bf16[4,8,2,2,16,512]{5,4,3,2,1,0:T(8,128)(2,1)} %bitcast.108, bf16[4,8,2,2,16,512]{5,4,3,2,1,0:T(8,128)(2,1)} %bitcast.105, bf16[4,8,2,2,16,512]{5,4,3,2,1,0:T(8,128)(2,1)} %bitcast.106, ...), custom_call_target="tpu_custom_call" | custom-call | tf_op jit(solution)/shard_map/settle_gradients/pallas_call | solution.py:554
  647.0 21.8 %fusion.34 = (bf16[3816,512]{1,0:T(8,128)(2,1)}, f32[3816,512]{1,0:T(8,128)}, f32[3816,512]{1,0:T(8,128)}, f32[3816,512]{1,0:T(8,128)}) fusion(f32[3816,512]{1,0:T(8,128)} %t_ref.1, f32[]{:T(128)} %bitcast.38, f32[]{:T(128)} %bitcast.37, f32[3840,512]{1,0:T(8,128)} %bitcast.99, f32[]{:T(128)} %min.3, f32[3816,512]{1,0:T(8,128)} %param.35, f32[3816,512]{1,0:T(8,128)} %param.34), kind=kLoop, calls=%fused_computation.125 | loop fusion | flops 33214464 | bytes 58613772 | tf_op jit(solution)/shard_map/convert_element_type | solution.py:1644
  670.8 22.7 %turn_slots.1 = (f32[6,512,512]{2,1,0:T(8,128)}, f32[6,512,512]{2,1,0:T(8,128)}, bf16[8,6,16,512]{3,2,1,0:T(8,128)(2,1)}) custom-call(s32[7]{0:T(128)} %pad_add_fusion.scalars, f32[3]{0:T(128)} %pad_maximum_fusion.numbers, f32[6,512,512]{2,1,0:T(8,128)} %left.1, f32[6,512,512]{2,1,0:T(8,128)} %right.1, f32[6,8,4,16,512]{4,3,2,1,0:T(8,128)} %bitcast.96, ...), custom_call_target="tpu_custom_call" | custom-call | tf_op jit(solution)/shard_map/turn_slots/pallas_call | solution.py:1144
  693.5 34.6 %slots_11.1 = bf16[8,6,4,16,512]{4,3,2,1,0:T(8,128)(2,1)} custom-call(bf16[8,6,16,512]{3,2,1,0:T(8,128)(2,1)} %get-tuple-element.251.x_ref), custom_call_target="tpu_custom_call" | custom-call | tf_op jit(solution)/shard_map/slots_11/pallas_call | solution.py:660
  728.1 2.6 gather_fusion.3
  730.7 6.1 fusion.36
  (145 shorter events, 36.0 us)
Async XLA Ops:
  5.8 114.2 %copy-start.35 = (s32[1024]{0:T(1024)}, s32[1024]{0:T(1024)S(1)}, u32[]{:S(2)}) copy-start(s32[1024]{0:T(1024)S(1)} %get-tuple-element.381) | copy-start | bytes 12292
  8.0 2.5 copy-start.28
  10.6 3.2 copy-start.1
  113.1 5.7 copy-start
  127.2 1.4 copy-start.21
  128.6 1.7 copy-start.13
  130.4 18.2 %copy-start.18 = (f32[1,512]{1,0:T(1,128)}, f32[1,512]{1,0:T(1,128)S(1)}, u32[]{:S(2)}) copy-start(f32[1,512]{1,0:T(1,128)S(1)} %slice.114.gain) | copy-start | bytes 6148
  130.6 35.9 %copy-start.2 = (s32[2,512,1]{2,1,0:T(8,128)}, s32[2,512,1]{2,1,0:T(8,128)S(1)}, u32[]{:S(2)}) copy-start(s32[2,512,1]{2,1,0:T(8,128)S(1)} %reshape_reshape.3.seg_col) | copy-start | bytes 12292
  130.6 35.9 %copy-start.20 = (f32[8]{0:T(128)}, f32[8]{0:T(128)S(1)}, u32[]{:S(2)}) copy-start(f32[8]{0:T(128)S(1)} %multiply_power_fusion.slopes) | copy-start | bytes 100
  148.5 1.1 copy-start.9
  149.6 1.0 copy-start.10
  151.1 13.0 %copy-start.3 = (f32[1024,512]{1,0:T(8,128)}, f32[1024,512]{1,0:T(8,128)S(1)}, u32[]{:S(2)}) copy-start(f32[1024,512]{1,0:T(8,128)S(1)} %get-tuple-element.209.x) | copy-start | bytes 6291460
  151.2 12.9 %copy-start.16 = (f32[1,512]{1,0:T(1,128)}, f32[1,512]{1,0:T(1,128)S(1)}, u32[]{:S(2)}) copy-start(f32[1,512]{1,0:T(1,128)S(1)} %slice.116.gain) | copy-start | bytes 6148
  164.1 1.3 copy-start.6
  165.4 1.0 copy-start.7
  166.5 17.7 %copy-start.19 = (f32[1,512]{1,0:T(1,128)}, f32[1,512]{1,0:T(1,128)S(1)}, u32[]{:S(2)}) copy-start(f32[1,512]{1,0:T(1,128)S(1)} %slice.118.gain) | copy-start | bytes 6148
  184.2 1.3 copy-start.4
  185.5 0.9 copy-start.11
  186.4 1.0 copy-start.12
  188.1 1.6 copy-start.5
  189.7 12.2 %copy-start.17 = (f32[1,512]{1,0:T(1,128)}, f32[1,512]{1,0:T(1,128)S(1)}, u32[]{:S(2)}) copy-start(f32[1,512]{1,0:T(1,128)S(1)} %slice.120.gain) | copy-start | bytes 6148
  201.9 1.0 copy-start.8
  334.4 2.5 copy-start.23
  425.7 28.0 %copy-start.22 = (f32[1024,512]{1,0:T(8,128)S(1)}, f32[1024,512]{1,0:T(8,128)}, u32[]{:S(2)}) copy-start(f32[1024,512]{1,0:T(8,128)} %copy-done.21) | copy-start | bytes 6291460
  453.6 2.4 copy-start.27
  453.7 2.4 copy-start.31
  453.7 2.4 copy-start.26
  453.7 2.4 copy-start.30
  458.1 2.4 copy-start.25
  646.9 21.8 %copy-start.29 = (f32[6,64]{1,0:T(8,128)S(1)}, f32[6,64]{1,0:T(8,128)}, u32[]{:S(2)}) copy-start(f32[6,64]{1,0:T(8,128)} %param.32) | copy-start | bytes 4612
  647.0 21.8 %copy-start.32 = (f32[6,64]{1,0:T(8,128)S(1)}, f32[6,64]{1,0:T(8,128)}, u32[]{:S(2)}) copy-start(f32[6,64]{1,0:T(8,128)} %param.37) | copy-start | bytes 4612
  647.0 21.8 %copy-start.33 = (f32[6,64]{1,0:T(8,128)S(1)}, f32[6,64]{1,0:T(8,128)}, u32[]{:S(2)}) copy-start(f32[6,64]{1,0:T(8,128)} %param.36) | copy-start | bytes 4612
  (5 other events, 3.2 us)

commit v4 on v3

--- a/solution.py
+++ b/solution.py
@@ -279,7 +279,7 @@
             dma((n - 1,)),
             dma((n - 1,)),
         ],
-        compiler_params=params(cid, 24 << 20),
+        compiler_params=params(cid, 60 << 20),
         name="open_step",
     )(shard, table, wanted, facts, gains)
 
@@ -381,6 +381,8 @@
         for h_turn in range(2):
             for way in range(2):
                 h = way if h_turn == 1 else 1 - way
+                if s == far - 1:
+                    h = h_turn
                 if s == 0 and h_turn == 0:
                     continue
                 if s == 1 and h_turn == 0:
@@ -1187,11 +1189,20 @@
         sends.append(cp)
         waiting[way] = cp
 
-    def columns(t):
-        return t * tile + lax.broadcasted_iota(jnp.int32, (picks, tile), 1)
+    def columns(t, count):
+        return t * tile + lax.broadcasted_iota(jnp.int32, (count, tile), 1)
 
     def span(t):
         return pl.ds(pl.multiple_of(t * tile, tile), tile)
+
+    def stack(ref, origins):
+        return jnp.concatenate([ref[o] for o in origins], axis=0)
+
+    def scores_of(origins, t):
+        return jnp.concatenate([logits[o, :, span(t)] for o in origins], axis=0)
+
+    def piece(value, i):
+        return value[i * picks : (i + 1) * picks]
 
     def fold(x, join):
         out = x[:, :128]
@@ -1199,34 +1210,36 @@
             out = join(out, x[:, k * 128 : (k + 1) * 128])
         return out
 
-    def forward(origin):
-        rows = rows_all[origin]
-        label = label_ref[origin]
+    def forward(*origins):
+        rows, label = stack(rows_all, origins), stack(label_ref, origins)
+        count = rows.shape[0]
 
         def product(t, top):
             scores = mm(rows, table[span(t)], NT)
-            scores = jnp.where(columns(t) < vocab, scores, masked_score)
-            logits[origin, :, span(t)] = scores
+            scores = jnp.where(columns(t, count) < vocab, scores, masked_score)
+            for i, o in enumerate(origins):
+                logits[o, :, span(t)] = piece(scores, i)
             return jnp.maximum(top, fold(scores, jnp.maximum))
 
-        top = lax.fori_loop(0, tiles, product, jnp.full((picks, 128), masked_score, f32))
+        top = lax.fori_loop(0, tiles, product, jnp.full((count, 128), masked_score, f32))
         top = jnp.max(top, axis=1, keepdims=True)
 
         def weigh(t, sums):
             total, target = sums
-            scores = logits[origin, :, span(t)]
+            scores = scores_of(origins, t)
             total = total + fold(jnp.exp(scores - top), jnp.add)
-            hit = jnp.where(columns(t) == label, scores, 0.0)
+            hit = jnp.where(columns(t, count) == label, scores, 0.0)
             return total, target + fold(hit, jnp.add)
 
-        zero = jnp.zeros((picks, 128), f32)
+        zero = jnp.zeros((count, 128), f32)
         total, target = lax.fori_loop(0, tiles, weigh, (zero, zero))
         log_sum = top + jnp.log(jnp.sum(total, axis=1, keepdims=True))
         target = jnp.sum(target, axis=1, keepdims=True)
-        lane = lax.broadcasted_iota(jnp.int32, (picks, 128), 1)
+        lane = lax.broadcasted_iota(jnp.int32, (count, 128), 1)
         both = jnp.where(lane == 0, log_sum, target).T
-        stats[pl.ds(origin, 1)] = both[0:1]
-        stats[pl.ds(n + origin, 1)] = both[1:2]
+        for i, o in enumerate(origins):
+            stats[pl.ds(o, 1)] = both[0:1, i * picks : (i + 1) * picks]
+            stats[pl.ds(n + o, 1)] = both[1:2, i * picks : (i + 1) * picks]
 
     rows_all[me] = x_ref[...]
     for way in range(2):
@@ -1239,8 +1252,7 @@
             if s < far - 1:
                 hop(way, s + 1)
         if s < far - 1:
-            forward(here.at(-s - 1))
-            forward(here.at(s + 1))
+            forward(here.at(-s - 1), here.at(s + 1))
         else:
             forward(here.at(far))
 
@@ -1269,20 +1281,21 @@
     mine = stats[pl.ds(n + me, 1)]
     loss_ref[...] = jnp.broadcast_to(jnp.sum(mine, axis=1, keepdims=True), loss_ref.shape)
 
-    def backward(q):
-        rows = rows_all[q]
-        label = label_ref[q]
-        norm = jnp.broadcast_to(stats[pl.ds(q, 1)], (128, picks)).T
+    def backward(*origins):
+        rows, label = stack(rows_all, origins), stack(label_ref, origins)
+        count = rows.shape[0]
+        norm = [jnp.broadcast_to(stats[pl.ds(o, 1)], (128, picks)) for o in origins]
+        norm = jnp.concatenate(norm, axis=1).T
 
         def product(t, out):
-            scores = logits[q, :, span(t)]
+            scores = scores_of(origins, t)
             parts = [jnp.exp(scores[:, k * 128 : (k + 1) * 128] - norm) for k in range(tile // 128)]
             soft = jnp.concatenate(parts, axis=1)
-            grad = (soft - jnp.where(columns(t) == label, 1.0, 0.0)).astype(bf16)
+            grad = (soft - jnp.where(columns(t, count) == label, 1.0, 0.0)).astype(bf16)
             table_ref[span(t)] += mm(grad, rows, TN)
             return out + mm(grad, table[span(t)])
 
-        return lax.fori_loop(0, tiles, product, jnp.zeros((picks, width), f32))
+        return lax.fori_loop(0, tiles, product, jnp.zeros((count, width), f32))
 
     ring = {}
 
@@ -1306,11 +1319,12 @@
     lane_send(0, 0, 0, out[:half])
     lane_send(1, 1, 0, out[half:])
     for s in range(1, far):
-        for way in range(2):
-            d = far - s
-            out = backward(here.at(d if way == 0 else -d))
-            for h in (1 - way, way):
-                lane_send(way, h, s, out[h * half : (h + 1) * half])
+        d = far - s
+        out = backward(here.at(d), here.at(-d))
+        for turn in range(2):
+            for way in range(2):
+                h = way if turn == 1 else 1 - way
+                lane_send(way, h, s, piece(out, way)[h * half : (h + 1) * half])
     out = backward(me)
     for h in range(2):
         total = out[h * half : (h + 1) * half]
@@ -1329,7 +1343,7 @@
     far = n // 2
     dma = pltpu.SemaphoreType.DMA
     return pl.pallas_call(
-        partial(head_kernel, n_rep, n, vocab, 256),
+        partial(head_kernel, n_rep, n, vocab, 768),
         out_shape=[
             jax.ShapeDtypeStruct((picks, width), f32),
             jax.ShapeDtypeStruct((padded, width), f32),

time: 751 us -> 696 us (0.927)
  Pallas kernels: 619 us -> 566 us
    pallas_call x1, Pallas kernels: 120 us -> 68.2 us  [head_step(): pl.pallas_call(partial(head_kernel, n_rep, n, vocab, 768), out_shape=[jax...]
    unnamed x74, local copies, waits for them, and re-layouts: 21.9 us -> 13 us
where the time goes in v4:
time: 696 us; the launch traced here: 686 us
  Pallas kernels  566 us (81%)
  other arithmetic  64.5 us (9%)
  local copies, waits for them, and re-layouts  33.3 us (5%)
  matrix products  13.7 us (2%)
  between operations  8 us (1%)
    pallas_call x1, Pallas kernels, settle_gradients(): pl.pallas_call(partial(reduce_kernel, n_rep, n, half, table_rows, each),...  147 us
    pallas_call x1, Pallas kernels, open_step(): pl.pallas_call(partial(opening_kernel, n_rep, n, half, half - 2 * (half /...  101 us
    pallas_call x1, Pallas kernels, head_step(): pl.pallas_call(partial(head_kernel, n_rep, n, vocab, 768), out_shape=[jax...  68.2 us
    pallas_call x2, Pallas kernels, feed_back(): pl.pallas_call(feed_back_kernel, grid=(pieces,), in_specs=[fixed((tokens,...  58.7 us
    pallas_call x2, Pallas kernels, attend_back(): pl.pallas_call(attend_back_kernel, grid=(packs, HEADS // 2), in_specs=[pl...  55.4 us
    pallas_call x2, Pallas kernels, attend(): pl.pallas_call(attend_kernel, grid=(packs, HEADS // 2), in_specs=[pl.Bloc...  35.6 us
    pallas_call x1, Pallas kernels, exchange_slots(): pl.pallas_call(partial(slots_kernel, n_rep, n, to_slots), out_shape=jax.S...  34.3 us
    pallas_call x2, Pallas kernels, feed(): pl.pallas_call(feed_kernel, grid=(pieces,), in_specs=[fixed((tokens, widt...  25.1 us

profile of v4, /device:TPU:25, one launch (start us, length us, event | category | flops | bytes accessed | tf_op | source)
XLA Modules:
  0.0 685.7 jit_solution(10557802020646602876)
XLA Ops:
  0.6 1.5 select_reduce_fusion.2
  2.9 1.5 convert_reduce_fusion
  9.2 3.8 convert_element_type.51.x_ref
  13.6 101.3 %open_step.1 = (bf16[32,512,512]{2,1,0:T(8,128)(2,1)}, bf16[8,128,512]{2,1,0:T(8,128)(2,1)}, s32[8,1,128]{2,1,0:T(1,128)}, s32[8,8,128]{2,1,0:T(8,128)}, f32[8,8,128]{2,1,0:T(8,128)}, /*index=5*/s32[8,128]{1,0:T(8,128)}) custom-call(bf16[32,64,512]{2,1,0:T(8,128)(2,1)} %convert_element_type.51.x_ref, f32[3816,512]{1,0:T(8,128)} %t_ref.1, ...), custom_call_target="tpu_custom_call" | custom-call | tf_op jit(solution)/shard_map/open_step/pallas_call | solution.py:247
  116.8 2.5 fusion.21
  119.4 3.7 convert_element_type.52
  123.1 2.2 pad.20.e_ref
  126.7 1.7 multiply_multiply_fusion.2.x
  128.7 17.9 %attend.2 = (f32[1024,512]{1,0:T(8,128)S(1)}, bf16[1024,512]{1,0:T(8,128)(2,1)S(1)}, bf16[1024,1536]{1,0:T(8,128)(2,1)}, bf16[1024,512]{1,0:T(8,128)(2,1)S(1)}, f32[2,8,512]{2,1,0:T(8,128)S(1)}) custom-call(f32[8]{0:T(128)S(1)} %multiply_power_fusion.slopes, f32[1024,512]{1,0:T(8,128)} %multiply_multiply_fusion.2.x, f32[1,512]{1,0:T(1,128)S(1)} %slice.114.gain, ...), custom_call_target="tpu_custom_call" | custom-call | tf_op jit(solution)/shard_map/attend/pallas_call | solution.py:789
  149.3 12.9 %feed.2 = (f32[1024,512]{1,0:T(8,128)S(1)}, bf16[1024,512]{1,0:T(8,128)(2,1)S(1)}, bf16[4,1024,512]{2,1,0:T(8,128)(2,1)}, bf16[4,1024,512]{2,1,0:T(8,128)(2,1)}) custom-call(f32[1024,512]{1,0:T(8,128)S(1)} %get-tuple-element.209.x, f32[1,512]{1,0:T(1,128)S(1)} %slice.116.gain, bf16[32,512,512]{2,1,0:T(8,128)(2,1)} %get-tuple-element.208.w.wg.wu.wd, ...), custom_call_target="tpu_custom_call" | custom-call | tf_op jit(solution)/shard_map/feed/pallas_call | solution.py:993
  164.5 17.7 %attend.3 = (f32[1024,512]{1,0:T(8,128)S(1)}, bf16[1024,512]{1,0:T(8,128)(2,1)S(1)}, bf16[1024,1536]{1,0:T(8,128)(2,1)}, bf16[1024,512]{1,0:T(8,128)(2,1)S(1)}, f32[2,8,512]{2,1,0:T(8,128)S(1)}) custom-call(f32[8]{0:T(128)S(1)} %multiply_power_fusion.slopes, f32[1024,512]{1,0:T(8,128)} %copy-done.4, f32[1,512]{1,0:T(1,128)S(1)} %slice.118.gain, ...), custom_call_target="tpu_custom_call" | custom-call | tf_op jit(solution)/shard_map/attend/pallas_call | solution.py:789
  186.1 1.6 copy-done.3
  187.7 12.2 %feed.3 = (f32[1024,512]{1,0:T(8,128)S(1)}, bf16[1024,512]{1,0:T(8,128)(2,1)S(1)}, bf16[4,1024,512]{2,1,0:T(8,128)(2,1)}, bf16[4,1024,512]{2,1,0:T(8,128)(2,1)}) custom-call(f32[1024,512]{1,0:T(8,128)S(1)} %copy-done.3, f32[1,512]{1,0:T(1,128)S(1)} %slice.120.gain, bf16[32,512,512]{2,1,0:T(8,128)(2,1)} %get-tuple-element.208.w.wg.wu.wd, ...), custom_call_target="tpu_custom_call" | custom-call | tf_op jit(solution)/shard_map/feed/pallas_call | solution.py:993
  207.1 68.2 %head_step.1 = (f32[256,512]{1,0:T(8,128)}, f32[3840,512]{1,0:T(8,128)}, f32[8,128]{1,0:T(8,128)}) custom-call(bf16[256,512]{1,0:T(8,128)(2,1)} %select_convert_fusion.x_ref, bf16[3840,512]{1,0:T(8,128)(2,1)} %get-tuple-element.555, s32[8,256,1]{2,1,0:T(8,128)} %and_select_fusion.label_ref), custom_call_target="tpu_custom_call" | custom-call | tf_op jit(solution)/shard_map/head_step/pallas_call | solution.py:1345
  275.5 6.3 gather_fusion.2
  281.8 2.5 multiply_reduce_fusion
  285.7 1.5 broadcast_add_fusion.dx
  287.2 29.4 %feed_back.2 = (f32[1024,512]{1,0:T(8,128)}, f32[8,512]{1,0:T(8,128)}, bf16[4,512,512]{2,1,0:T(8,128)(2,1)}, bf16[4,512,512]{2,1,0:T(8,128)(2,1)}, bf16[4,512,512]{2,1,0:T(8,128)(2,1)}) custom-call(f32[1024,512]{1,0:T(8,128)} %broadcast_add_fusion.dx, f32[1024,512]{1,0:T(8,128)} %copy-done.2, f32[1,512]{1,0:T(1,128)} %copy-done.15, ...), custom_call_target="tpu_custom_call" | custom-call | tf_op jit(solution)/shard_map/feed_back/pallas_call | solution.py:1066
  316.6 27.6 %attend_back.2 = (f32[1024,512]{1,0:T(8,128)}, f32[2,8,512]{2,1,0:T(8,128)}, bf16[4,512,512]{2,1,0:T(8,128)(2,1)}) custom-call(f32[8]{0:T(128)} %copy-done.18, f32[1024,512]{1,0:T(8,128)} %get-tuple-element.218.dx, f32[1024,512]{1,0:T(8,128)} %copy-done.4, f32[1,512]{1,0:T(1,128)} %copy-done.17, bf16[32,512,512]{2,1,0:T(8,128)(2,1)} %get-tuple-element.208.w.wg.wu.wd, ...), custom_call_target="tpu_custom_call" | custom-call | tf_op jit(solution)/shard_map/attend_back/pallas_call | solution.py:907
  344.2 29.3 %feed_back.3 = (f32[1024,512]{1,0:T(8,128)}, f32[8,512]{1,0:T(8,128)}, bf16[4,512,512]{2,1,0:T(8,128)(2,1)}, bf16[4,512,512]{2,1,0:T(8,128)(2,1)}, bf16[4,512,512]{2,1,0:T(8,128)(2,1)}) custom-call(f32[1024,512]{1,0:T(8,128)} %get-tuple-element.223.dx, f32[1024,512]{1,0:T(8,128)} %copy-done.1, f32[1,512]{1,0:T(1,128)} %copy-done.14, ...), custom_call_target="tpu_custom_call" | custom-call | tf_op jit(solution)/shard_map/feed_back/pallas_call | solution.py:1066
  373.5 27.8 %attend_back.3 = (f32[1024,512]{1,0:T(8,128)}, f32[2,8,512]{2,1,0:T(8,128)}, bf16[4,512,512]{2,1,0:T(8,128)(2,1)}) custom-call(f32[8]{0:T(128)} %copy-done.18, f32[1024,512]{1,0:T(8,128)} %get-tuple-element.227.dx, f32[1024,512]{1,0:T(8,128)} %multiply_multiply_fusion.2.x, f32[1,512]{1,0:T(1,128)} %copy-done.16, ...), custom_call_target="tpu_custom_call" | custom-call | tf_op jit(solution)/shard_map/attend_back/pallas_call | solution.py:907
  401.3 2.3 multiply_reduce_fusion.1
  406.0 2.4 fusion.38
  409.0 2.2 fusion.26
  411.2 17.5 %group_7.1 = bf16[8,128,512]{2,1,0:T(8,128)(2,1)} custom-call(bf16[8,128,512]{2,1,0:T(8,128)(2,1)} %bitcast.109), custom_call_target="tpu_custom_call" | custom-call | tf_op jit(solution)/shard_map/group_7/pallas_call | solution.py:107
  428.8 8.9 %fusion.19 = f32[3840,512]{1,0:T(8,128)} fusion(f32[3840,512]{1,0:T(8,128)} %get-tuple-element.240, bf16[1024,512]{1,0:T(8,128)(2,1)} %bitcast.108, s32[1024]{0:T(1024)S(1)} %bitcast.126), kind=kOutput, calls=%fused_computation.38 | convolution fusion | flops 4032430080 | bytes 16781312 | tf_op jit(solution)/shard_map/dot_general | solution.py:1560
  439.6 147.2 %settle_gradients.1 = (bf16[6,8,4,16,512]{4,3,2,1,0:T(8,128)(2,1)}, f32[4,960,512]{2,1,0:T(8,128)}, f32[8,512]{1,0:T(8,128)}) custom-call(bf16[4,8,2,2,16,512]{5,4,3,2,1,0:T(8,128)(2,1)} %bitcast.105, bf16[4,8,2,2,16,512]{5,4,3,2,1,0:T(8,128)(2,1)} %bitcast.102, bf16[4,8,2,2,16,512]{5,4,3,2,1,0:T(8,128)(2,1)} %bitcast.103, ...), custom_call_target="tpu_custom_call" | custom-call | tf_op jit(solution)/shard_map/settle_gradients/pallas_call | solution.py:556
  591.6 21.8 %fusion.34 = (bf16[3816,512]{1,0:T(8,128)(2,1)}, f32[3816,512]{1,0:T(8,128)}, f32[3816,512]{1,0:T(8,128)}, f32[3816,512]{1,0:T(8,128)}) fusion(f32[3816,512]{1,0:T(8,128)} %t_ref.1, f32[]{:T(128)} %bitcast.38, f32[]{:T(128)} %bitcast.37, f32[3840,512]{1,0:T(8,128)} %bitcast.96, f32[]{:T(128)} %min.3, f32[3816,512]{1,0:T(8,128)} %param.35, f32[3816,512]{1,0:T(8,128)} %param.34), kind=kLoop, calls=%fused_computation.125 | loop fusion | flops 33214464 | bytes 58613772 | tf_op jit(solution)/shard_map/convert_element_type | solution.py:1658
  615.4 22.7 %turn_slots.1 = (f32[6,512,512]{2,1,0:T(8,128)}, f32[6,512,512]{2,1,0:T(8,128)}, bf16[8,6,16,512]{3,2,1,0:T(8,128)(2,1)}) custom-call(s32[7]{0:T(128)} %pad_add_fusion.scalars, f32[3]{0:T(128)} %pad_maximum_fusion.numbers, f32[6,512,512]{2,1,0:T(8,128)} %left.1, f32[6,512,512]{2,1,0:T(8,128)} %right.1, f32[6,8,4,16,512]{4,3,2,1,0:T(8,128)} %bitcast.93, ...), custom_call_target="tpu_custom_call" | custom-call | tf_op jit(solution)/shard_map/turn_slots/pallas_call | solution.py:1146
  638.2 34.3 %slots_11.1 = bf16[8,6,4,16,512]{4,3,2,1,0:T(8,128)(2,1)} custom-call(bf16[8,6,16,512]{3,2,1,0:T(8,128)(2,1)} %get-tuple-element.251.x_ref), custom_call_target="tpu_custom_call" | custom-call | tf_op jit(solution)/shard_map/slots_11/pallas_call | solution.py:662
  672.5 2.6 gather_fusion.3
  675.1 6.1 fusion.36
  (145 shorter events, 36.6 us)
Async XLA Ops:
  5.8 111.0 %copy-start.35 = (s32[1024]{0:T(1024)}, s32[1024]{0:T(1024)S(1)}, u32[]{:S(2)}) copy-start(s32[1024]{0:T(1024)S(1)} %get-tuple-element.381) | copy-start | bytes 12292
  9.2 3.8 copy-start.27
  116.8 2.5 copy-start.33
  125.3 1.4 copy-start.19
  125.3 0.8 copy-start.24
  126.7 1.7 copy-start.11
  128.4 18.1 %copy-start.16 = (f32[1,512]{1,0:T(1,128)}, f32[1,512]{1,0:T(1,128)S(1)}, u32[]{:S(2)}) copy-start(f32[1,512]{1,0:T(1,128)S(1)} %slice.114.gain) | copy-start | bytes 6148
  128.7 35.8 %copy-start = (s32[2,512,1]{2,1,0:T(8,128)}, s32[2,512,1]{2,1,0:T(8,128)S(1)}, u32[]{:S(2)}) copy-start(s32[2,512,1]{2,1,0:T(8,128)S(1)} %reshape_reshape.3.seg_col) | copy-start | bytes 12292
  128.7 35.8 %copy-start.18 = (f32[8]{0:T(128)}, f32[8]{0:T(128)S(1)}, u32[]{:S(2)}) copy-start(f32[8]{0:T(128)S(1)} %multiply_power_fusion.slopes) | copy-start | bytes 100
  146.6 1.1 copy-start.7
  147.6 1.0 copy-start.8
  149.2 13.0 %copy-start.1 = (f32[1024,512]{1,0:T(8,128)}, f32[1024,512]{1,0:T(8,128)S(1)}, u32[]{:S(2)}) copy-start(f32[1024,512]{1,0:T(8,128)S(1)} %get-tuple-element.209.x) | copy-start | bytes 6291460
  149.3 12.9 %copy-start.14 = (f32[1,512]{1,0:T(1,128)}, f32[1,512]{1,0:T(1,128)S(1)}, u32[]{:S(2)}) copy-start(f32[1,512]{1,0:T(1,128)S(1)} %slice.116.gain) | copy-start | bytes 6148
  162.1 1.3 copy-start.4
  163.4 1.0 copy-start.5
  164.5 17.7 %copy-start.17 = (f32[1,512]{1,0:T(1,128)}, f32[1,512]{1,0:T(1,128)S(1)}, u32[]{:S(2)}) copy-start(f32[1,512]{1,0:T(1,128)S(1)} %slice.118.gain) | copy-start | bytes 6148
  182.2 1.3 copy-start.2
  183.5 0.9 copy-start.9
  184.5 1.0 copy-start.10
  186.1 1.6 copy-start.3
  187.7 12.2 %copy-start.15 = (f32[1,512]{1,0:T(1,128)}, f32[1,512]{1,0:T(1,128)S(1)}, u32[]{:S(2)}) copy-start(f32[1,512]{1,0:T(1,128)S(1)} %slice.120.gain) | copy-start | bytes 6148
  199.9 1.0 copy-start.6
  281.8 2.6 copy-start.21
  373.5 27.8 %copy-start.20 = (f32[1024,512]{1,0:T(8,128)S(1)}, f32[1024,512]{1,0:T(8,128)}, u32[]{:S(2)}) copy-start(f32[1024,512]{1,0:T(8,128)} %copy-done.19) | copy-start | bytes 6291460
  401.3 2.4 copy-start.26
  401.3 2.4 copy-start.30
  401.3 2.4 copy-start.25
  401.3 2.4 copy-start.29
  405.9 2.4 copy-start.23
  591.6 21.8 %copy-start.28 = (f32[6,64]{1,0:T(8,128)S(1)}, f32[6,64]{1,0:T(8,128)}, u32[]{:S(2)}) copy-start(f32[6,64]{1,0:T(8,128)} %param.32) | copy-start | bytes 4612
  591.6 21.8 %copy-start.31 = (f32[6,64]{1,0:T(8,128)S(1)}, f32[6,64]{1,0:T(8,128)}, u32[]{:S(2)}) copy-start(f32[6,64]{1,0:T(8,128)} %param.37) | copy-start | bytes 4612
  591.6 21.8 %copy-start.32 = (f32[6,64]{1,0:T(8,128)S(1)}, f32[6,64]{1,0:T(8,128)}, u32[]{:S(2)}) copy-start(f32[6,64]{1,0:T(8,128)} %param.36) | copy-start | bytes 4612
  (5 other events, 3.2 us)

commit v5 on v4

--- a/solution.py
+++ b/solution.py
@@ -115,9 +115,50 @@
     )(x)
 
 
+def distinct(here, n, capacity, ids_row, ids_col, own_row, own_col, local_col, rank_ref, first_ref, ask):
+    tokens = ids_col.shape[0]
+    step = 128
+    lane = lax.broadcasted_iota(jnp.int32, (1, tokens), 1)
+
+    def rows_at(t):
+        return pl.ds(pl.multiple_of(t * step, step), step)
+
+    def place(t, width):
+        return t * step + lax.broadcasted_iota(jnp.int32, (step, width), 0)
+
+    def earliest(t, first):
+        same = ids_col[rows_at(t)] == ids_row[...]
+        return jnp.minimum(first, jnp.min(jnp.where(same, place(t, tokens), tokens), axis=0, keepdims=True))
+
+    first_row = lax.fori_loop(0, tokens // step, earliest, jnp.full((1, tokens), tokens, jnp.int32))
+    member = jnp.where(first_row == lane, own_row[...], -1)
+
+    def number(t, carry):
+        wanted, most = carry
+        at = rows_at(t)
+        same = ids_col[at] == ids_row[...]
+        first = jnp.min(jnp.where(same, lane, tokens), axis=1, keepdims=True)
+        ahead = (member == own_col[at]) & (lane < first)
+        rank = jnp.sum(jnp.where(ahead, 1, 0), axis=1, keepdims=True)
+        rank_ref[at] = rank
+        first_ref[at] = first
+        slot = jnp.where((first == place(t, 1)) & (rank < capacity), own_col[at] * capacity + rank, -1)
+        slots = lax.broadcasted_iota(jnp.int32, (1, n * capacity), 1)
+        wanted = wanted + jnp.sum(jnp.where(slot == slots, local_col[at], 0), axis=0, keepdims=True)
+        return wanted, jnp.maximum(most, jnp.max(rank, axis=0, keepdims=True))
+
+    start = (jnp.zeros((1, n * capacity), jnp.int32), jnp.zeros((1, 1), jnp.int32))
+    wanted, most = lax.fori_loop(0, tokens // step, number, start)
+    for o in range(n):
+        ask[o] = wanted[:, o * capacity : (o + 1) * capacity]
+    return most + 1
+
+
 def opening_kernel(
-    n_rep, n, half, shared, x_ref, t_ref, w_ref, facts_ref, gains_ref, o_ref, rows_ref, asked, facts, gains, most,
-    table, index, stage, ready, held, got,
+    n_rep, n, half, shared,
+    x_ref, t_ref, ids_row, ids_col, own_row, own_col, local_col, facts_ref, gains_ref,
+    o_ref, rows_ref, asked, facts, gains, most, rank_ref, first_ref, low_ref,
+    table, low, index, ask, fact, stage, ready, held, got,
     t_s, ring_s, ring_r, core_s, core_r, y_s, y_r, over_s, over_r, ask_s, ask_r, top_s, top_r, rows_s, rows_r,
 ):
     here = Place(n_rep, n)
@@ -125,18 +166,13 @@
     ypeer = (lax.rem(here.r + 2, 4), here.f)
     others = [lax.rem(me + k, n) for k in range(1, n)]
     rows = x_ref.shape[1]
+    part = rows // 2
     alone = (half - shared) // 2
     enter([(here.r, o) for o in others] + [here.core, ypeer])
-    load = pltpu.make_async_copy(t_ref, table, t_s.at[0])
+    vocab = t_ref.shape[0]
+    load = pltpu.make_async_copy(t_ref, table.at[pl.ds(0, vocab)], t_s.at[0])
     load.start()
-    asks = []
-    for k, o in enumerate(others):
-        peer = (here.r, o)
-        asks.append(remote(w_ref.at[o], asked.at[me], ask_s.at[0, k], ask_r.at[0, k], peer))
-        asks.append(remote(facts_ref, facts.at[me], ask_s.at[1, k], ask_r.at[1, k], peer))
-        asks.append(remote(gains_ref, gains.at[me], ask_s.at[2, k], ask_r.at[2, k], peer))
-    for cp in asks:
-        cp.start()
+    table[vocab:] = jnp.zeros((table.shape[0] - vocab, table.shape[1]), table.dtype)
 
     mine = pl.ds(here.c * half + here.y * alone, alone + shared)
     given = pl.ds(here.c * half + here.y * (alone + shared), alone)
@@ -144,44 +180,63 @@
     hops = n // 2
     copies, sends = [], []
 
-    def rows_of(origin, way, s):
-        if s == hops - 1:
-            return pl.ds(pl.multiple_of(origin * rows + way * (rows // 2), rows // 2), rows // 2)
-        return pl.ds(pl.multiple_of(origin * rows, rows), rows)
-
-    own = remote(x_ref, o_ref.at[:, rows_of(here.f, 0, -1)], core_s.at[0, 0], core_r.at[0, 0], here.core)
+    def rows_of(origin, lane):
+        return pl.ds(pl.multiple_of(origin * rows + lane * part, part), part)
+
+    own = remote(
+        x_ref, o_ref.at[:, pl.ds(pl.multiple_of(me * rows, rows), rows)], core_s.at[0, 0, 0], core_r.at[0, 0, 0], here.core
+    )
+    waiting = {}
+    across = []
+
+    def pass_on(way, s, lane):
+        waiting[way, s, lane].wait_recv()
+        where = rows_of(here.at(-s - 1 if way == 0 else s + 1), lane)
+        kept = o_ref.at[given, where]
+        cp = remote(kept, kept, y_s.at[way, s, lane], y_r.at[way, s, lane], ypeer)
+        cp.start()
+        across.append((cp, o_ref.at[taken, where], way, s, lane))
+        kept = o_ref.at[mine, where]
+        cp = remote(kept, kept, core_s.at[way, s + 1, lane], core_r.at[way, s + 1, lane], here.core)
+        cp.start()
+        copies.append(cp)
+
+    def hop(way, s, lane):
+        where = rows_of(here.at(-s if way == 0 else s), lane)
+        src = x_ref.at[mine, pl.ds(lane * part, part)] if s == 0 else o_ref.at[mine, where]
+        cp = remote(
+            src,
+            o_ref.at[mine, where],
+            ring_s.at[way, s, lane],
+            ring_r.at[way, s, lane],
+            here.next if way == 0 else here.prev,
+        )
+        cp.start()
+        waiting[way, s, lane] = cp
+        sends.append(cp)
+
+    for way in range(2):
+        hop(way, 0, way)
+    for way in range(2):
+        hop(way, 0, 1 - way)
     own.start()
     copies.append(own)
-    waiting = [None, None]
-    across = []
-
-    def pass_on(way, s):
-        waiting[way].wait_recv()
-        where = rows_of(here.at(-s - 1 if way == 0 else s + 1), way, s)
-        kept = o_ref.at[given, where]
-        cp = remote(kept, kept, y_s.at[way, s], y_r.at[way, s], ypeer)
+
+    count = distinct(
+        here, n, ask.shape[2], ids_row, ids_col, own_row, own_col, local_col, rank_ref, first_ref, ask
+    )
+    line = lax.broadcasted_iota(jnp.int32, fact.shape, 0)
+    fact[...] = jnp.where(line == fact.shape[0] - 1, count, facts_ref[...])
+    asks = []
+    for k, o in enumerate(others):
+        peer = (here.r, o)
+        asks.append(remote(ask.at[o], asked.at[me], ask_s.at[0, k], ask_r.at[0, k], peer))
+        asks.append(remote(fact, facts.at[me], ask_s.at[1, k], ask_r.at[1, k], peer))
+        asks.append(remote(gains_ref, gains.at[me], ask_s.at[2, k], ask_r.at[2, k], peer))
+    for cp in asks:
         cp.start()
-        across.append((cp, o_ref.at[taken, where], way, s))
-        kept = o_ref.at[mine, where]
-        cp = remote(kept, kept, core_s.at[way, s + 1], core_r.at[way, s + 1], here.core)
-        cp.start()
-        copies.append(cp)
-
-    def hop(way, s):
-        where = rows_of(here.at(-s if way == 0 else s), way, s)
-        src = x_ref.at[mine] if s == 0 else o_ref.at[mine, where]
-        cp = remote(
-            src, o_ref.at[mine, where], ring_s.at[way, s], ring_r.at[way, s], here.next if way == 0 else here.prev
-        )
-        cp.start()
-        waiting[way] = cp
-        sends.append(cp)
-
-    for way in range(2):
-        hop(way, 0)
-
-    asked[me] = w_ref[me]
-    facts[me] = facts_ref[...]
+    asked[me] = ask[me]
+    facts[me] = fact[...]
     gains[me] = gains_ref[...]
     for cp in asks:
         cp.wait_recv()
@@ -210,23 +265,43 @@
         cp = remote(ready.at[o], rows_ref.at[me], rows_s.at[k], rows_r.at[k], (here.r, o))
         cp.start()
         asks.append(cp)
+    for way in range(2):
+        pass_on(way, 0, way)
+        hop(way, 1, way)
+    for way in range(2):
+        pass_on(way, 0, 1 - way)
+        hop(way, 1, 1 - way)
     rows_ref[me] = collect(me)
     first.wait_recv()
     held[1] = jnp.maximum(top, got[0])
     second = remote(held.at[1], got.at[1], top_s.at[1], top_r.at[1], ypeer)
     second.start()
 
-    for s in range(1, hops):
+    step = 96
+
+    @pl.loop(0, table.shape[0] // step)
+    def _(i):
+        at = pl.ds(pl.multiple_of(i * step, step), step)
+        low[at] = table[at].astype(bf16)
+
+    put = pltpu.make_async_copy(low, low_ref, t_s.at[0])
+    put.start()
+
+    for s in range(2, hops):
         for way in range(2):
-            pass_on(way, s - 1)
-            hop(way, s)
+            pass_on(way, s - 1, way)
+            hop(way, s, way)
+        for way in range(2):
+            pass_on(way, s - 1, 1 - way)
+            if s < hops - 1:
+                hop(way, s, 1 - way)
     second.wait_recv()
     most[...] = jnp.maximum(held[1], got[1])
     for way in range(2):
-        pass_on(way, hops - 1)
-    for cp, kept, way, s in across:
+        pass_on(way, hops - 1, way)
+    for cp, kept, way, s, lane in across:
         cp.wait_recv()
-        over = remote(kept, kept, over_s.at[way, s], over_r.at[way, s], here.core)
+        over = remote(kept, kept, over_s.at[way, s, lane], over_r.at[way, s, lane], here.core)
         over.start()
         copies.append(over)
         sends.append(cp)
@@ -236,42 +311,53 @@
         cp.wait_send()
     for cp in copies:
         cp.wait()
-
-
-def open_step(mesh_sizes, cid, shard, table, wanted, facts, gains):
+    put.wait()
+
+
+def open_step(mesh_sizes, cid, shard, table, ids, owner, local, facts, gains, padded):
     n_rep, n = mesh_sizes
     count, rows, width = shard.shape
+    tokens = ids.shape[0]
     half = count // 2
-    places = wanted.shape[2]
+    hops = n // 2
     dma = pltpu.SemaphoreType.DMA
+    wanted = (n, 1, CAPACITY)
+    like = facts.shape
+    i32 = jnp.int32
     return pl.pallas_call(
         partial(opening_kernel, n_rep, n, half, half - 2 * (half // 3)),
         out_shape=[
             jax.ShapeDtypeStruct((count, rows * n, width), shard.dtype),
-            jax.ShapeDtypeStruct((n, places, width), bf16),
-            jax.ShapeDtypeStruct(wanted.shape, wanted.dtype),
-            jax.ShapeDtypeStruct((n,) + facts.shape, facts.dtype),
+            jax.ShapeDtypeStruct((n, CAPACITY, width), bf16),
+            jax.ShapeDtypeStruct(wanted, i32),
+            jax.ShapeDtypeStruct((n,) + like, i32),
             jax.ShapeDtypeStruct((n,) + gains.shape, gains.dtype),
-            jax.ShapeDtypeStruct(facts.shape, facts.dtype),
+            jax.ShapeDtypeStruct(like, i32),
+            jax.ShapeDtypeStruct((tokens, 1), i32),
+            jax.ShapeDtypeStruct((tokens, 1), i32),
+            jax.ShapeDtypeStruct((padded, width), bf16),
         ],
-        in_specs=[ANY, ANY] + [VMEM] * 3,
-        out_specs=[ANY] + [VMEM] * 5,
+        in_specs=[ANY, ANY] + [VMEM] * 7,
+        out_specs=[ANY] + [VMEM] * 7 + [ANY],
         scratch_shapes=[
-            pltpu.VMEM(table.shape, table.dtype),
-            pltpu.SMEM(wanted.shape, wanted.dtype),
-            pltpu.VMEM((places, width), table.dtype),
-            pltpu.VMEM((n, places, width), bf16),
-            pltpu.VMEM((2,) + facts.shape, facts.dtype),
-            pltpu.VMEM((2,) + facts.shape, facts.dtype),
+            pltpu.VMEM((padded, width), f32),
+            pltpu.VMEM((padded, width), bf16),
+            pltpu.SMEM(wanted, i32),
+            pltpu.VMEM(wanted, i32),
+            pltpu.VMEM(like, i32),
+            pltpu.VMEM((CAPACITY, width), f32),
+            pltpu.VMEM((n, CAPACITY, width), bf16),
+            pltpu.VMEM((2,) + like, i32),
+            pltpu.VMEM((2,) + like, i32),
             dma((2,)),
-            dma((2, n // 2)),
-            dma((2, n // 2)),
-            dma((2, n // 2 + 1)),
-            dma((2, n // 2 + 1)),
-            dma((2, n // 2)),
-            dma((2, n // 2)),
-            dma((2, n // 2)),
-            dma((2, n // 2)),
+            dma((2, hops, 2)),
+            dma((2, hops, 2)),
+            dma((2, hops + 1, 2)),
+            dma((2, hops + 1, 2)),
+            dma((2, hops, 2)),
+            dma((2, hops, 2)),
+            dma((2, hops, 2)),
+            dma((2, hops, 2)),
             dma((3, n - 1)),
             dma((3, n - 1)),
             dma((2,)),
@@ -281,7 +367,17 @@
         ],
         compiler_params=params(cid, 60 << 20),
         name="open_step",
-    )(shard, table, wanted, facts, gains)
+    )(
+        shard,
+        table,
+        ids.reshape(1, tokens),
+        ids.reshape(tokens, 1),
+        owner.reshape(1, tokens),
+        owner.reshape(tokens, 1),
+        local.reshape(tokens, 1),
+        facts,
+        gains,
+    )
 
 
 def squares_row(square):
@@ -1377,12 +1473,24 @@
         self.sizes = (n_rep, n_fsdp)
         self.kernels = n_rep == 4 and n_fsdp == 8 and shard_rows == 64
 
-    def open(self, cid, shard, table, wanted, facts, gains):
+    def open(self, cid, shard, table, ids, owner, local, facts, gains, padded):
         if self.kernels:
-            return open_step(self.sizes, cid, shard, table, wanted, facts, gains)
+            return open_step(self.sizes, cid, shard, table, ids, owner, local, facts, gains, padded)
+        tokens = ids.shape[0]
+        groups = self.sizes[1]
+        index = jnp.arange(tokens, dtype=jnp.int32)
+        first_at = jnp.min(jnp.where(ids[:, None] == ids[None, :], index[None, :], tokens), axis=1)
+        is_first = first_at == index
+        ahead = is_first[None, :] & (owner[:, None] == owner[None, :]) & (index[None, :] < first_at[:, None])
+        rank = jnp.sum(ahead.astype(jnp.int32), axis=1)
+        facts = facts.at[facts.shape[0] - 1].set(jnp.max(rank) + 1)
+        slot = jnp.where(is_first & (rank < CAPACITY), owner * CAPACITY + rank, -1)
+        slot_index = jnp.arange(groups * CAPACITY, dtype=jnp.int32)
+        wanted = jnp.sum(jnp.where(slot[None, :] == slot_index[:, None], local[None, :], 0), axis=1)
+        wanted = wanted.reshape(groups, 1, CAPACITY)
         asked = lax.all_to_all(wanted, "fsdp", split_axis=0, concat_axis=0, tiled=True)
-        rows = jnp.take(table.astype(bf16), asked.reshape(-1), axis=0)
-        rows = rows.reshape(wanted.shape[0], wanted.shape[2], table.shape[1])
+        low = jnp.pad(table.astype(bf16), ((0, padded - table.shape[0]), (0, 0)))
+        rows = jnp.take(low, asked.reshape(-1), axis=0).reshape(groups, CAPACITY, table.shape[1])
         return (
             lax.all_gather(shard, "fsdp", axis=1, tiled=True),
             self.spread(cid, rows),
@@ -1390,6 +1498,9 @@
             lax.all_gather(facts, "fsdp"),
             lax.all_gather(gains, "fsdp"),
             lax.pmax(facts, ("rep", "fsdp")),
+            rank,
+            first_at,
+            low,
         )
 
     def spread(self, cid, x):
@@ -1431,23 +1542,18 @@
     picks = micro_count * pick_count
     move = Transport(replicas, groups, shard_rows)
     padded_rows = -(-vocab_rows // 768) * 768
-    table_low = jnp.pad(embed.astype(bf16), ((0, padded_rows - vocab_rows), (0, 0)))
 
     ids = token_ids.reshape(tokens)
     index = jnp.arange(tokens, dtype=jnp.int32)
     owner = ids // vocab_rows
     local = ids - owner * vocab_rows
-    first_at = jnp.min(jnp.where(ids[:, None] == ids[None, :], index[None, :], tokens), axis=1)
-    is_first = first_at == index
-    ahead = is_first[None, :] & (owner[:, None] == owner[None, :]) & (index[None, :] < first_at[:, None])
-    rank = jnp.sum(ahead.astype(jnp.int32), axis=1)
-    most = jnp.max(rank) + 1
-
     my_labels = labels.reshape(picks // 128, 128)
-    facts = jnp.concatenate(
-        [my_labels, jnp.full((8 - picks // 128, 128), most, jnp.int32)], axis=0
+    facts = jnp.pad(my_labels, ((0, 8 - my_labels.shape[0]), (0, 0)))
+    gain_pad = jnp.pad(gains, ((0, 8 - gain_count), (0, 128 - gains.shape[1])))
+    full_blocks, rows, asked, group_facts, gain_rows, most_facts, rank, first_at, table_low = move.open(
+        0, blocks.astype(bf16), embed, ids, owner, local, facts, gain_pad, padded_rows
     )
-    gain_pad = jnp.pad(gains, ((0, 8 - gain_count), (0, 128 - gains.shape[1])))
+    rank, is_first = rank.reshape(tokens), first_at.reshape(tokens) == index
     slots = groups * CAPACITY
     most_rounds = (tokens + CAPACITY - 1) // CAPACITY
     slot_index = jnp.arange(slots, dtype=jnp.int32)
@@ -1465,9 +1571,6 @@
         return jnp.dot(chosen, rows.reshape(slots, model_width), preferred_element_type=f32)
 
     slot = slot_of(0)
-    full_blocks, rows, asked, group_facts, gain_rows, most_facts = move.open(
-        0, blocks.astype(bf16), embed, wanted_in(slot), facts, gain_pad
-    )
     rounds = (most_facts[7, 0] + CAPACITY - 1) // CAPACITY
     all_labels = group_facts[:, : picks // 128].reshape(groups * picks)
     gain_rows = gain_rows[:, :gain_count, : gains.shape[1]].transpose(1, 0, 2).reshape(gain_count, model_width)

time: 696 us -> 688 us (0.989)
    pallas_call x1, Pallas kernels: 68.2 us -> 75.8 us  [head_step(): pl.pallas_call(partial(head_kernel, n_rep, n, vocab, 768), out_shape=[jax...]
    pallas_call x1, Pallas kernels: 101 us -> 93.9 us  [open_step(): pl.pallas_call(partial(opening_kernel, n_rep, n, half, half - 2 * (half /...]
where the time goes in v5:
time: 688 us; the launch traced here: 679 us
  Pallas kernels  566 us (82%)
  other arithmetic  59.5 us (9%)
  local copies, waits for them, and re-layouts  31.8 us (5%)
  matrix products  13.7 us (2%)
  between operations  7.42 us (1%)
    pallas_call x1, Pallas kernels, settle_gradients(): pl.pallas_call(partial(reduce_kernel, n_rep, n, half, table_rows, each),...  147 us
    pallas_call x1, Pallas kernels, open_step(): pl.pallas_call(partial(opening_kernel, n_rep, n, half, half - 2 * (half /...  93.9 us
    pallas_call x1, Pallas kernels, head_step(): pl.pallas_call(partial(head_kernel, n_rep, n, vocab, 768), out_shape=[jax...  75.8 us
    pallas_call x2, Pallas kernels, feed_back(): pl.pallas_call(feed_back_kernel, grid=(pieces,), in_specs=[fixed((tokens,...  58.8 us
    pallas_call x2, Pallas kernels, attend_back(): pl.pallas_call(attend_back_kernel, grid=(packs, HEADS // 2), in_specs=[pl...  55.4 us
    pallas_call x2, Pallas kernels, attend(): pl.pallas_call(attend_kernel, grid=(packs, HEADS // 2), in_specs=[pl.Bloc...  35.5 us
    pallas_call x1, Pallas kernels, exchange_slots(): pl.pallas_call(partial(slots_kernel, n_rep, n, to_slots), out_shape=jax.S...  34.3 us
    pallas_call x2, Pallas kernels, feed(): pl.pallas_call(feed_kernel, grid=(pieces,), in_specs=[fixed((tokens, widt...  25.1 us

profile of v5, /device:TPU:25, one launch (start us, length us, event | category | flops | bytes accessed | tf_op | source)
XLA Modules:
  0.0 678.7 jit_solution(11719736240108957271)
XLA Ops:
  2.7 1.4 multiply_subtract_fusion.2
  4.7 3.8 convert_element_type.42.x_ref
  9.7 93.9 %open_step.1 = (bf16[32,512,512]{2,1,0:T(8,128)(2,1)}, bf16[8,128,512]{2,1,0:T(8,128)(2,1)}, s32[8,1,128]{2,1,0:T(1,128)}, s32[8,8,128]{2,1,0:T(8,128)}, f32[8,8...) custom-call(bf16[32,64,512]{2,1,0:T(8,128)(2,1)} %convert_element_ty, ...), custom_call_target="tpu_custom_call" | custom-call | tf_op jit(solution)/shard_map/open_step/pallas_call | solution.py:327
  105.5 1.7 fusion.33
  107.3 2.6 fusion.20
  112.1 1.7 multiply_multiply_fusion.2.x
  114.1 17.9 %attend.2 = (f32[1024,512]{1,0:T(8,128)S(1)}, bf16[1024,512]{1,0:T(8,128)(2,1)S(1)}, bf16[1024,1536]{1,0:T(8,128)(2,1)}, bf16[1024,512]{1,0:T(8,128)(2,1)S(1)}, f32[2,8,512]{2,1,0:T(8,128)S(1)}) custom-call(f32[8]{0:T(128)S(1)} %multiply_power_fusion.slopes, f32[1024,512]{1,0:T(8,128)} %multiply_multiply_fusion.2.x, f32[1,512]{1,0:T(1,128)S(1)} %slice.114.gain, ...), custom_call_target="tpu_custom_call" | custom-call | tf_op jit(solution)/shard_map/attend/pallas_call | solution.py:885
  134.6 12.9 %feed.2 = (f32[1024,512]{1,0:T(8,128)S(1)}, bf16[1024,512]{1,0:T(8,128)(2,1)S(1)}, bf16[4,1024,512]{2,1,0:T(8,128)(2,1)}, bf16[4,1024,512]{2,1,0:T(8,128)(2,1)}) custom-call(f32[1024,512]{1,0:T(8,128)S(1)} %get-tuple-element.215.x, f32[1,512]{1,0:T(1,128)S(1)} %slice.116.gain, bf16[32,512,512]{2,1,0:T(8,128)(2,1)} %get-tuple-element.214.w.wg.wu.wd, ...), custom_call_target="tpu_custom_call" | custom-call | tf_op jit(solution)/shard_map/feed/pallas_call | solution.py:1089
  149.9 17.7 %attend.3 = (f32[1024,512]{1,0:T(8,128)S(1)}, bf16[1024,512]{1,0:T(8,128)(2,1)S(1)}, bf16[1024,1536]{1,0:T(8,128)(2,1)}, bf16[1024,512]{1,0:T(8,128)(2,1)S(1)}, f32[2,8,512]{2,1,0:T(8,128)S(1)}) custom-call(f32[8]{0:T(128)S(1)} %multiply_power_fusion.slopes, f32[1024,512]{1,0:T(8,128)} %copy-done.4, f32[1,512]{1,0:T(1,128)S(1)} %slice.118.gain, ...), custom_call_target="tpu_custom_call" | custom-call | tf_op jit(solution)/shard_map/attend/pallas_call | solution.py:885
  167.6 1.3 copy-done.2
  171.5 1.6 copy-done.3
  173.1 12.2 %feed.3 = (f32[1024,512]{1,0:T(8,128)S(1)}, bf16[1024,512]{1,0:T(8,128)(2,1)S(1)}, bf16[4,1024,512]{2,1,0:T(8,128)(2,1)}, bf16[4,1024,512]{2,1,0:T(8,128)(2,1)}) custom-call(f32[1024,512]{1,0:T(8,128)S(1)} %copy-done.3, f32[1,512]{1,0:T(1,128)S(1)} %slice.120.gain, bf16[32,512,512]{2,1,0:T(8,128)(2,1)} %get-tuple-element.214.w.wg.wu.wd, ...), custom_call_target="tpu_custom_call" | custom-call | tf_op jit(solution)/shard_map/feed/pallas_call | solution.py:1089
  192.6 75.8 %head_step.1 = (f32[256,512]{1,0:T(8,128)}, f32[3840,512]{1,0:T(8,128)}, f32[8,128]{1,0:T(8,128)}) custom-call(bf16[256,512]{1,0:T(8,128)(2,1)} %select_convert_fusion.x_ref, bf16[3840,512]{1,0:T(8,128)(2,1)} %get-tuple-element.565, s32[8,256,1]{2,1,0:T(8,128)} %and_select_fusion.label_ref), custom_call_target="tpu_custom_call" | custom-call | tf_op jit(solution)/shard_map/head_step/pallas_call | solution.py:1441
  268.6 6.4 gather_fusion.2
  275.0 2.5 multiply_reduce_fusion
  278.8 1.5 broadcast_add_fusion.dx
  280.4 29.5 %feed_back.2 = (f32[1024,512]{1,0:T(8,128)}, f32[8,512]{1,0:T(8,128)}, bf16[4,512,512]{2,1,0:T(8,128)(2,1)}, bf16[4,512,512]{2,1,0:T(8,128)(2,1)}, bf16[4,512,512]{2,1,0:T(8,128)(2,1)}) custom-call(f32[1024,512]{1,0:T(8,128)} %broadcast_add_fusion.dx, f32[1024,512]{1,0:T(8,128)} %copy-done.2, f32[1,512]{1,0:T(1,128)} %copy-done.15, ...), custom_call_target="tpu_custom_call" | custom-call | tf_op jit(solution)/shard_map/feed_back/pallas_call | solution.py:1162
  309.9 27.6 %attend_back.2 = (f32[1024,512]{1,0:T(8,128)}, f32[2,8,512]{2,1,0:T(8,128)}, bf16[4,512,512]{2,1,0:T(8,128)(2,1)}) custom-call(f32[8]{0:T(128)} %copy-done.18, f32[1024,512]{1,0:T(8,128)} %get-tuple-element.224.dx, f32[1024,512]{1,0:T(8,128)} %copy-done.4, f32[1,512]{1,0:T(1,128)} %copy-done.17, bf16[32,512,512]{2,1,0:T(8,128)(2,1)} %get-tuple-element.214.w.wg.wu.wd, ...), custom_call_target="tpu_custom_call" | custom-call | tf_op jit(solution)/shard_map/attend_back/pallas_call | solution.py:1003
  337.5 29.3 %feed_back.3 = (f32[1024,512]{1,0:T(8,128)}, f32[8,512]{1,0:T(8,128)}, bf16[4,512,512]{2,1,0:T(8,128)(2,1)}, bf16[4,512,512]{2,1,0:T(8,128)(2,1)}, bf16[4,512,512]{2,1,0:T(8,128)(2,1)}) custom-call(f32[1024,512]{1,0:T(8,128)} %get-tuple-element.229.dx, f32[1024,512]{1,0:T(8,128)} %copy-done.1, f32[1,512]{1,0:T(1,128)} %copy-done.14, ...), custom_call_target="tpu_custom_call" | custom-call | tf_op jit(solution)/shard_map/feed_back/pallas_call | solution.py:1162
  366.8 27.7 %attend_back.3 = (f32[1024,512]{1,0:T(8,128)}, f32[2,8,512]{2,1,0:T(8,128)}, bf16[4,512,512]{2,1,0:T(8,128)(2,1)}) custom-call(f32[8]{0:T(128)} %copy-done.18, f32[1024,512]{1,0:T(8,128)} %get-tuple-element.233.dx, f32[1024,512]{1,0:T(8,128)} %multiply_multiply_fusion.2.x, f32[1,512]{1,0:T(1,128)} %copy-done.16, ...), custom_call_target="tpu_custom_call" | custom-call | tf_op jit(solution)/shard_map/attend_back/pallas_call | solution.py:1003
  394.6 2.3 multiply_reduce_fusion.1
  399.2 2.4 fusion.38
  402.3 2.2 fusion.24
  404.5 17.6 %group_7.1 = bf16[8,128,512]{2,1,0:T(8,128)(2,1)} custom-call(bf16[8,128,512]{2,1,0:T(8,128)(2,1)} %bitcast.110), custom_call_target="tpu_custom_call" | custom-call | tf_op jit(solution)/shard_map/group_7/pallas_call | solution.py:107
  422.1 8.8 %fusion.19 = f32[3840,512]{1,0:T(8,128)} fusion(f32[3840,512]{1,0:T(8,128)} %get-tuple-element.246, bf16[1024,512]{1,0:T(8,128)(2,1)} %bitcast.109, s32[1024]{0:T(1024)S(1)} %bitcast.128), kind=kOutput, calls=%fused_computation.38 | convolution fusion | flops 4032430080 | bytes 16781312 | tf_op jit(solution)/shard_map/dot_general | solution.py:1663
  432.9 147.0 %settle_gradients.1 = (bf16[6,8,4,16,512]{4,3,2,1,0:T(8,128)(2,1)}, f32[4,960,512]{2,1,0:T(8,128)}, f32[8,512]{1,0:T(8,128)}) custom-call(bf16[4,8,2,2,16,512]{5,4,3,2,1,0:T(8,128)(2,1)} %bitcast.106, bf16[4,8,2,2,16,512]{5,4,3,2,1,0:T(8,128)(2,1)} %bitcast.103, bf16[4,8,2,2,16,512]{5,4,3,2,1,0:T(8,128)(2,1)} %bitcast.104, ...), custom_call_target="tpu_custom_call" | custom-call | tf_op jit(solution)/shard_map/settle_gradients/pallas_call | solution.py:652
  579.9 1.3 fusion.40
  584.7 21.8 %fusion.34 = (bf16[3816,512]{1,0:T(8,128)(2,1)}, f32[3816,512]{1,0:T(8,128)}, f32[3816,512]{1,0:T(8,128)}, f32[3816,512]{1,0:T(8,128)}) fusion(f32[3816,512]{1,0:T(8,128)} %t_ref.1, f32[]{:T(128)} %bitcast.39, f32[]{:T(128)} %bitcast.38, f32[3840,512]{1,0:T(8,128)} %bitcast.97, f32[]{:T(128)} %min.3, f32[3816,512]{1,0:T(8,128)} %param.35, f32[3816,512]{1,0:T(8,128)} %param.34), kind=kLoop, calls=%fused_computation.126 | loop fusion | flops 33214464 | bytes 58613772 | tf_op jit(solution)/shard_map/convert_element_type | solution.py:1761
  608.5 22.7 %turn_slots.1 = (f32[6,512,512]{2,1,0:T(8,128)}, f32[6,512,512]{2,1,0:T(8,128)}, bf16[8,6,16,512]{3,2,1,0:T(8,128)(2,1)}) custom-call(s32[7]{0:T(128)} %pad_add_fusion.scalars, f32[3]{0:T(128)} %pad_maximum_fusion.numbers, f32[6,512,512]{2,1,0:T(8,128)} %left.1, f32[6,512,512]{2,1,0:T(8,128)} %right.1, f32[6,8,4,16,512]{4,3,2,1,0:T(8,128)} %bitcast.94, ...), custom_call_target="tpu_custom_call" | custom-call | tf_op jit(solution)/shard_map/turn_slots/pallas_call | solution.py:1242
  631.2 34.3 %slots_11.1 = bf16[8,6,4,16,512]{4,3,2,1,0:T(8,128)(2,1)} custom-call(bf16[8,6,16,512]{3,2,1,0:T(8,128)(2,1)} %get-tuple-element.257.x_ref), custom_call_target="tpu_custom_call" | custom-call | tf_op jit(solution)/shard_map/slots_11/pallas_call | solution.py:758
  665.5 2.6 gather_fusion.3
  668.1 6.1 fusion.36
  (156 shorter events, 33.2 us)
Async XLA Ops:
  0.6 3.4 copy-start.26
  1.6 6.9 %copy-start.22 = (s32[1024,1]{1,0:T(8,128)}, s32[1024,1]{1,0:T(8,128)S(1)}, u32[]{:S(2)}) copy-start(s32[1024,1]{1,0:T(8,128)S(1)} %copy.59.ids_col) | copy-start | bytes 12292
  4.7 3.9 copy-start.41
  4.7 4.5 copy-start.32
  9.7 95.8 %copy-start.23 = (s32[1024,1]{1,0:T(8,128)S(1)}, s32[1024,1]{1,0:T(8,128)}, u32[]{:S(2)}) copy-start(s32[1024,1]{1,0:T(8,128)} %copy-done.22) | copy-start | bytes 12292
  107.3 2.6 copy-start.27
  107.3 3.2 copy-start.39
  107.3 3.2 copy-start.25
  110.8 1.4 copy-start.19
  112.1 1.7 copy-start.11
  113.9 18.1 %copy-start.16 = (f32[1,512]{1,0:T(1,128)}, f32[1,512]{1,0:T(1,128)S(1)}, u32[]{:S(2)}) copy-start(f32[1,512]{1,0:T(1,128)S(1)} %slice.114.gain) | copy-start | bytes 6148
  114.1 35.8 %copy-start = (s32[2,512,1]{2,1,0:T(8,128)}, s32[2,512,1]{2,1,0:T(8,128)S(1)}, u32[]{:S(2)}) copy-start(s32[2,512,1]{2,1,0:T(8,128)S(1)} %reshape_reshape.16.seg_col) | copy-start | bytes 12292
  114.1 35.8 %copy-start.18 = (f32[8]{0:T(128)}, f32[8]{0:T(128)S(1)}, u32[]{:S(2)}) copy-start(f32[8]{0:T(128)S(1)} %multiply_power_fusion.slopes) | copy-start | bytes 100
  134.5 13.0 %copy-start.1 = (f32[1024,512]{1,0:T(8,128)}, f32[1024,512]{1,0:T(8,128)S(1)}, u32[]{:S(2)}) copy-start(f32[1024,512]{1,0:T(8,128)S(1)} %get-tuple-element.215.x) | copy-start | bytes 6291460
  134.6 12.9 %copy-start.14 = (f32[1,512]{1,0:T(1,128)}, f32[1,512]{1,0:T(1,128)S(1)}, u32[]{:S(2)}) copy-start(f32[1,512]{1,0:T(1,128)S(1)} %slice.116.gain) | copy-start | bytes 6148
  147.5 1.3 copy-start.4
  149.9 17.7 %copy-start.17 = (f32[1,512]{1,0:T(1,128)}, f32[1,512]{1,0:T(1,128)S(1)}, u32[]{:S(2)}) copy-start(f32[1,512]{1,0:T(1,128)S(1)} %slice.118.gain) | copy-start | bytes 6148
  167.6 1.3 copy-start.2
  169.9 1.0 copy-start.10
  171.5 1.6 copy-start.3
  173.1 12.2 %copy-start.15 = (f32[1,512]{1,0:T(1,128)}, f32[1,512]{1,0:T(1,128)S(1)}, u32[]{:S(2)}) copy-start(f32[1,512]{1,0:T(1,128)S(1)} %slice.120.gain) | copy-start | bytes 6148
  185.3 1.0 copy-start.6
  275.0 2.5 copy-start.21
  366.8 27.8 %copy-start.20 = (f32[1024,512]{1,0:T(8,128)S(1)}, f32[1024,512]{1,0:T(8,128)}, u32[]{:S(2)}) copy-start(f32[1024,512]{1,0:T(8,128)} %copy-done.19) | copy-start | bytes 6291460
  394.6 2.4 copy-start.31
  394.6 2.4 copy-start.35
  394.6 2.4 copy-start.30
  394.6 2.4 copy-start.34
  399.2 2.4 copy-start.28
  584.6 21.8 %copy-start.33 = (f32[6,64]{1,0:T(8,128)S(1)}, f32[6,64]{1,0:T(8,128)}, u32[]{:S(2)}) copy-start(f32[6,64]{1,0:T(8,128)} %param.32) | copy-start | bytes 4612
  584.7 21.8 %copy-start.36 = (f32[6,64]{1,0:T(8,128)S(1)}, f32[6,64]{1,0:T(8,128)}, u32[]{:S(2)}) copy-start(f32[6,64]{1,0:T(8,128)} %param.37) | copy-start | bytes 4612
  584.7 21.8 %copy-start.37 = (f32[6,64]{1,0:T(8,128)S(1)}, f32[6,64]{1,0:T(8,128)}, u32[]{:S(2)}) copy-start(f32[6,64]{1,0:T(8,128)} %param.36) | copy-start | bytes 4612
  (10 other events, 7.9 us)

commit v6 on v5

--- a/solution.py
+++ b/solution.py
@@ -703,67 +703,162 @@
     )(*views, table, small, block_of, taken)
 
 
-def slots_kernel(n_rep, n, to_slots, x_ref, o_ref, keep, a_s, a_r, f_s, f_r):
+def return_kernel(
+    n_rep, n, vocab, x_ref, numbers, g_ref, e_ref, m_ref, v_ref, o_ref, e_new, m_new, v_new, low_new,
+    fetched, made, made_low, keep, a_s, a_r, f_s, f_r, in_s, out_s,
+):
     here = Place(n_rep, n)
     ypeer = (lax.rem(here.r + 2, 4), here.f)
     me = here.f
     others = [lax.rem(me + k, n) for k in range(1, n)]
+    chunk = fetched.shape[2]
+    strip = 48
+    chunks = -(-vocab // chunk)
+
+    def extent(t):
+        return min(chunk, vocab - t * chunk)
+
+    def fetch(t):
+        spot, size = t % 2, extent(t)
+        loads = [
+            pltpu.make_async_copy(
+                ref.at[pl.ds(t * chunk, size)], fetched.at[spot, k, pl.ds(0, size)], in_s.at[spot, k]
+            )
+            for k, ref in enumerate((g_ref, e_ref, m_ref, v_ref))
+        ]
+        for ld in loads:
+            ld.start()
+        return loads
+
+    def store(t):
+        spot, size = t % 2, extent(t)
+        puts = [
+            pltpu.make_async_copy(
+                made.at[spot, k, pl.ds(0, size)], ref.at[pl.ds(t * chunk, size)], out_s.at[spot, k]
+            )
+            for k, ref in enumerate((e_new, m_new, v_new))
+        ]
+        puts.append(
+            pltpu.make_async_copy(
+                made_low.at[spot, pl.ds(0, size)], low_new.at[pl.ds(t * chunk, size)], out_s.at[spot, 3]
+            )
+        )
+        for cp in puts:
+            cp.start()
+        return puts
+
+    loads = {t: fetch(t) for t in range(min(2, chunks))}
     enter([(here.r, o) for o in others] + [here.core, ypeer])
 
-    def spot(source, r):
-        return o_ref.at[:, source, r] if to_slots else o_ref.at[source, :, r]
+    def piece(source, r):
+        return o_ref.at[source, :, r]
 
     copies = []
     for k, o in enumerate(others):
-        cp = remote(x_ref.at[o], spot(me, here.r), a_s.at[k], a_r.at[k], (here.r, o))
+        cp = remote(x_ref.at[o], piece(me, here.r), a_s.at[k], a_r.at[k], (here.r, o))
         cp.start()
         copies.append(cp)
-    own = pltpu.make_async_copy(x_ref.at[me], spot(me, here.r), keep)
+    own = pltpu.make_async_copy(x_ref.at[me], piece(me, here.r), keep)
     own.start()
     sends, far = [], []
-    for k in range(n):
-        source = me if k == 0 else lax.rem(me - k + n, n)
+    yr = lax.rem(here.r + 2, 4)
+
+    def source_of(k):
+        return me if k == 0 else lax.rem(me - k + n, n)
+
+    def forward(k):
         if k == 0:
             own.wait()
         else:
             copies[k - 1].wait_recv()
-        held = spot(source, here.r)
+        held = piece(source_of(k), here.r)
         over = remote(held, held, f_s.at[0, k], f_r.at[0, k], ypeer)
         over.start()
         beside = remote(held, held, f_s.at[1, k], f_r.at[1, k], here.core)
         beside.start()
-        far.append((over, source))
+        far.append(over)
         sends.append(beside)
-    yr = lax.rem(here.r + 2, 4)
-    for k, (over, source) in enumerate(far):
-        over.wait_recv()
-        src = me if k == 0 else lax.rem(me - k + n, n)
-        held = spot(src, yr)
+
+    def finish(k):
+        far[k].wait_recv()
+        held = piece(source_of(k), yr)
         beside = remote(held, held, f_s.at[2, k], f_r.at[2, k], here.core)
         beside.start()
         sends.append(beside)
-    for cp in copies:
+
+    factor, first_scale, second_scale = numbers[0], numbers[1], numbers[2]
+    puts = {}
+    lag = 5
+    for t in range(chunks):
+        spot = t % 2
+        for ld in loads[t]:
+            ld.wait()
+        if t >= 2:
+            for cp in puts[t - 2]:
+                cp.wait()
+
+        @pl.loop(0, -(-extent(t) // strip))
+        def _(i, spot=spot):
+            at = pl.ds(pl.multiple_of(i * strip, strip), strip)
+            grad = factor * fetched[spot, 0, at]
+            old = fetched[spot, 1, at]
+            moment = beta_first * fetched[spot, 2, at] + (1.0 - beta_first) * grad
+            second = beta_second * fetched[spot, 3, at] + (1.0 - beta_second) * grad * grad
+            step = moment * first_scale / (jnp.sqrt(second * second_scale) + adam_epsilon)
+            value = old - step_rate * (step + weight_decay * old)
+            made[spot, 0, at] = value
+            made[spot, 1, at] = moment
+            made[spot, 2, at] = second
+            made_low[spot, at] = value.astype(bf16)
+
+        puts[t] = store(t)
+        if t + 2 < chunks:
+            loads[t + 2] = fetch(t + 2)
+        if t < n:
+            forward(t)
+        if lag <= t < n + lag:
+            finish(t - lag)
+    for k in range(chunks, n):
+        forward(k)
+    for k in range(max(0, chunks - lag), n):
+        finish(k)
+    for t in range(max(0, chunks - 2), chunks):
+        for cp in puts[t]:
+            cp.wait()
+    for cp in copies + far:
         cp.wait_send()
-    for over, _ in far:
-        over.wait_send()
     for cp in sends:
         cp.wait()
 
 
-def exchange_slots(mesh_sizes, cid, x, to_slots):
+def return_slots(mesh_sizes, cid, x, numbers, grad_table, embed, embed_m, embed_v):
     n_rep, n = mesh_sizes
     _, cap, rows, width = x.shape
-    shape = (cap, n, 4, rows, width) if to_slots else (n, cap, 4, rows, width)
+    vocab = embed.shape[0]
+    chunk = 432
     dma = pltpu.SemaphoreType.DMA
     return pl.pallas_call(
-        partial(slots_kernel, n_rep, n, to_slots),
-        out_shape=jax.ShapeDtypeStruct(shape, x.dtype),
-        in_specs=[VMEM],
-        out_specs=ANY,
-        scratch_shapes=[dma, dma((n - 1,)), dma((n - 1,)), dma((3, n)), dma((3, n))],
-        compiler_params=params(cid),
-        name=f"slots_{cid}",
-    )(x)
+        partial(return_kernel, n_rep, n, vocab),
+        out_shape=[jax.ShapeDtypeStruct((n, cap, 4, rows, width), x.dtype)]
+        + [jax.ShapeDtypeStruct(embed.shape, f32)] * 3
+        + [jax.ShapeDtypeStruct(embed.shape, bf16)],
+        in_specs=[VMEM, pl.BlockSpec(memory_space=pltpu.SMEM)] + [ANY] * 4,
+        out_specs=[ANY] * 5,
+        scratch_shapes=[
+            pltpu.VMEM((2, 4, chunk, width), f32),
+            pltpu.VMEM((2, 3, chunk, width), f32),
+            pltpu.VMEM((2, chunk, width), bf16),
+            dma,
+            dma((n - 1,)),
+            dma((n - 1,)),
+            dma((3, n)),
+            dma((3, n)),
+            dma((2, 4)),
+            dma((2, 4)),
+        ],
+        compiler_params=params(cid, 48 << 20),
+        name="return_slots",
+    )(x, numbers, grad_table, embed, embed_m, embed_v)
 
 
 def layer_norm(inputs, gain_row):
@@ -1693,7 +1788,7 @@
             taken.astype(jnp.int32),
             slot_cap,
         )
-        grad_table = grad_table.reshape(padded_rows, model_width)[:vocab_rows]
+        grad_table = grad_table.reshape(padded_rows, model_width)
         squares = jnp.sum(small[6])
         owned = owned.reshape(slot_cap, model_width, model_width)
     else:
@@ -1722,7 +1817,16 @@
             soap_m,
             soap_v,
         )
-        returned = exchange_slots(move.sizes, 11, turned, False)
+        returned, embed_new, embed_m_new, embed_v_new, embed_new_low = return_slots(
+            move.sizes,
+            11,
+            turned,
+            jnp.stack([factor, 1.0 / first_fix, 1.0 / second_fix]),
+            grad_table,
+            embed,
+            embed_m,
+            embed_v,
+        )
         returned = returned.reshape(slot_total, shard_rows, model_width)
     else:
         rotated = jnp.einsum("bji,bjk->bik", left_basis, owned, precision=high)
@@ -1733,13 +1837,14 @@
         turned = jnp.einsum("bij,bjk->bik", left_basis, rotated_step, precision=high)
         turned = jnp.einsum("bik,blk->bil", turned, right_basis, precision=high)
         returned = lax.all_to_all(turned, "fsdp", split_axis=1, concat_axis=0, tiled=True)
+        embed_m_new, embed_v_new, table_step = adam_moments(
+            embed_m, embed_v, factor * grad_table, first_fix, second_fix
+        )
+        embed_new = embed - step_rate * (table_step + weight_decay * embed)
+        embed_new_low = embed_new.astype(bf16)
     update = jnp.take(returned, block_slots, axis=0).astype(f32)
     blocks_new = blocks - step_rate * (update + weight_decay * blocks)
 
-    embed_m_new, embed_v_new, table_step = adam_moments(
-        embed_m, embed_v, factor * grad_table, first_fix, second_fix
-    )
-    embed_new = embed - step_rate * (table_step + weight_decay * embed)
     gains_m_new, gains_v_new, gain_step = adam_moments(
         gains_m, gains_v, factor * grad_gains, first_fix, second_fix
     )
@@ -1758,7 +1863,7 @@
         soap_m_new,
         soap_v_new,
         blocks_new.astype(bf16),
-        embed_new.astype(bf16),
+        embed_new_low,
     )
 
 

time: 688 us -> 684 us (level)
  other arithmetic: 59.5 us -> 38.9 us
  local copies, waits for them, and re-layouts: 31.8 us -> 49.4 us
    convert_element_type x1 -> x0, other arithmetic: 21.8 us -> none  [body(): embed_new.astype(bf16)]
    unnamed x84 -> x102, local copies, waits for them, and re-layouts: 13 us -> 31 us
where the time goes in v6:
time: 684 us; the launch traced here: 675 us
  Pallas kernels  565 us (83%)
  local copies, waits for them, and re-layouts  49.4 us (7%)
  other arithmetic  38.9 us (6%)
  matrix products  13.7 us (2%)
  between operations  7.58 us (1%)
    pallas_call x1, Pallas kernels, settle_gradients(): pl.pallas_call(partial(reduce_kernel, n_rep, n, half, table_rows, each),...  147 us
    pallas_call x1, Pallas kernels, open_step(): pl.pallas_call(partial(opening_kernel, n_rep, n, half, half - 2 * (half /...  93.9 us
    pallas_call x1, Pallas kernels, head_step(): pl.pallas_call(partial(head_kernel, n_rep, n, vocab, 768), out_shape=[jax...  75.8 us
    pallas_call x2, Pallas kernels, feed_back(): pl.pallas_call(feed_back_kernel, grid=(pieces,), in_specs=[fixed((tokens,...  58.6 us
    pallas_call x2, Pallas kernels, attend_back(): pl.pallas_call(attend_back_kernel, grid=(packs, HEADS // 2), in_specs=[pl...  55.4 us
    pallas_call x2, Pallas kernels, attend(): pl.pallas_call(attend_kernel, grid=(packs, HEADS // 2), in_specs=[pl.Bloc...  35.6 us
    pallas_call x1, Pallas kernels, return_slots(): pl.pallas_call(partial(return_kernel, n_rep, n, vocab), out_shape=[jax.Sh...  33.5 us
    unnamed x102, local copies, waits for them, and re-layouts  31 us

profile of v6, /device:TPU:25, one launch (start us, length us, event | category | flops | bytes accessed | tf_op | source)
XLA Modules:
  0.0 675.1 jit_solution(4886805325152603456)
XLA Ops:
  4.7 3.8 convert_element_type.39.x_ref
  9.7 93.9 %open_step.1 = (bf16[32,512,512]{2,1,0:T(8,128)(2,1)}, bf16[8,128,512]{2,1,0:T(8,128)(2,1)}, s32[8,1,128]{2,1,0:T(1,128)}, s32[8,8,128]{2,1,0:T(8,128)}, f32[8,8...) custom-call(bf16[32,64,512]{2,1,0:T(8,128)(2,1)} %convert_element_ty, ...), custom_call_target="tpu_custom_call" | custom-call | tf_op jit(solution)/shard_map/open_step/pallas_call | solution.py:327
  105.5 1.7 fusion.32
  107.3 2.6 fusion.19
  112.1 1.7 multiply_multiply_fusion.1.x
  114.1 17.9 %attend.2 = (f32[1024,512]{1,0:T(8,128)S(1)}, bf16[1024,512]{1,0:T(8,128)(2,1)S(1)}, bf16[1024,1536]{1,0:T(8,128)(2,1)}, bf16[1024,512]{1,0:T(8,128)(2,1)S(1)}, f32[2,8,512]{2,1,0:T(8,128)S(1)}) custom-call(f32[8]{0:T(128)S(1)} %multiply_power_fusion.slopes, f32[1024,512]{1,0:T(8,128)} %multiply_multiply_fusion.1.x, f32[1,512]{1,0:T(1,128)S(1)} %slice.111.gain, ...), custom_call_target="tpu_custom_call" | custom-call | tf_op jit(solution)/shard_map/attend/pallas_call | solution.py:980
  134.7 12.9 %feed.2 = (f32[1024,512]{1,0:T(8,128)S(1)}, bf16[1024,512]{1,0:T(8,128)(2,1)S(1)}, bf16[4,1024,512]{2,1,0:T(8,128)(2,1)}, bf16[4,1024,512]{2,1,0:T(8,128)(2,1)}) custom-call(f32[1024,512]{1,0:T(8,128)S(1)} %get-tuple-element.220.x, f32[1,512]{1,0:T(1,128)S(1)} %slice.113.gain, bf16[32,512,512]{2,1,0:T(8,128)(2,1)} %get-tuple-element.219.w.wg.wu.wd, ...), custom_call_target="tpu_custom_call" | custom-call | tf_op jit(solution)/shard_map/feed/pallas_call | solution.py:1184
  149.9 17.7 %attend.3 = (f32[1024,512]{1,0:T(8,128)S(1)}, bf16[1024,512]{1,0:T(8,128)(2,1)S(1)}, bf16[1024,1536]{1,0:T(8,128)(2,1)}, bf16[1024,512]{1,0:T(8,128)(2,1)S(1)}, f32[2,8,512]{2,1,0:T(8,128)S(1)}) custom-call(f32[8]{0:T(128)S(1)} %multiply_power_fusion.slopes, f32[1024,512]{1,0:T(8,128)} %copy-done.4, f32[1,512]{1,0:T(1,128)S(1)} %slice.115.gain, ...), custom_call_target="tpu_custom_call" | custom-call | tf_op jit(solution)/shard_map/attend/pallas_call | solution.py:980
  171.6 1.6 copy-done.3
  173.2 12.2 %feed.3 = (f32[1024,512]{1,0:T(8,128)S(1)}, bf16[1024,512]{1,0:T(8,128)(2,1)S(1)}, bf16[4,1024,512]{2,1,0:T(8,128)(2,1)}, bf16[4,1024,512]{2,1,0:T(8,128)(2,1)}) custom-call(f32[1024,512]{1,0:T(8,128)S(1)} %copy-done.3, f32[1,512]{1,0:T(1,128)S(1)} %slice.117.gain, bf16[32,512,512]{2,1,0:T(8,128)(2,1)} %get-tuple-element.219.w.wg.wu.wd, ...), custom_call_target="tpu_custom_call" | custom-call | tf_op jit(solution)/shard_map/feed/pallas_call | solution.py:1184
  192.6 75.8 %head_step.1 = (f32[256,512]{1,0:T(8,128)}, f32[3840,512]{1,0:T(8,128)}, f32[8,128]{1,0:T(8,128)}) custom-call(bf16[256,512]{1,0:T(8,128)(2,1)} %select_convert_fusion.x_ref, bf16[3840,512]{1,0:T(8,128)(2,1)} %get-tuple-element.599, s32[8,256,1]{2,1,0:T(8,128)} %and_select_fusion.label_ref), custom_call_target="tpu_custom_call" | custom-call | tf_op jit(solution)/shard_map/head_step/pallas_call | solution.py:1536
  268.7 6.4 gather_fusion.2
  275.0 2.5 multiply_reduce_fusion
  278.9 1.5 broadcast_add_fusion.dx
  280.4 29.3 %feed_back.2 = (f32[1024,512]{1,0:T(8,128)}, f32[8,512]{1,0:T(8,128)}, bf16[4,512,512]{2,1,0:T(8,128)(2,1)}, bf16[4,512,512]{2,1,0:T(8,128)(2,1)}, bf16[4,512,512]{2,1,0:T(8,128)(2,1)}) custom-call(f32[1024,512]{1,0:T(8,128)} %broadcast_add_fusion.dx, f32[1024,512]{1,0:T(8,128)} %copy-done.2, f32[1,512]{1,0:T(1,128)} %copy-done.16, ...), custom_call_target="tpu_custom_call" | custom-call | tf_op jit(solution)/shard_map/feed_back/pallas_call | solution.py:1257
  309.7 27.6 %attend_back.2 = (f32[1024,512]{1,0:T(8,128)}, f32[2,8,512]{2,1,0:T(8,128)}, bf16[4,512,512]{2,1,0:T(8,128)(2,1)}) custom-call(f32[8]{0:T(128)} %copy-done.19, f32[1024,512]{1,0:T(8,128)} %get-tuple-element.229.dx, f32[1024,512]{1,0:T(8,128)} %copy-done.4, f32[1,512]{1,0:T(1,128)} %copy-done.18, bf16[32,512,512]{2,1,0:T(8,128)(2,1)} %get-tuple-element.219.w.wg.wu.wd, ...), custom_call_target="tpu_custom_call" | custom-call | tf_op jit(solution)/shard_map/attend_back/pallas_call | solution.py:1098
  337.3 29.3 %feed_back.3 = (f32[1024,512]{1,0:T(8,128)}, f32[8,512]{1,0:T(8,128)}, bf16[4,512,512]{2,1,0:T(8,128)(2,1)}, bf16[4,512,512]{2,1,0:T(8,128)(2,1)}, bf16[4,512,512]{2,1,0:T(8,128)(2,1)}) custom-call(f32[1024,512]{1,0:T(8,128)} %get-tuple-element.234.dx, f32[1024,512]{1,0:T(8,128)} %copy-done.1, f32[1,512]{1,0:T(1,128)} %copy-done.15, ...), custom_call_target="tpu_custom_call" | custom-call | tf_op jit(solution)/shard_map/feed_back/pallas_call | solution.py:1257
  366.6 27.7 %attend_back.3 = (f32[1024,512]{1,0:T(8,128)}, f32[2,8,512]{2,1,0:T(8,128)}, bf16[4,512,512]{2,1,0:T(8,128)(2,1)}) custom-call(f32[8]{0:T(128)} %copy-done.19, f32[1024,512]{1,0:T(8,128)} %get-tuple-element.238.dx, f32[1024,512]{1,0:T(8,128)} %multiply_multiply_fusion.1.x, f32[1,512]{1,0:T(1,128)} %copy-done.17, ...), custom_call_target="tpu_custom_call" | custom-call | tf_op jit(solution)/shard_map/attend_back/pallas_call | solution.py:1098
  394.4 2.3 multiply_reduce_fusion.1
  399.1 2.4 fusion.35
  402.2 2.2 fusion.23
  404.4 17.7 %group_7.1 = bf16[8,128,512]{2,1,0:T(8,128)(2,1)} custom-call(bf16[8,128,512]{2,1,0:T(8,128)(2,1)} %bitcast.116), custom_call_target="tpu_custom_call" | custom-call | tf_op jit(solution)/shard_map/group_7/pallas_call | solution.py:107
  422.1 8.8 %fusion.18 = f32[3840,512]{1,0:T(8,128)} fusion(f32[3840,512]{1,0:T(8,128)} %get-tuple-element.251, bf16[1024,512]{1,0:T(8,128)(2,1)} %bitcast.115, s32[1024]{0:T(1024)S(1)} %bitcast.134), kind=kOutput, calls=%fused_computation.33 | convolution fusion | flops 4032430080 | bytes 16781312 | tf_op jit(solution)/shard_map/dot_general | solution.py:1758
  432.8 146.9 %settle_gradients.1 = (bf16[6,8,4,16,512]{4,3,2,1,0:T(8,128)(2,1)}, f32[4,960,512]{2,1,0:T(8,128)}, f32[8,512]{1,0:T(8,128)}) custom-call(bf16[4,8,2,2,16,512]{5,4,3,2,1,0:T(8,128)(2,1)} %bitcast.112, bf16[4,8,2,2,16,512]{5,4,3,2,1,0:T(8,128)(2,1)} %bitcast.109, bf16[4,8,2,2,16,512]{5,4,3,2,1,0:T(8,128)(2,1)} %bitcast.110, ...), custom_call_target="tpu_custom_call" | custom-call | tf_op jit(solution)/shard_map/settle_gradients/pallas_call | solution.py:652
  586.6 22.7 %turn_slots.1 = (f32[6,512,512]{2,1,0:T(8,128)}, f32[6,512,512]{2,1,0:T(8,128)}, bf16[8,6,16,512]{3,2,1,0:T(8,128)(2,1)}) custom-call(s32[7]{0:T(128)} %pad_add_fusion.scalars, f32[3]{0:T(128)} %get-tuple-element.399.numbers, f32[6,512,512]{2,1,0:T(8,128)} %left.1, f32[6,512,512]{2,1,0:T(8,128)} %right.1, f32[6,8,4,16,512]{4,3,2,1,0:T(8,128)} %bitcast.97, ...), custom_call_target="tpu_custom_call" | custom-call | tf_op jit(solution)/shard_map/turn_slots/pallas_call | solution.py:1337
  610.4 33.5 %return_slots.1 = (bf16[8,6,4,16,512]{4,3,2,1,0:T(8,128)(2,1)S(1)}, f32[3816,512]{1,0:T(8,128)}, f32[3816,512]{1,0:T(8,128)}, f32[3816,512]{1,0:T(8,128)}, bf16[3816,512]{1,0:T(8,128)(2,1)}) custom-call(bf16[8,6,16,512]{3,2,1,0:T(8,128)(2,1)S(1)} %copy-done.11, f32[3]{0:T(128)S(1)} %get-tuple-element.400.numbers, f32[3840,512]{1,0:T(8,128)} %bitcast.98, ...), custom_call_target="tpu_custom_call" | custom-call | tf_op jit(solution)/shard_map/return_slots/pallas_call | solution.py:840
  644.0 2.0 gather_fusion.3
  646.0 7.3 %fusion.33 = (bf16[32,64,512]{2,1,0:T(8,128)(2,1)}, f32[32,64,512]{2,1,0:T(8,128)}) fusion(f32[32,64,512]{2,1,0:T(8,128)} %param.31, bf16[32,64,512]{2,1,0:T(8,128)(2,1)} %gather_fusion.3, pred[32]{0:T(512)(128)(4,1)S(1)} %compare_and_fusion.1), kind=kLoop, calls=%fused_computation.122 | loop fusion | flops 7340032 | bytes 12582944 | tf_op jit(solution)/shard_map/convert_element_type | solution.py:1865
  655.3 4.0 copy.92
  660.0 4.0 copy.93
  665.5 4.0 copy.94
  670.4 1.9 copy.95
  (175 shorter events, 41.6 us)
Async XLA Ops:
  0.6 3.4 copy-start.29
  1.6 6.9 %copy-start.23 = (s32[1024,1]{1,0:T(8,128)}, s32[1024,1]{1,0:T(8,128)S(1)}, u32[]{:S(2)}) copy-start(s32[1024,1]{1,0:T(8,128)S(1)} %copy.59.ids_col) | copy-start | bytes 12292
  4.7 3.9 copy-start.44
  4.7 4.5 copy-start.35
  9.7 95.8 %copy-start.24 = (s32[1024,1]{1,0:T(8,128)S(1)}, s32[1024,1]{1,0:T(8,128)}, u32[]{:S(2)}) copy-start(s32[1024,1]{1,0:T(8,128)} %copy-done.23) | copy-start | bytes 12292
  107.3 2.6 copy-start.30
  107.3 3.2 copy-start.42
  107.3 3.2 copy-start.28
  112.1 1.7 copy-start.12
  113.9 18.2 %copy-start.17 = (f32[1,512]{1,0:T(1,128)}, f32[1,512]{1,0:T(1,128)S(1)}, u32[]{:S(2)}) copy-start(f32[1,512]{1,0:T(1,128)S(1)} %slice.111.gain) | copy-start | bytes 6148
  114.1 35.8 %copy-start = (s32[2,512,1]{2,1,0:T(8,128)}, s32[2,512,1]{2,1,0:T(8,128)S(1)}, u32[]{:S(2)}) copy-start(s32[2,512,1]{2,1,0:T(8,128)S(1)} %reshape_reshape.16.seg_col) | copy-start | bytes 12292
  114.1 35.8 %copy-start.19 = (f32[8]{0:T(128)}, f32[8]{0:T(128)S(1)}, u32[]{:S(2)}) copy-start(f32[8]{0:T(128)S(1)} %multiply_power_fusion.slopes) | copy-start | bytes 100
  134.6 13.0 %copy-start.1 = (f32[1024,512]{1,0:T(8,128)}, f32[1024,512]{1,0:T(8,128)S(1)}, u32[]{:S(2)}) copy-start(f32[1024,512]{1,0:T(8,128)S(1)} %get-tuple-element.220.x) | copy-start | bytes 6291460
  134.7 12.9 %copy-start.15 = (f32[1,512]{1,0:T(1,128)}, f32[1,512]{1,0:T(1,128)S(1)}, u32[]{:S(2)}) copy-start(f32[1,512]{1,0:T(1,128)S(1)} %slice.113.gain) | copy-start | bytes 6148
  149.9 17.7 %copy-start.18 = (f32[1,512]{1,0:T(1,128)}, f32[1,512]{1,0:T(1,128)S(1)}, u32[]{:S(2)}) copy-start(f32[1,512]{1,0:T(1,128)S(1)} %slice.115.gain) | copy-start | bytes 6148
  173.2 12.2 %copy-start.16 = (f32[1,512]{1,0:T(1,128)}, f32[1,512]{1,0:T(1,128)S(1)}, u32[]{:S(2)}) copy-start(f32[1,512]{1,0:T(1,128)S(1)} %slice.117.gain) | copy-start | bytes 6148
  275.0 2.5 copy-start.22
  366.6 27.8 %copy-start.21 = (f32[1024,512]{1,0:T(8,128)S(1)}, f32[1024,512]{1,0:T(8,128)}, u32[]{:S(2)}) copy-start(f32[1024,512]{1,0:T(8,128)} %copy-done.20) | copy-start | bytes 6291460
  394.4 2.4 copy-start.34
  394.4 2.4 copy-start.38
  394.4 2.4 copy-start.33
  394.4 2.4 copy-start.37
  399.1 2.4 copy-start.31
  432.8 151.7 %copy-start.36 = (f32[6,64]{1,0:T(8,128)S(1)}, f32[6,64]{1,0:T(8,128)}, u32[]{:S(2)}) copy-start(f32[6,64]{1,0:T(8,128)} %param.32) | copy-start | bytes 4612
  432.8 151.7 %copy-start.39 = (f32[6,64]{1,0:T(8,128)S(1)}, f32[6,64]{1,0:T(8,128)}, u32[]{:S(2)}) copy-start(f32[6,64]{1,0:T(8,128)} %param.37) | copy-start | bytes 4612
  432.8 151.7 %copy-start.40 = (f32[6,64]{1,0:T(8,128)S(1)}, f32[6,64]{1,0:T(8,128)}, u32[]{:S(2)}) copy-start(f32[6,64]{1,0:T(8,128)} %param.36) | copy-start | bytes 4612
  646.0 9.3 %copy-start.25 = (f32[3816,512]{1,0:T(8,128)S(1)}, f32[3816,512]{1,0:T(8,128)}, u32[]{:S(2)}) copy-start(f32[3816,512]{1,0:T(8,128)} %get-tuple-element.590) | copy-start | bytes 23445508
  646.0 13.3 %slice-start.2 = ((s8[7815168]{0:T(1024)(128)(4,1)}), s8[4194304]{0:T(1024)(128)(4,1)S(1)}, s32[]{:S(2)}) async-start(s8[7815168]{0:T(1024)(128)(4,1)} %bitcast.102), calls=%async_computation.2 | async-start | bytes 8388608
  655.3 4.7 slice-start.3
  655.3 8.6 %slice-start = ((s8[7815168]{0:T(1024)(128)(4,1)}), s8[4194304]{0:T(1024)(128)(4,1)S(1)}, s32[]{:S(2)}) async-start(s8[7815168]{0:T(1024)(128)(4,1)} %bitcast.100), calls=%async_computation | async-start | bytes 8388608
  660.0 5.5 slice-start.1
  665.5 4.9 copy-start.26
  (17 other events, 16.6 us)
